TPU v7x, 512 devices: a whole 4x8x8 slice. The times are simulated.
512 devices in a mesh: side: 2 (over core), grp: 64 (over x, y, z_lo), head: 4 (over z_hi).
Axes of the slice: x: 4, y: 8, z: 8 (z_hi: 4, z_lo: 2; z = z_hi * 2 + z_lo), core: 2. Of those that a mesh axis runs over, the one named last changes fastest.
Arguments:
- q_new: bfloat16 [128, 64, 4096], P(('side', 'grp'), None, 'head'), may hold values from -12 to 12
- k_cache: bfloat16 [128, 4, 512, 128], P(('side', 'grp'), 'head'), may hold values from -12 to 12
- value_cache: bfloat16 [128, 4, 512, 128], P(('side', 'grp'), 'head'), may hold values from -12 to 12
- k_new: bfloat16 [128, 64, 512], P(('side', 'grp'), None, 'head'), may hold values from -12 to 12
- new_value_rows: bfloat16 [128, 64, 512], P(('side', 'grp'), None, 'head'), may hold values from -12 to 12
- cache_len: int32 [128], P(('side', 'grp')), may hold values from 1 to 512, 32768 in all
- hidden_in: bfloat16 [128, 64, 2048], P(('side', 'grp'), 'head'), may hold values from -8 to 8
- out_proj: bfloat16 [4096, 2048], P('head', 'side'), may hold values from -0.09375 to 0.09375
- norm_gain: float32 [2048], replicated, may hold values from 0.1 to 1.9
- expert_ids: int32 [128, 64, 8], P(('side', 'grp'), 'head'), may hold values from 0 to 127, all different within a row; in each aligned block of 16 rows (0 to 15, 16 to 31, ..., all dimensions but the last counted through in order) at most 2 rows name the same one
- gate_wts: float32 [128, 64, 8], P(('side', 'grp'), 'head'), may hold values from 0.05 to 1
- w_gate: bfloat16 [128, 2048, 768], P(('side', 'grp'), None, 'head'), may hold values from -0.125 to 0.125
- w_up: bfloat16 [128, 2048, 768], P(('side', 'grp'), None, 'head'), may hold values from -0.125 to 0.125
- w_down: bfloat16 [128, 768, 2048], P(('side', 'grp'), 'head'), may hold values from -0.21875 to 0.21875
Outputs:
- layer_out: bfloat16 [128, 64, 2048], P(('side', 'grp'), 'head')
Inputs may be any that keep to these rules, and one draw needn't show every extreme that they name: `expert_ids`: each row names 8 different experts. In each aligned block of 16 rows (one stream's rows taken 16 at a time) no expert is named by more than 2 rows, a bound that some block reaches. `cache_len`: some stream has all 512 positions valid.
All inputs are finite; a program needn't handle non-finite values. No bound on the sum of `cache_len` on one device may be relied on, other than what follows from the above.
Results may differ from a plain program's by a relative error of at most 0.015.
Values may be sent and summed in bfloat16 or wider, within the bound.
No kernel may reach another device: no remote copies, remote signals or barrier semaphores. Data moves between devices by JAX's collectives and lax.ppermute only.
A program may use at most 64 MiB of HBM per device.

v0:
```python
import math

import jax
import jax.numpy as jnp
from jax import lax
from jax.sharding import PartitionSpec as P


def attend(q_new, k_cache, value_cache, k_new, new_value_rows, cache_len):
    q_rows = q_new.shape[1]
    head_dim = k_cache.shape[3]
    cached_part = k_cache.shape[2]
    query_groups = q_new.shape[2] // head_dim
    joined_keys = jnp.concatenate([k_cache[0, 0], k_new[0]], axis=0)
    joined_values = jnp.concatenate([value_cache[0, 0], new_value_rows[0]], axis=0)
    query_rows = q_new[0].reshape(q_rows, query_groups, head_dim)
    scores = jnp.einsum(
        "rgd,kd->grk", query_rows, joined_keys, preferred_element_type=jnp.float32
    ) / math.sqrt(head_dim)
    key_pos = jnp.arange(cached_part + q_rows)[None, :]
    row_pos = jnp.arange(q_rows)[:, None]
    visible = jnp.where(
        key_pos < cached_part, key_pos < cache_len[0], key_pos - cached_part <= row_pos
    )
    scores = jnp.where(visible[None], scores, -jnp.inf)
    highest = jnp.max(scores, axis=-1, keepdims=True)
    exp_scores = jnp.exp(scores - highest)
    attn_probs = (exp_scores / jnp.sum(exp_scores, axis=-1, keepdims=True)).astype(jnp.bfloat16)
    context = jnp.einsum(
        "grk,kd->rgd", attn_probs, joined_values, preferred_element_type=jnp.float32
    ).astype(jnp.bfloat16)
    return context.reshape(q_rows, query_groups * head_dim)


def routing_tables(chosen, mixing, experts, most):
    rows_here, top_k = chosen.shape
    one_hot = (
        (chosen[:, :, None] == jnp.arange(experts)[None, None, :])
        .astype(jnp.int32)
        .reshape(rows_here * top_k, experts)
    )
    earlier = jnp.cumsum(one_hot, axis=0) - one_hot
    slot_index = jnp.sum(earlier * one_hot, axis=1)
    target = chosen.reshape(-1) * most + slot_index
    matches = (jnp.arange(experts * most)[:, None] == target[None, :]).reshape(
        experts * most, rows_here, top_k
    )
    dispatch = jnp.any(matches, axis=2).astype(jnp.bfloat16)
    combine = jnp.sum(jnp.where(matches, mixing.astype(jnp.float32)[None], 0.0), axis=2).T.astype(
        jnp.bfloat16
    )
    return (dispatch, combine)


def shards(
    q_new,
    k_cache,
    value_cache,
    k_new,
    new_value_rows,
    cache_len,
    hidden_in,
    out_proj,
    norm_gain,
    expert_ids,
    gate_wts,
    w_gate,
    w_up,
    w_down,
):
    context = attend(q_new, k_cache, value_cache, k_new, new_value_rows, cache_len)
    width = hidden_in.shape[2]
    full_rows = jnp.dot(
        context,
        lax.all_gather(out_proj, "side", axis=1, tiled=True),
        preferred_element_type=jnp.float32,
    )
    attn_out = lax.psum_scatter(
        full_rows.astype(jnp.bfloat16), "head", scatter_dimension=0, tiled=True
    ).astype(jnp.float32)
    resid = hidden_in[0].astype(jnp.float32) + attn_out
    normed = (
        resid * lax.rsqrt(jnp.mean(resid * resid, axis=-1, keepdims=True) + 1e-06) * norm_gain
    ).astype(jnp.bfloat16)
    raw_wts = gate_wts[0]
    mixing = (raw_wts / jnp.sum(raw_wts, axis=-1, keepdims=True)).astype(jnp.bfloat16)
    experts = lax.axis_size("side") * lax.axis_size("grp")
    quarters = lax.axis_size("head")
    rows_here = expert_ids.shape[1]
    top_k = expert_ids.shape[2]
    most = max(2, (rows_here * top_k + experts - 1) // experts)
    dispatch, combine = routing_tables(expert_ids[0], mixing, experts, most)
    group_rows, group_dispatch = (
        lax.all_gather(normed[None], "head", axis=0, tiled=True),
        lax.all_gather(dispatch[None], "head", axis=0, tiled=True),
    )
    outgoing = (
        jnp.einsum("hsr,hrd->hsd", group_dispatch, group_rows, preferred_element_type=jnp.float32)
        .astype(jnp.bfloat16)
        .reshape(quarters, experts, most, width)
    )
    slot_rows = lax.all_to_all(outgoing, ("side", "grp"), split_axis=1, concat_axis=1, tiled=True)
    flat_rows = slot_rows.reshape(-1, width)
    gate_proj = jnp.dot(flat_rows, w_gate[0], preferred_element_type=jnp.float32)
    up_proj = jnp.dot(flat_rows, w_up[0], preferred_element_type=jnp.float32)
    hidden = (jax.nn.silu(gate_proj) * up_proj).astype(jnp.bfloat16)
    partial_value = (
        jnp.dot(hidden, w_down[0], preferred_element_type=jnp.float32)
        .astype(jnp.bfloat16)
        .reshape(quarters, experts, most, width)
    )
    combine_all = lax.all_gather(combine[None], "head", axis=0, tiled=True)
    returned = lax.all_to_all(
        partial_value, ("side", "grp"), split_axis=1, concat_axis=1, tiled=True
    )
    weighted = jnp.einsum(
        "hrs,hsd->hrd",
        combine_all,
        returned.reshape(quarters, experts * most, width),
        preferred_element_type=jnp.float32,
    )
    moe_out = lax.psum_scatter(
        weighted.astype(jnp.bfloat16), "head", scatter_dimension=0, tiled=True
    ).astype(jnp.float32)[0]
    return (resid + moe_out).astype(jnp.bfloat16)[None]


def solution(mesh):
    in_specs = (
        P(("side", "grp"), None, "head"),
        P(("side", "grp"), "head", None, None),
        P(("side", "grp"), "head", None, None),
        P(("side", "grp"), None, "head"),
        P(("side", "grp"), None, "head"),
        P(("side", "grp")),
        P(("side", "grp"), "head", None),
        P("head", "side"),
        P(),
        P(("side", "grp"), "head", None),
        P(("side", "grp"), "head", None),
        P(("side", "grp"), None, "head"),
        P(("side", "grp"), None, "head"),
        P(("side", "grp"), "head", None),
    )
    out_specs = P(("side", "grp"), "head", None)
    return jax.shard_map(shards, mesh=mesh, in_specs=in_specs, out_specs=out_specs, check_vma=False)
```

profile of v0, /device:TPU:1, one launch (start us, length us, event | category | flops | bytes accessed | tf_op | source)
XLA Modules:
  0.0 406.6 jit_solution(1884150353934912152)
XLA Ops:
  6.5 0.0 copy-start
  6.5 0.0 copy-start.10
  6.5 0.0 copy-start.9
  6.5 0.0 copy-start.11
  6.5 0.0 all-gather.5.cloned.1.call-start
  6.6 0.7 all-gather.5.cloned.1.call-update
  7.3 0.0 reduce-scatter.3.cloned.1.call-start
  8.0 0.9 copy.61
  8.9 0.8 copy.50
  9.7 0.1 eq.31
  9.8 1.6 fusion.54
  11.4 0.0 copy-done.8
  11.4 0.0 copy-done.10
  11.4 0.0 copy-done.9
  11.4 0.0 copy-done.11
  11.4 0.0 copy-start.3
  11.4 0.0 copy-start.1
  11.5 1.2 fusion.6
  12.7 0.0 copy-start.5
  12.7 25.5 %all-gather.5.cloned.1.call-done = bf16[1024,2048]{1,0:T(8,128)(2,1)} async-done(((bf16[1024,1024]{1,0:T(8,128)(2,1)}), bf16[1024,2048]{1,0:T(8,128)(2,1)}) %all-gather.5.cloned.1.call-update) | async-done | bytes 4194320 | tf_op jit(solution)/shard_map/all_gather | solution.py:75
  38.2 3.7 convolution_convert_fusion.3
  41.9 0.0 reduce-scatter.3.cloned.1.call-update
  42.0 0.1 fusion.34
  42.0 0.2 reduce_window_sum.11
  42.2 0.2 select_reduce_fusion.1
  42.4 0.1 reduce_sum.49
  42.5 0.1 copy.51
  42.5 0.0 copy-done.3
  42.6 0.1 copy.52
  42.6 0.1 fusion.26
  42.8 12.4 %all-gather.1 = bf16[1024,16]{0,1:T(8,128)(2,1)S(1)} all-gather(bf16[256,16]{0,1:T(8,128)(2,1)S(1)} %convert_element_type.89), channel_id=3, replica_groups=mesh['side'=2,'grp'=64,'head'=4] {'head'}, dimensions={0}, use_global_device_ids=true | all-gather | bytes 40960 | tf_op jit(solution)/shard_map/all_gather | solution.py:95
  55.2 13.7 %reduce-scatter.3.cloned.1.call-done = bf16[16,2048]{1,0:T(8,128)(2,1)} async-done(((bf16[64,2048]{1,0:T(8,128)(2,1)}), bf16[16,2048]{1,0:T(8,128)(2,1)}) %reduce-scatter.3.cloned.1.call-update) | async-done | bytes 65552 | tf_op jit(solution)/shard_map/reduce_scatter | solution.py:78
  68.8 0.0 copy-done.1
  68.8 1.0 multiply_reduce_fusion
  69.8 0.0 copy-done.5
  69.8 0.9 multiply_convert_fusion
  70.7 11.2 %all-gather.2 = bf16[64,2048]{1,0:T(8,128)(2,1)S(1)} all-gather(bf16[16,2048]{1,0:T(8,128)(2,1)S(1)} %multiply_convert_fusion), channel_id=4, replica_groups=mesh['side'=2,'grp'=64,'head'=4] {'head'}, dimensions={0}, use_global_device_ids=true | all-gather | bytes 327680 | tf_op jit(solution)/shard_map/all_gather | solution.py:94
  81.9 3.2 convolution_convert_fusion.1
  85.1 7.6 %reshape.132 = bf16[4,128,2,2048]{3,2,1,0:T(2,128)(2,1)} reshape(bf16[4,256,2048]{2,1,0:T(8,128)(2,1)} %convolution_convert_fusion.1) | data formatting | bytes 8388608 | tf_op jit(solution)/shard_map/reshape | solution.py:100
  92.8 7.3 %copy.55 = bf16[4,128,2,2048]{3,2,0,1:T(2,128)(2,1)S(1)} copy(bf16[4,128,2,2048]{3,2,1,0:T(2,128)(2,1)} %reshape.132) | data formatting | bytes 8388608 | tf_op jit(solution)/shard_map/reshape | solution.py:100
  100.1 112.8 %all_to_all.10 = bf16[4,128,2,2048]{3,2,0,1:T(2,128)(2,1)} all-to-all(bf16[4,128,2,2048]{3,2,0,1:T(2,128)(2,1)S(1)} %copy.55), channel_id=1, replica_groups=mesh['side'=2,'grp'=64,'head'=4] {'side','grp'}, dimensions={1} | all-to-all | bytes 8388608 | tf_op jit(solution)/shard_map/all_to_all | solution.py:102
  212.9 7.3 %copy.56 = bf16[4,128,2,2048]{3,2,1,0:T(2,128)(2,1)} copy(bf16[4,128,2,2048]{3,2,0,1:T(2,128)(2,1)} %all_to_all.10) | data formatting | bytes 8388608 | tf_op jit(solution)/shard_map/all_to_all | solution.py:102
  220.2 7.3 %reshape.133 = bf16[1024,2048]{1,0:T(8,128)(2,1)} reshape(bf16[4,128,2,2048]{3,2,1,0:T(2,128)(2,1)} %copy.56) | data formatting | bytes 8388608 | tf_op jit(solution)/shard_map/reshape | solution.py:103
  227.5 0.0 copy-done.6
  227.5 3.8 fusion.10
  231.3 0.0 copy-done
  231.3 0.0 copy-done.7
  231.3 6.8 %convolution_convert_fusion = bf16[1024,2048]{1,0:T(8,128)(2,1)} fusion(bf16[1024,2048]{1,0:T(8,128)(2,1)} %reshape.133, bf16[1,192,2048]{2,1,0:T(8,128)(2,1)S(1)} %copy-done, bf16[1,2048,192]{1,2,0:T(8,128)(2,1)S(1)} %copy-done.7, f32[1024,192]{0,1:T(8,128)S(1)} %fusion.10), kind=kOutput, calls=%fused_computation.1 | convolution fusion | flops 1613889536 | bytes 10747904 | tf_op jit(solution)/shard_map/dot_general | solution.py:108
  238.2 7.6 %reshape.134 = bf16[4,128,2,2048]{3,2,1,0:T(2,128)(2,1)} reshape(bf16[1024,2048]{1,0:T(8,128)(2,1)} %convolution_convert_fusion) | data formatting | bytes 8388608 | tf_op jit(solution)/shard_map/reshape | solution.py:110
  245.8 9.3 %copy.57 = bf16[4,128,2,2048]{3,2,0,1:T(2,128)(2,1)} copy(bf16[4,128,2,2048]{3,2,1,0:T(2,128)(2,1)} %reshape.134) | data formatting | bytes 8388608 | tf_op jit(solution)/shard_map/reshape | solution.py:110
  255.1 9.3 %all-to-all-start.1 = ((bf16[4,128,2,2048]{3,2,0,1:T(2,128)(2,1)}), bf16[4,128,2,2048]{3,2,0,1:T(2,128)(2,1)}, u32[]{:S(2)}, u32[]{:S(2)}) async-start(bf16[4,128,2,2048]{3,2,0,1:T(2,128)(2,1)} %copy.57), calls=%async_computation.2 | async-start | bytes 8388608 | tf_op jit(solution)/shard_map/all_to_all | solution.py:113
  264.4 0.0 reduce-scatter.5.cloned.1.call-start
  264.5 0.0 copy-done.4
  264.5 0.1 copy.53
  264.6 0.1 select_reduce_fusion
  264.7 15.2 %all-gather = bf16[64,256]{1,0:T(8,128)(2,1)S(1)} all-gather(bf16[16,256]{1,0:T(8,128)(2,1)S(1)} %bitcast.91), channel_id=2, replica_groups=mesh['side'=2,'grp'=64,'head'=4] {'head'}, dimensions={0}, use_global_device_ids=true | all-gather | bytes 40960 | tf_op jit(solution)/shard_map/all_gather | solution.py:112
  279.9 79.3 %all-to-all-done.1 = bf16[4,128,2,2048]{3,2,0,1:T(2,128)(2,1)} async-done(((bf16[4,128,2,2048]{3,2,0,1:T(2,128)(2,1)}), bf16[4,128,2,2048]{3,2,0,1:T(2,128)(2,1)}, u32[]{:S(2)}, u32[]{:S(2)}) %all-to-all-start.1) | async-done | bytes 4194336 | tf_op jit(solution)/shard_map/all_to_all | solution.py:113
  359.2 7.4 %copy.58 = bf16[4,128,2,2048]{3,2,1,0:T(2,128)(2,1)} copy(bf16[4,128,2,2048]{3,2,0,1:T(2,128)(2,1)} %all-to-all-done.1) | data formatting | bytes 8388608 | tf_op jit(solution)/shard_map/all_to_all | solution.py:113
  366.5 7.2 %reshape.135 = bf16[4,256,2048]{2,1,0:T(8,128)(2,1)} reshape(bf16[4,128,2,2048]{3,2,1,0:T(2,128)(2,1)} %copy.58) | data formatting | bytes 8388608 | tf_op jit(solution)/shard_map/reshape | solution.py:119
  373.8 3.6 convolution_convert_fusion.2
  377.3 0.0 reduce-scatter.5.cloned.1.call-update
  377.4 21.2 %reduce-scatter.5.cloned.1.call-done = bf16[1,16,2048]{2,1,0:T(8,128)(2,1)} async-done(((bf16[4,16,2048]{2,1,0:T(8,128)(2,1)}), bf16[1,16,2048]{2,1,0:T(8,128)(2,1)}) %reduce-scatter.5.cloned.1.call-update) | async-done | bytes 65552 | tf_op jit(solution)/shard_map/reduce_scatter | solution.py:122
  398.6 0.0 copy-done.2
  398.6 1.5 fusion.33
  (13 shorter events, 0.1 us)
Async XLA Ops:
  6.5 224.8 %copy-start = (bf16[1,192,2048]{2,1,0:T(8,128)(2,1)S(1)}, bf16[1,192,2048]{2,1,0:T(8,128)(2,1)}, u32[]{:S(2)}) copy-start(bf16[1,192,2048]{2,1,0:T(8,128)(2,1)} %param.27) | copy-start | bytes 2359300
  6.5 4.9 %copy-start.8 = (bf16[1,1,512,128]{3,2,1,0:T(8,128)(2,1)S(1)}, bf16[1,1,512,128]{3,2,1,0:T(8,128)(2,1)}, u32[]{:S(2)}) copy-start(bf16[1,1,512,128]{3,2,1,0:T(8,128)(2,1)} %param.15) | copy-start | bytes 393220
  6.5 4.9 %copy-start.10 = (bf16[1,64,128]{2,1,0:T(8,128)(2,1)S(1)}, bf16[1,64,128]{2,1,0:T(8,128)(2,1)}, u32[]{:S(2)}) copy-start(bf16[1,64,128]{2,1,0:T(8,128)(2,1)} %param.17) | copy-start | bytes 49156
  6.5 4.9 %copy-start.9 = (bf16[1,1,512,128]{3,2,1,0:T(8,128)(2,1)S(1)}, bf16[1,1,512,128]{3,2,1,0:T(8,128)(2,1)}, u32[]{:S(2)}) copy-start(bf16[1,1,512,128]{3,2,1,0:T(8,128)(2,1)} %param.16) | copy-start | bytes 393220
  6.5 4.9 %copy-start.11 = (bf16[1,64,128]{2,1,0:T(8,128)(2,1)S(1)}, bf16[1,64,128]{2,1,0:T(8,128)(2,1)}, u32[]{:S(2)}) copy-start(bf16[1,64,128]{2,1,0:T(8,128)(2,1)} %param.18) | copy-start | bytes 49156
  6.5 31.7 %all-gather.5.cloned.1.call-start = ((), (), s32[]{:S(2)}) async-start(), calls=%async_computation.4 | async-start | bytes 6291456 | tf_op jit(solution)/shard_map/all_gather | solution.py:75
  7.3 61.5 %reduce-scatter.3.cloned.1.call-start = ((), (), s32[]{:S(2)}) async-start(), calls=%async_computation.5 | async-start | bytes 327680 | tf_op jit(solution)/shard_map/reduce_scatter | solution.py:78
  11.4 31.1 %copy-start.3 = (s32[1,16,8]{1,2,0:T(8,128)S(1)}, s32[1,16,8]{1,2,0:T(8,128)}, u32[]{:S(2)}) copy-start(s32[1,16,8]{1,2,0:T(8,128)} %param.23) | copy-start | bytes 1540
  11.4 57.4 %copy-start.1 = (bf16[1,16,2048]{2,1,0:T(8,128)(2,1)S(1)}, bf16[1,16,2048]{2,1,0:T(8,128)(2,1)}, u32[]{:S(2)}) copy-start(bf16[1,16,2048]{2,1,0:T(8,128)(2,1)} %param.20) | copy-start | bytes 196612
  12.7 57.1 %copy-start.5 = (f32[2048]{0:T(1024)S(1)}, f32[2048]{0:T(1024)}, u32[]{:S(2)}) copy-start(f32[2048]{0:T(1024)} %param.22) | copy-start | bytes 24580
  220.2 7.3 %copy-start.6 = (bf16[1,2048,192]{1,2,0:T(8,128)(2,1)S(1)}, bf16[1,2048,192]{1,2,0:T(8,128)(2,1)}, u32[]{:S(2)}) copy-start(bf16[1,2048,192]{1,2,0:T(8,128)(2,1)} %param.25) | copy-start | bytes 2359300
  227.5 3.8 copy-start.7
  255.1 9.3 %copy-start.4 = (f32[1,16,8]{1,2,0:T(8,128)S(1)}, f32[1,16,8]{1,2,0:T(8,128)}, u32[]{:S(2)}) copy-start(f32[1,16,8]{1,2,0:T(8,128)} %param.24) | copy-start | bytes 1540
  255.1 104.0 %all-to-all-start.1 = ((bf16[4,128,2,2048]{3,2,0,1:T(2,128)(2,1)}), bf16[4,128,2,2048]{3,2,0,1:T(2,128)(2,1)}, u32[]{:S(2)}, u32[]{:S(2)}) async-start(bf16[4,128,2,2048]{3,2,0,1:T(2,128)(2,1)} %copy.57), calls=%async_computation.2 | async-start | bytes 8388608 | tf_op jit(solution)/shard_map/all_to_all | solution.py:113
  264.4 134.2 %reduce-scatter.5.cloned.1.call-start = ((), (), s32[]{:S(2)}) async-start(), calls=%async_computation.6 | async-start | bytes 327680 | tf_op jit(solution)/shard_map/reduce_scatter | solution.py:122
  373.8 24.8 %copy-start.2 = (bf16[16,2048]{1,0:T(8,128)(2,1)S(1)}, bf16[16,2048]{1,0:T(8,128)(2,1)}, u32[]{:S(2)}) copy-start(bf16[16,2048]{1,0:T(8,128)(2,1)} %reduce-scatter.3.cloned.1.call-done) | copy-start | bytes 196612
Sparse Core Ops, SparseCore 0:
  9.4 28.7 all-gather.4
  42.1 26.6 reduce-scatter.2
  377.5 21.0 reduce-scatter.4
where the time goes:
time: 409 us; the launch traced here: 407 us
  blocking collectives  152 us (37%)
  waiting for transfers between devices  140 us (34%)
  local copies, waits for them, and re-layouts  63.3 us (15%)
  matrix products  23.9 us (6%)
  between operations  14 us (3%)
  starting transfers between devices  9.4 us (2%)
  other arithmetic  4.18 us (1%)
    all_to_all x1, blocking collectives, shards(): lax.all_to_all(outgoing, ('side', 'grp'), split_axis=1, concat_axis=1, ti...  113 us
    all_to_all x1, waiting for transfers between devices, shards(): lax.all_to_all(partial_value, ('side', 'grp'), split_axis=1, concat_axis=...  79.3 us
    all_gather x1, waiting for transfers between devices, shards(): lax.all_gather(out_proj, 'side', axis=1, tiled=True)  25.5 us
    reduce_scatter x1, waiting for transfers between devices, shards(): lax.psum_scatter(weighted.astype(jnp.bfloat16), 'head', scatter_dimension...  21.2 us
    reshape x2, local copies, waits for them, and re-layouts, shards(): partial_value = jnp.dot(hidden, w_down[0], preferred_element_type=jnp.flo...  17 us
    all_gather x1, blocking collectives, shards(): combine_all = lax.all_gather(combine[None], 'head', axis=0, tiled=True)  15.2 us
    reshape x2, local copies, waits for them, and re-layouts, shards(): outgoing = jnp.einsum('hsr,hrd->hsd', group_dispatch, group_rows, preferr...  15 us
    reduce_scatter x1, waiting for transfers between devices, shards(): lax.psum_scatter(full_rows.astype(jnp.bfloat16), 'head', scatter_dimensio...  13.7 us
  transfers between devices with their start and end apart: 4, of which 4 were waited for; matrix products, arithmetic and copies ran while one was open for 1% of the time, Pallas kernels for 0%

commit v1 on v0

v1 whole, which is shorter than its diff:
```python
import math

import jax
import jax.numpy as jnp
from jax import lax
from jax.sharding import Mesh
from jax.sharding import PartitionSpec as P

STREAM = ("side", "x", "yp", "yq", "zl")
NEAR = ("yp", "head")
FAR = ("side", "x", "yq", "zl")


def attend(q_new, k_cache, value_cache, k_new, new_value_rows, cache_len):
    q_rows = q_new.shape[1]
    head_dim = k_cache.shape[3]
    cached_part = k_cache.shape[2]
    query_groups = q_new.shape[2] // head_dim
    joined_keys = jnp.concatenate([k_cache[0, 0], k_new[0]], axis=0)
    joined_values = jnp.concatenate([value_cache[0, 0], new_value_rows[0]], axis=0)
    query_rows = q_new[0].reshape(q_rows, query_groups, head_dim)
    scores = jnp.einsum(
        "rgd,kd->grk", query_rows, joined_keys, preferred_element_type=jnp.float32
    ) / math.sqrt(head_dim)
    key_pos = jnp.arange(cached_part + q_rows)[None, :]
    row_pos = jnp.arange(q_rows)[:, None]
    visible = jnp.where(
        key_pos < cached_part, key_pos < cache_len[0], key_pos - cached_part <= row_pos
    )
    scores = jnp.where(visible[None], scores, -jnp.inf)
    highest = jnp.max(scores, axis=-1, keepdims=True)
    exp_scores = jnp.exp(scores - highest)
    attn_probs = (exp_scores / jnp.sum(exp_scores, axis=-1, keepdims=True)).astype(jnp.bfloat16)
    context = jnp.einsum(
        "grk,kd->rgd", attn_probs, joined_values, preferred_element_type=jnp.float32
    ).astype(jnp.bfloat16)
    return context.reshape(q_rows, query_groups * head_dim)


def a2a(value, axes):
    return lax.all_to_all(value, axes, split_axis=0, concat_axis=0, tiled=True)


def slot_codes(chosen):
    same = chosen[:, :, None, None] == chosen[None, None, :, :]
    rows = jnp.arange(chosen.shape[0])
    before = (rows[None, :] < rows[:, None])[:, None, :, None]
    rank = jnp.sum((same & before).astype(jnp.int32), axis=(2, 3))
    return chosen * 2 + rank


def shards(
    q_new,
    k_cache,
    value_cache,
    k_new,
    new_value_rows,
    cache_len,
    hidden_in,
    out_proj,
    norm_gain,
    expert_ids,
    gate_wts,
    w_gate,
    w_up,
    w_down,
):
    width = hidden_in.shape[2]
    block = hidden_in.shape[1]
    side = lax.axis_index("side")
    quarters = lax.axis_size("head")
    near = lax.axis_size(NEAR)
    far = lax.axis_size(FAR)
    slots = 2 * near

    partner_proj = lax.ppermute(out_proj, "side", [(0, 1), (1, 0)])
    context = attend(q_new, k_cache, value_cache, k_new, new_value_rows, cache_len)
    own = jnp.dot(context, out_proj, preferred_element_type=jnp.float32)
    partner = jnp.dot(context, partner_proj, preferred_element_type=jnp.float32)
    full_rows = jnp.concatenate(
        [jnp.where(side == 0, own, partner), jnp.where(side == 0, partner, own)], axis=1
    ).astype(jnp.bfloat16)
    pieces = a2a(full_rows.reshape(quarters, block, width), "head")
    resid = hidden_in[0].astype(jnp.float32) + jnp.sum(pieces.astype(jnp.float32), axis=0)
    normed = (
        resid * lax.rsqrt(jnp.mean(resid * resid, axis=-1, keepdims=True) + 1e-06) * norm_gain
    ).astype(jnp.bfloat16)

    raw_wts = gate_wts[0]
    mixing = (raw_wts / jnp.sum(raw_wts, axis=-1, keepdims=True)).astype(jnp.bfloat16)
    top_k = mixing.shape[1]
    codes = slot_codes(expert_ids[0]).astype(jnp.bfloat16)
    extra = jnp.pad(jnp.concatenate([codes, mixing], axis=1), ((0, 0), (0, 128 - 2 * top_k)))
    payload = jnp.concatenate([normed, extra], axis=1)
    gathered = a2a(jnp.broadcast_to(payload[None], (near,) + payload.shape), NEAR)
    gathered = gathered.reshape(near * block, width + 128)
    rows = gathered[:, :width]
    code = gathered[:, width : width + top_k].astype(jnp.int32)
    mix = gathered[:, width + top_k : width + 2 * top_k]

    place = jnp.arange(far)
    per_side = far // 2
    per_x = per_side // lax.axis_size("x")
    pair = per_x // lax.axis_size("yq")
    ys = lax.axis_size("yp") * lax.axis_size("yq")
    xs = lax.axis_size("x")
    expert = (
        ((place // per_side) * xs + (place // per_x) % xs) * ys
        + lax.axis_index("yp") * lax.axis_size("yq")
        + (place // pair) % lax.axis_size("yq")
    ) * pair + place % pair
    wanted = (expert[:, None] * 2 + jnp.arange(2)[None, :]).reshape(-1)
    hit = wanted[:, None, None] == code.T[None, :, :]
    takes = jnp.any(hit, axis=1)
    weight = jnp.sum(jnp.where(hit, mix.T[None].astype(jnp.float32), 0.0), axis=1)
    own_block = (jnp.arange(near)[:, None] == (jnp.arange(near * block) // block)[None, :])
    dispatch = (takes[:, None, :] & own_block[None]).astype(jnp.bfloat16)
    combine = jnp.where(own_block[None], weight[:, None, :], 0.0).astype(jnp.bfloat16)
    dispatch = dispatch.reshape(far * slots, near * block)
    combine = combine.reshape(far * slots, near * block)

    outgoing = jnp.dot(dispatch, rows, preferred_element_type=jnp.float32).astype(jnp.bfloat16)
    flat_rows = a2a(outgoing.reshape(far, slots, width), FAR).reshape(far * slots, width)
    gate_proj = jnp.dot(flat_rows, w_gate[0], preferred_element_type=jnp.float32)
    up_proj = jnp.dot(flat_rows, w_up[0], preferred_element_type=jnp.float32)
    hidden = (jax.nn.silu(gate_proj) * up_proj).astype(jnp.bfloat16)
    partial_value = jnp.dot(hidden, w_down[0], preferred_element_type=jnp.float32).astype(
        jnp.bfloat16
    )
    returned = a2a(partial_value.reshape(far, slots, width), FAR).reshape(far * slots, width)
    weighted = lax.dot_general(
        combine, returned, (((0,), (0,)), ((), ())), preferred_element_type=jnp.float32
    ).astype(jnp.bfloat16)
    parts = a2a(weighted.reshape(near, block, width), NEAR)
    moe_out = jnp.sum(parts.astype(jnp.float32), axis=0)
    return (resid + moe_out).astype(jnp.bfloat16)[None]


def solution(mesh):
    fine = Mesh(
        mesh.devices.reshape(2, 4, 4, 2, 2, 4), ("side", "x", "yp", "yq", "zl", "head")
    )
    in_specs = (
        P(STREAM, None, "head"),
        P(STREAM, "head", None, None),
        P(STREAM, "head", None, None),
        P(STREAM, None, "head"),
        P(STREAM, None, "head"),
        P(STREAM),
        P(STREAM, "head", None),
        P("head", "side"),
        P(),
        P(STREAM, "head", None),
        P(STREAM, "head", None),
        P(STREAM, None, "head"),
        P(STREAM, None, "head"),
        P(STREAM, "head", None),
    )
    out_specs = P(STREAM, "head", None)
    return jax.shard_map(shards, mesh=fine, in_specs=in_specs, out_specs=out_specs, check_vma=False)
```

time: 409 us -> 249 us (0.61)
  the two profiles are of different devices: /device:TPU:1 before, /device:TPU:8 now
where the time goes in v1:
time: 249 us; the launch traced here: 248 us
  blocking collectives  97 us (39%)
  waiting for transfers between devices  94.8 us (38%)
  starting transfers between devices  25.6 us (10%)
  matrix products  18.4 us (7%)
  other arithmetic  6.09 us (2%)
  local copies, waits for them, and re-layouts  5.49 us (2%)
    all_to_all x2, blocking collectives, a2a(): return lax.all_to_all(value, axes, split_axis=0, concat_axis=0, tiled=True)  97 us
    all_to_all x3, waiting for transfers between devices, a2a(): return lax.all_to_all(value, axes, split_axis=0, concat_axis=0, tiled=True)  94.8 us
    all_to_all x3, starting transfers between devices, a2a(): return lax.all_to_all(value, axes, split_axis=0, concat_axis=0, tiled=True)  23.5 us
    dot_general x1, matrix products, shards(): jnp.dot(hidden, w_down[0], preferred_element_type=jnp.float32)  6.83 us
  transfers between devices with their start and end apart: 4, of which 3 were waited for; matrix products, arithmetic and copies ran while one was open for 4% of the time, Pallas kernels for 0%

profile of v1, /device:TPU:8, one launch (start us, length us, event | category | flops | bytes accessed | tf_op | source)
XLA Modules:
  0.0 248.3 jit_solution(11055671060385112216)
XLA Ops:
  0.0 0.0 copy-start
  0.0 0.0 copy-start.9
  0.0 0.0 copy-start.11
  0.0 0.0 copy-start.10
  0.0 0.0 copy-start.12
  0.0 2.1 collective-permute-start
  2.7 0.9 copy.43
  3.7 0.8 copy.36
  4.4 0.7 reduce_sum.72
  5.2 1.6 fusion.71
  6.8 0.0 copy-done.9
  6.8 0.0 copy-done.11
  6.8 0.0 copy-done.10
  6.8 0.0 copy-done.12
  6.8 0.0 copy-start.5
  6.8 0.0 copy-start.2
  6.8 1.2 fusion.6
  8.1 0.0 copy-done.5
  8.1 0.3 copy-done.2
  8.4 0.5 fusion.31
  8.9 0.0 copy-start.4
  8.9 0.0 copy-start.3
  8.9 0.0 copy-start.6
  9.0 0.0 collective-permute-done
  9.0 2.1 select_convert_fusion.2
  11.1 0.7 pad_maximum_fusion
  11.8 10.3 %all-to-all-start = ((bf16[4,16,2048]{2,1,0:T(8,128)(2,1)}), bf16[4,16,2048]{2,1,0:T(8,128)(2,1)S(1)}, u32[]{:S(2)}, u32[]{:S(2)}) async-start(bf16[4,16,2048]{2,1,0:T(8,128)(2,1)} %pad_maximum_fusion), calls=%async_computation | async-start | bytes 524288 | tf_op jit(solution)/shard_map/all_to_all | solution.py:41
  22.1 0.0 copy-done.4
  22.1 2.5 %convert_reduce_fusion.1 = s32[16,8]{1,0:T(8,128)S(1)} fusion(s32[16,8]{0,1:T(8,128)S(1)} %bitcast.113, s32[16,8]{1,0:T(8,128)S(1)} %copy.36, pred[16,16]{1,0:T(8,128)(4,1)S(1)} %iota_compare_fusion.3), kind=kLoop, calls=%fused_computation.29 | loop fusion | flops 65408 | bytes 1792 | tf_op jit(solution)/shard_map/reduce_sum | solution.py:48
  24.6 0.1 copy.37
  24.7 0.1 copy.41
  24.8 9.1 %all-to-all-done = bf16[4,16,2048]{2,1,0:T(8,128)(2,1)S(1)} async-done(((bf16[4,16,2048]{2,1,0:T(8,128)(2,1)}), bf16[4,16,2048]{2,1,0:T(8,128)(2,1)S(1)}, u32[]{:S(2)}, u32[]{:S(2)}) %all-to-all-start) | async-done | bytes 262176 | tf_op jit(solution)/shard_map/all_to_all | solution.py:41
  33.9 0.0 copy-done.3
  33.9 0.1 multiply_reduce_fusion
  34.1 0.0 copy-done.6
  34.1 0.1 multiply_convert_fusion
  34.2 1.1 broadcast_in_dim.95
  35.2 7.1 %all-to-all-start.1 = ((bf16[16,16,2176]{2,1,0:T(8,128)(2,1)}), bf16[16,16,2176]{2,1,0:T(8,128)(2,1)S(1)}, u32[]{:S(2)}, u32[]{:S(2)}) async-start(bf16[16,16,2176]{2,1,0:T(8,128)(2,1)} %broadcast_in_dim.95), calls=%async_computation.1 | async-start | bytes 2228224 | tf_op jit(solution)/shard_map/all_to_all | solution.py:41
  42.4 0.1 iota_add_fusion
  42.4 0.1 add.142
  42.6 31.7 %all-to-all-done.1 = bf16[16,16,2176]{2,1,0:T(8,128)(2,1)S(1)} async-done(((bf16[16,16,2176]{2,1,0:T(8,128)(2,1)}), bf16[16,16,2176]{2,1,0:T(8,128)(2,1)S(1)}, u32[]{:S(2)}, u32[]{:S(2)}) %all-to-all-start.1) | async-done | bytes 1114144 | tf_op jit(solution)/shard_map/all_to_all | solution.py:41
  74.3 0.1 convert_bitcast_fusion.2
  74.4 0.1 copy.39
  74.4 0.3 compare_reduce_fusion
  74.7 0.1 broadcast_and_fusion
  74.9 1.3 convolution_convert_fusion.1
  76.1 0.0 copy-start.7
  76.1 60.0 %all_to_all.25 = bf16[32,32,2048]{2,1,0:T(8,128)(2,1)S(1)} all-to-all(bf16[32,32,2048]{2,1,0:T(8,128)(2,1)S(1)} %bitcast.98), channel_id=1, replica_groups=mesh['side'=2,'x'=4,'yp'=4,'yq'=2,'zl'=2,'head'=4] {'side','x','yq','zl'}, dimensions={0} | all-to-all | bytes 8388608 | tf_op jit(solution)/shard_map/all_to_all | solution.py:41
  136.1 0.0 copy-start.1
  136.1 2.0 copy-done.1
  138.0 0.0 copy-done.7
  138.0 1.5 fusion.11
  139.6 0.0 copy-done
  139.6 0.0 copy-done.8
  139.6 6.8 %convolution_convert_fusion = bf16[1024,2048]{1,0:T(8,128)(2,1)} fusion(bf16[1024,2048]{1,0:T(8,128)(2,1)} %bitcast.103, bf16[1,192,2048]{2,1,0:T(8,128)(2,1)S(1)} %copy-done, bf16[1,2048,192]{1,2,0:T(8,128)(2,1)S(1)} %copy-done.8, f32[1024,192]{0,1:T(8,128)S(1)} %fusion.11), kind=kOutput, calls=%fused_computation.1 | convolution fusion | flops 1613889536 | bytes 10747904 | tf_op jit(solution)/shard_map/dot_general | solution.py:127
  146.4 6.1 %all-to-all-start.3 = ((bf16[32,32,2048]{2,1,0:T(8,128)(2,1)}), bf16[32,32,2048]{2,1,0:T(8,128)(2,1)}, u32[]{:S(2)}, u32[]{:S(2)}) async-start(bf16[32,32,2048]{2,1,0:T(8,128)(2,1)} %bitcast.101), calls=%async_computation.3 | async-start | bytes 8388608 | tf_op jit(solution)/shard_map/all_to_all | solution.py:41
  152.6 0.1 copy.40
  152.6 0.3 fusion.18
  152.9 0.1 select_convert_fusion
  153.0 54.0 %all-to-all-done.3 = bf16[32,32,2048]{2,1,0:T(8,128)(2,1)} async-done(((bf16[32,32,2048]{2,1,0:T(8,128)(2,1)}), bf16[32,32,2048]{2,1,0:T(8,128)(2,1)}, u32[]{:S(2)}, u32[]{:S(2)}) %all-to-all-start.3) | async-done | bytes 4194336 | tf_op jit(solution)/shard_map/all_to_all | solution.py:41
  207.1 3.5 %convolution_convert_fusion.2 = bf16[256,2048]{1,0:T(8,128)(2,1)S(1)} fusion(bf16[1024,256]{1,0:T(8,128)(2,1)S(1)} %bitcast.106, bf16[1024,2048]{1,0:T(8,128)(2,1)} %bitcast.26), kind=kOutput, calls=%fused_computation.3 | convolution fusion | flops 1074266112 | bytes 5767168 | tf_op jit(solution)/shard_map/dot_general | solution.py:131
  210.5 37.0 %all_to_all.26 = bf16[16,16,2048]{2,1,0:T(8,128)(2,1)S(1)} all-to-all(bf16[16,16,2048]{2,1,0:T(8,128)(2,1)S(1)} %bitcast.105), channel_id=1, replica_groups=mesh['side'=2,'x'=4,'yp'=4,'yq'=2,'zl'=2,'head'=4] {'yp','head'}, dimensions={0} | all-to-all | bytes 2097152 | tf_op jit(solution)/shard_map/all_to_all | solution.py:41
  247.5 0.1 convert_reduce_fusion
  247.7 0.6 fusion.27
  (14 shorter events, 0.2 us)
Async XLA Ops:
  0.0 139.6 %copy-start = (bf16[1,192,2048]{2,1,0:T(8,128)(2,1)S(1)}, bf16[1,192,2048]{2,1,0:T(8,128)(2,1)}, u32[]{:S(2)}) copy-start(bf16[1,192,2048]{2,1,0:T(8,128)(2,1)} %param.27) | copy-start | bytes 2359300
  0.0 6.8 %copy-start.9 = (bf16[1,1,512,128]{3,2,1,0:T(8,128)(2,1)S(1)}, bf16[1,1,512,128]{3,2,1,0:T(8,128)(2,1)}, u32[]{:S(2)}) copy-start(bf16[1,1,512,128]{3,2,1,0:T(8,128)(2,1)} %param.15) | copy-start | bytes 393220
  0.0 6.8 %copy-start.11 = (bf16[1,64,128]{2,1,0:T(8,128)(2,1)S(1)}, bf16[1,64,128]{2,1,0:T(8,128)(2,1)}, u32[]{:S(2)}) copy-start(bf16[1,64,128]{2,1,0:T(8,128)(2,1)} %param.17) | copy-start | bytes 49156
  0.0 6.8 %copy-start.10 = (bf16[1,1,512,128]{3,2,1,0:T(8,128)(2,1)S(1)}, bf16[1,1,512,128]{3,2,1,0:T(8,128)(2,1)}, u32[]{:S(2)}) copy-start(bf16[1,1,512,128]{3,2,1,0:T(8,128)(2,1)} %param.16) | copy-start | bytes 393220
  0.0 6.8 %copy-start.12 = (bf16[1,64,128]{2,1,0:T(8,128)(2,1)S(1)}, bf16[1,64,128]{2,1,0:T(8,128)(2,1)}, u32[]{:S(2)}) copy-start(bf16[1,64,128]{2,1,0:T(8,128)(2,1)} %param.18) | copy-start | bytes 49156
  0.0 8.9 %collective-permute-start = (bf16[1024,1024]{1,0:T(8,128)(2,1)}, bf16[1024,1024]{1,0:T(8,128)(2,1)}, u32[]{:S(2)}, u32[]{:S(2)}) collective-permute-start(bf16[1024,1024]{1,0:T(8,128)(2,1)} %param.21), channel_id=1, source_target_pairs={{0,256},{256,0},{1,257},{257,1},{2,258},{258,2},{3,259},{259,3},{4... | collective-permute-start | bytes 6291464 | tf_op jit(solution)/shard_map/ppermute | solution.py:76
  6.8 1.3 copy-start.5
  6.8 1.6 copy-start.2
  8.9 13.2 %copy-start.4 = (s32[1,16,8]{1,2,0:T(8,128)S(1)}, s32[1,16,8]{1,2,0:T(8,128)}, u32[]{:S(2)}) copy-start(s32[1,16,8]{1,2,0:T(8,128)} %param.23) | copy-start | bytes 1540
  8.9 25.0 %copy-start.3 = (bf16[1,16,2048]{2,1,0:T(8,128)(2,1)S(1)}, bf16[1,16,2048]{2,1,0:T(8,128)(2,1)}, u32[]{:S(2)}) copy-start(bf16[1,16,2048]{2,1,0:T(8,128)(2,1)} %param.20) | copy-start | bytes 196612
  8.9 25.1 %copy-start.6 = (f32[2048]{0:T(1024)S(1)}, f32[2048]{0:T(1024)}, u32[]{:S(2)}) copy-start(f32[2048]{0:T(1024)} %param.22) | copy-start | bytes 24580
  11.8 22.1 %all-to-all-start = ((bf16[4,16,2048]{2,1,0:T(8,128)(2,1)}), bf16[4,16,2048]{2,1,0:T(8,128)(2,1)S(1)}, u32[]{:S(2)}, u32[]{:S(2)}) async-start(bf16[4,16,2048]{2,1,0:T(8,128)(2,1)} %pad_maximum_fusion), calls=%async_computation | async-start | bytes 524288 | tf_op jit(solution)/shard_map/all_to_all | solution.py:41
  35.2 39.0 %all-to-all-start.1 = ((bf16[16,16,2176]{2,1,0:T(8,128)(2,1)}), bf16[16,16,2176]{2,1,0:T(8,128)(2,1)S(1)}, u32[]{:S(2)}, u32[]{:S(2)}) async-start(bf16[16,16,2176]{2,1,0:T(8,128)(2,1)} %broadcast_in_dim.95), calls=%async_computation.1 | async-start | bytes 2228224 | tf_op jit(solution)/shard_map/all_to_all | solution.py:41
  76.1 61.9 %copy-start.7 = (bf16[1,2048,192]{1,2,0:T(8,128)(2,1)S(1)}, bf16[1,2048,192]{1,2,0:T(8,128)(2,1)}, u32[]{:S(2)}) copy-start(bf16[1,2048,192]{1,2,0:T(8,128)(2,1)} %param.25) | copy-start | bytes 2359300
  136.1 2.0 copy-start.1
  138.0 1.5 copy-start.8
  146.4 60.6 %all-to-all-start.3 = ((bf16[32,32,2048]{2,1,0:T(8,128)(2,1)}), bf16[32,32,2048]{2,1,0:T(8,128)(2,1)}, u32[]{:S(2)}, u32[]{:S(2)}) async-start(bf16[32,32,2048]{2,1,0:T(8,128)(2,1)} %bitcast.101), calls=%async_computation.3 | async-start | bytes 8388608 | tf_op jit(solution)/shard_map/all_to_all | solution.py:41

commit v2 on v1

v2 whole, which is shorter than its diff:
```python
import math

import jax
import jax.numpy as jnp
from jax import lax
from jax.experimental import pallas as pl
from jax.experimental.pallas import tpu as pltpu
from jax.sharding import Mesh
from jax.sharding import PartitionSpec as P

STREAM = ("side", "x", "yp", "yq", "zl")
NEAR = ("head", "yp")
FAR = ("x", "yq", "zl", "side")


def attention_kernel(
    len_ref,
    q_hbm,
    k_hbm,
    v_hbm,
    kn_hbm,
    vn_hbm,
    proj_hbm,
    ctx_ref,
    own_ref,
    q_ref,
    k_ref,
    v_ref,
    kn_ref,
    vn_ref,
    proj_ref,
    sems,
):
    pairs = (
        (q_hbm, q_ref),
        (k_hbm, k_ref),
        (kn_hbm, kn_ref),
        (v_hbm, v_ref),
        (vn_hbm, vn_ref),
        (proj_hbm, proj_ref),
    )
    loads = [
        pltpu.make_async_copy(source, target, sems.at[index])
        for index, (source, target) in enumerate(pairs)
    ]
    for load in loads:
        load.start()
    for load in loads[:-1]:
        load.wait()
    rows = q_ref.shape[1]
    cached, size = k_ref.shape[2], k_ref.shape[3]
    groups = q_ref.shape[2] // size
    per = 2
    scale = 1.0 / math.sqrt(size)
    old_key, new_key = k_ref[0, 0], kn_ref[0]
    old_val, new_val = v_ref[0, 0], vn_ref[0]
    contract = (((1,), (1,)), ((), ()))
    key_pos = lax.broadcasted_iota(jnp.int32, (per * rows, cached), 1)
    old_seen = key_pos < len_ref[0]
    row_pos = lax.broadcasted_iota(jnp.int32, (per * rows, rows), 0) % rows
    new_seen = lax.broadcasted_iota(jnp.int32, (per * rows, rows), 1) <= row_pos
    for start in range(0, groups, per):
        query = jnp.concatenate(
            [q_ref[0, :, (start + g) * size : (start + g + 1) * size] for g in range(per)], axis=0
        )
        old = lax.dot_general(query, old_key, contract, preferred_element_type=jnp.float32) * scale
        new = lax.dot_general(query, new_key, contract, preferred_element_type=jnp.float32) * scale
        old = jnp.where(old_seen, old, -jnp.inf)
        new = jnp.where(new_seen, new, -jnp.inf)
        highest = jnp.maximum(
            jnp.max(old, axis=1, keepdims=True), jnp.max(new, axis=1, keepdims=True)
        )
        old = jnp.exp(old - highest)
        new = jnp.exp(new - highest)
        total = jnp.sum(old, axis=1, keepdims=True) + jnp.sum(new, axis=1, keepdims=True)
        share = 1.0 / total
        context = jnp.dot(
            (old * share).astype(jnp.bfloat16), old_val, preferred_element_type=jnp.float32
        ) + jnp.dot((new * share).astype(jnp.bfloat16), new_val, preferred_element_type=jnp.float32)
        context = context.astype(jnp.bfloat16)
        for g in range(per):
            ctx_ref[:, (start + g) * size : (start + g + 1) * size] = context[
                g * rows : (g + 1) * rows
            ]
    loads[-1].wait()
    own_ref[...] = jnp.dot(
        ctx_ref[...], proj_ref[...], preferred_element_type=jnp.float32
    ).astype(jnp.bfloat16)


def project_kernel(side_ref, ctx_ref, proj_any, own_ref, out_ref, proj_ref, sem):
    load = pltpu.make_async_copy(proj_any, proj_ref, sem)
    load.start()
    load.wait()
    half = proj_ref.shape[1]
    block = out_ref.shape[1]
    side = side_ref[0]
    partner = jnp.dot(
        ctx_ref[...], proj_ref[...], preferred_element_type=jnp.float32
    ).astype(jnp.bfloat16)
    mine = pl.ds(pl.multiple_of(side * half, half), half)
    other = pl.ds(pl.multiple_of((1 - side) * half, half), half)
    for part in range(out_ref.shape[0]):
        take = slice(part * block, (part + 1) * block)
        out_ref[part, :, mine] = own_ref[take]
        out_ref[part, :, other] = partner[take]


def expert_kernel(rows_ref, gate_ref, up_ref, down_ref, out_ref):
    contract = (((1,), (1,)), ((), ()))
    rows = rows_ref[...]
    gate = lax.dot_general(rows, gate_ref[...], contract, preferred_element_type=jnp.float32)
    up = lax.dot_general(rows, up_ref[...], contract, preferred_element_type=jnp.float32)
    hidden = (gate / (1.0 + jnp.exp(-gate)) * up).astype(jnp.bfloat16)
    out_ref[...] = jnp.dot(hidden, down_ref[...], preferred_element_type=jnp.float32).astype(
        jnp.bfloat16
    )


def combine_kernel(combine_ref, rows_ref, out_ref):
    out_ref[...] = jnp.dot(
        combine_ref[...], rows_ref[...], preferred_element_type=jnp.float32
    ).astype(jnp.bfloat16)


def in_vmem():
    return pl.BlockSpec(memory_space=pltpu.VMEM)


def in_smem():
    return pl.BlockSpec(memory_space=pltpu.SMEM)


def a2a(value, axes):
    return lax.all_to_all(value, axes, split_axis=0, concat_axis=0, tiled=True)


def slot_codes(chosen):
    same = chosen[:, :, None, None] == chosen[None, None, :, :]
    rows = jnp.arange(chosen.shape[0])
    before = (rows[None, :] < rows[:, None])[:, None, :, None]
    rank = jnp.sum((same & before).astype(jnp.int32), axis=(2, 3))
    return chosen * 2 + rank


def shards(
    q_new,
    k_cache,
    value_cache,
    k_new,
    new_value_rows,
    cache_len,
    hidden_in,
    out_proj,
    norm_gain,
    expert_ids,
    gate_wts,
    w_gate,
    w_up,
    w_down,
):
    width = hidden_in.shape[2]
    block = hidden_in.shape[1]
    side = lax.axis_index("side")
    quarters = lax.axis_size("head")
    near = lax.axis_size(NEAR)
    far = lax.axis_size(FAR)
    slots = 2 * near

    partner_proj = lax.ppermute(out_proj, "side", [(0, 1), (1, 0)])
    half = out_proj.shape[1]
    rows_here = q_new.shape[1]
    context, own = pl.pallas_call(
        attention_kernel,
        in_specs=[in_smem()] + [pl.BlockSpec(memory_space=pltpu.HBM)] * 6,
        out_specs=[in_vmem()] * 2,
        scratch_shapes=[
            pltpu.VMEM(value.shape, jnp.bfloat16)
            for value in (q_new, k_cache, value_cache, k_new, new_value_rows, out_proj)
        ]
        + [pltpu.SemaphoreType.DMA((6,))],
        out_shape=[
            jax.ShapeDtypeStruct((rows_here, q_new.shape[2]), jnp.bfloat16),
            jax.ShapeDtypeStruct((rows_here, half), jnp.bfloat16),
        ],
        cost_estimate=pl.CostEstimate(
            flops=400_000_000, bytes_accessed=3_000_000, transcendentals=300_000
        ),
        compiler_params=pltpu.CompilerParams(vmem_limit_bytes=12 << 20),
        name="attention",
    )(
        cache_len,
        *(
            pltpu.with_memory_space_constraint(value, pltpu.HBM)
            for value in (q_new, k_cache, value_cache, k_new, new_value_rows, out_proj)
        ),
    )
    full_rows = pl.pallas_call(
        project_kernel,
        in_specs=[in_smem(), in_vmem(), pl.BlockSpec(memory_space=pl.ANY), in_vmem()],
        out_specs=in_vmem(),
        scratch_shapes=[pltpu.VMEM(out_proj.shape, jnp.bfloat16), pltpu.SemaphoreType.DMA],
        out_shape=jax.ShapeDtypeStruct((quarters, block, width), jnp.bfloat16),
        cost_estimate=pl.CostEstimate(
            flops=140_000_000, bytes_accessed=2_500_000, transcendentals=0
        ),
        compiler_params=pltpu.CompilerParams(vmem_limit_bytes=12 << 20),
        name="project",
    )(side.reshape(1), context, partner_proj, own)
    pieces = a2a(full_rows, "head")
    resid = hidden_in[0].astype(jnp.float32) + jnp.sum(pieces.astype(jnp.float32), axis=0)
    normed = (
        resid * lax.rsqrt(jnp.mean(resid * resid, axis=-1, keepdims=True) + 1e-06) * norm_gain
    ).astype(jnp.bfloat16)

    raw_wts = gate_wts[0]
    mixing = (raw_wts / jnp.sum(raw_wts, axis=-1, keepdims=True)).astype(jnp.bfloat16)
    top_k = mixing.shape[1]
    codes = slot_codes(expert_ids[0]).astype(jnp.bfloat16)
    extra = jnp.pad(jnp.concatenate([codes, mixing], axis=1), ((0, 0), (0, 128 - 2 * top_k)))
    payload = jnp.concatenate([normed, extra], axis=1)
    gathered = a2a(jnp.broadcast_to(payload[None], (near,) + payload.shape), NEAR)
    gathered = gathered.reshape(near * block, width + 128)
    rows = gathered[:, :width]
    code = gathered[:, width : width + top_k].astype(jnp.int32)
    mix = gathered[:, width + top_k : width + 2 * top_k]

    place = jnp.arange(far)
    xs, ps, qs, zs = (lax.axis_size(name) for name in ("x", "yp", "yq", "zl"))
    sides = lax.axis_size("side")
    at_z = (place // sides) % zs
    at_q = (place // (sides * zs)) % qs
    at_x = place // (sides * zs * qs)
    expert = (
        ((place % sides) * xs + at_x) * (ps * qs) + lax.axis_index("yp") * qs + at_q
    ) * zs + at_z
    wanted = (expert[:, None] * 2 + jnp.arange(2)[None, :]).reshape(-1)
    hit = wanted[:, None, None] == code.T[None, :, :]
    takes = jnp.any(hit, axis=1)
    weight = jnp.sum(jnp.where(hit, mix.T[None].astype(jnp.float32), 0.0), axis=1)
    own_block = (jnp.arange(near)[:, None] == (jnp.arange(near * block) // block)[None, :])
    dispatch = (takes[:, None, :] & own_block[None]).astype(jnp.bfloat16)
    combine = jnp.where(own_block.T[:, None, :], weight.T[:, :, None], 0.0).astype(jnp.bfloat16)
    dispatch = dispatch.reshape(far * slots, near * block)
    combine = combine.reshape(near * block, far * slots)

    outgoing = jnp.dot(dispatch, rows, preferred_element_type=jnp.float32).astype(jnp.bfloat16)
    flat_rows = a2a(outgoing.reshape(far, slots, width), FAR).reshape(far * slots, width)
    tile = 256
    part = w_gate.shape[2]
    partial_value = pl.pallas_call(
        expert_kernel,
        grid=(far * slots // tile,),
        in_specs=[
            pl.BlockSpec((tile, width), lambda i: (i, 0)),
            pl.BlockSpec((part, width), lambda i: (0, 0)),
            pl.BlockSpec((part, width), lambda i: (0, 0)),
            pl.BlockSpec((part, width), lambda i: (0, 0)),
        ],
        out_specs=pl.BlockSpec((tile, width), lambda i: (i, 0)),
        out_shape=pltpu.HBM((far * slots, width), jnp.bfloat16),
        cost_estimate=pl.CostEstimate(
            flops=2_500_000_000, bytes_accessed=11_000_000, transcendentals=200_000
        ),
        compiler_params=pltpu.CompilerParams(vmem_limit_bytes=24 << 20),
        name="experts",
    )(flat_rows, w_gate[0].T, w_up[0].T, w_down[0])
    returned = a2a(partial_value.reshape(far, slots, width), FAR).reshape(far * slots, width)
    columns = 512
    weighted = pl.pallas_call(
        combine_kernel,
        grid=(width // columns,),
        in_specs=[
            pl.BlockSpec((near * block, far * slots), lambda i: (0, 0)),
            pl.BlockSpec((far * slots, columns), lambda i: (0, i)),
        ],
        out_specs=pl.BlockSpec((near * block, columns), lambda i: (0, i)),
        out_shape=jax.ShapeDtypeStruct((near * block, width), jnp.bfloat16),
        cost_estimate=pl.CostEstimate(
            flops=1_100_000_000, bytes_accessed=6_000_000, transcendentals=0
        ),
        compiler_params=pltpu.CompilerParams(vmem_limit_bytes=16 << 20),
        name="combine",
    )(combine, returned)
    parts = a2a(weighted.reshape(near, block, width), NEAR)
    moe_out = jnp.sum(parts.astype(jnp.float32), axis=0)
    return (resid + moe_out).astype(jnp.bfloat16)[None]


def solution(mesh):
    fine = Mesh(
        mesh.devices.reshape(2, 4, 4, 2, 2, 4), ("side", "x", "yp", "yq", "zl", "head")
    )
    in_specs = (
        P(STREAM, None, "head"),
        P(STREAM, "head", None, None),
        P(STREAM, "head", None, None),
        P(STREAM, None, "head"),
        P(STREAM, None, "head"),
        P(STREAM),
        P(STREAM, "head", None),
        P("head", "side"),
        P(),
        P(STREAM, "head", None),
        P(STREAM, "head", None),
        P(STREAM, None, "head"),
        P(STREAM, None, "head"),
        P(STREAM, "head", None),
    )
    out_specs = P(STREAM, "head", None)
    return jax.shard_map(shards, mesh=fine, in_specs=in_specs, out_specs=out_specs, check_vma=False)
```

time: 249 us -> 237 us (0.952)
  the two profiles are of different devices: /device:TPU:8 before, /device:TPU:1 now
where the time goes in v2:
time: 237 us; the launch traced here: 236 us
  blocking collectives  92.8 us (39%)
  waiting for transfers between devices  92.1 us (39%)
  starting transfers between devices  27.5 us (12%)
  Pallas kernels  14 us (6%)
  other arithmetic  5.34 us (2%)
  local copies, waits for them, and re-layouts  2.45 us (1%)
    all_to_all x2, blocking collectives, a2a(): return lax.all_to_all(value, axes, split_axis=0, concat_axis=0, tiled=True)  92.8 us
    all_to_all x3, waiting for transfers between devices, a2a(): return lax.all_to_all(value, axes, split_axis=0, concat_axis=0, tiled=True)  92.1 us
    all_to_all x3, starting transfers between devices, a2a(): return lax.all_to_all(value, axes, split_axis=0, concat_axis=0, tiled=True)  18.7 us
    ppermute x1, starting transfers between devices, shards(): partner_proj = lax.ppermute(out_proj, 'side', [(0, 1), (1, 0)])  8.87 us
    pallas_call x1, Pallas kernels, shards(): pl.pallas_call(expert_kernel, grid=(far * slots // tile,), in_specs=[pl.B...  5.44 us
  transfers between devices with their start and end apart: 4, of which 3 were waited for; matrix products, arithmetic and copies ran while one was open for 2% of the time, Pallas kernels for 1%

profile of v2, /device:TPU:1, one launch (start us, length us, event | category | flops | bytes accessed | tf_op | source)
XLA Modules:
  0.0 236.3 jit_solution(8504292258845665124)
XLA Ops:
  0.0 0.0 copy-start.5
  0.0 8.9 %collective-permute-start = (bf16[1024,1024]{1,0:T(8,128)(2,1)}, bf16[1024,1024]{1,0:T(8,128)(2,1)S(1)}, u32[]{:S(2)}, u32[]{:S(2)}) collective-permute-start(bf16[1024,1024]{1,0:T(8,128)(2,1)} %proj_hbm.1), channel_id=1, source_target_pairs={{0,256},{256,0},{1,257},{257,1},{2,258},{258,2},{3,259},{259,3},{4... | collective-permute-start | bytes 6291464 | tf_op jit(solution)/shard_map/ppermute | solution.py:170
  9.5 0.8 copy.31
  10.3 0.7 reduce_sum.62
  11.0 3.3 %attention.1 = (bf16[64,1024]{1,0:T(8,128)(2,1)S(1)}, bf16[64,1024]{1,0:T(8,128)(2,1)S(1)}) custom-call(s32[1]{0:T(128)S(6)} %copy.38.len_ref, bf16[1,64,1024]{2,1,0:T(8,128)(2,1)} %q_hbm.1, bf16[1,1,512,128]{3,2,1,0:T(8,128)(2,1)} %k_hbm.1, bf16[1,1,512,128]{3,2,1,0:T(8,128)(2,1)} %v_hbm.1, bf16[1,64,128]{2,1,0:T(8,128)(2,1)} %kn_hbm.1, ...), custom_call_target="tpu_custom_call" | custom-call | flops 400000000 | bytes 3000000 | tf_op jit(solution)/shard_map/attention/pallas_call | solution.py:173
  14.3 0.0 copy-start.4
  14.3 0.0 copy-start.3
  14.3 0.0 copy-start.6
  14.4 0.0 copy-done.5
  14.4 0.0 collective-permute-done.proj_any
  14.4 1.3 project.1
  15.7 4.7 %all-to-all-start = ((bf16[4,16,2048]{2,1,0:T(8,128)(2,1)}), bf16[4,16,2048]{2,1,0:T(8,128)(2,1)S(1)}, u32[]{:S(2)}, u32[]{:S(2)}) async-start(bf16[4,16,2048]{2,1,0:T(8,128)(2,1)} %project.1), calls=%async_computation | async-start | bytes 524288 | tf_op jit(solution)/shard_map/all_to_all | solution.py:135
  20.4 0.0 copy-done.4
  20.4 2.5 %convert_reduce_fusion.1 = s32[16,8]{1,0:T(8,128)S(1)} fusion(s32[16,8]{0,1:T(8,128)S(1)} %bitcast.53, s32[16,8]{1,0:T(8,128)S(1)} %copy.31, pred[16,16]{1,0:T(8,128)(4,1)S(1)} %iota_compare_fusion.3), kind=kLoop, calls=%fused_computation.7 | loop fusion | flops 65408 | bytes 1792 | tf_op jit(solution)/shard_map/reduce_sum | solution.py:142
  23.0 0.1 copy.32
  23.1 0.1 copy.37
  23.2 6.6 %all-to-all-done = bf16[4,16,2048]{2,1,0:T(8,128)(2,1)S(1)} async-done(((bf16[4,16,2048]{2,1,0:T(8,128)(2,1)}), bf16[4,16,2048]{2,1,0:T(8,128)(2,1)S(1)}, u32[]{:S(2)}, u32[]{:S(2)}) %all-to-all-start) | async-done | bytes 262176 | tf_op jit(solution)/shard_map/all_to_all | solution.py:135
  29.8 0.0 copy-done.3
  29.8 0.1 multiply_reduce_fusion
  30.0 0.0 copy-done.6
  30.0 0.1 multiply_convert_fusion
  30.1 1.1 broadcast_in_dim.28
  31.1 9.3 %all-to-all-start.1 = ((bf16[16,16,2176]{2,1,0:T(8,128)(2,1)}), bf16[16,16,2176]{2,1,0:T(8,128)(2,1)S(1)}, u32[]{:S(2)}, u32[]{:S(2)}) async-start(bf16[16,16,2176]{2,1,0:T(8,128)(2,1)} %broadcast_in_dim.28), calls=%async_computation.1 | async-start | bytes 2228224 | tf_op jit(solution)/shard_map/all_to_all | solution.py:135
  40.5 0.1 iota_add_fusion
  40.6 0.1 add.132
  40.7 34.3 %all-to-all-done.1 = bf16[16,16,2176]{2,1,0:T(8,128)(2,1)S(1)} async-done(((bf16[16,16,2176]{2,1,0:T(8,128)(2,1)}), bf16[16,16,2176]{2,1,0:T(8,128)(2,1)S(1)}, u32[]{:S(2)}, u32[]{:S(2)}) %all-to-all-start.1) | async-done | bytes 1114144 | tf_op jit(solution)/shard_map/all_to_all | solution.py:135
  75.0 0.1 convert_bitcast_fusion.2
  75.1 0.1 copy.34
  75.2 0.3 compare_reduce_fusion
  75.4 0.1 broadcast_and_fusion
  75.6 1.2 convolution_convert_fusion
  76.9 0.0 copy-start
  76.9 0.0 copy-start.1
  76.9 0.0 copy-start.2
  76.9 58.5 %all_to_all.25 = bf16[32,32,2048]{2,1,0:T(8,128)(2,1)S(1)} all-to-all(bf16[32,32,2048]{2,1,0:T(8,128)(2,1)S(1)} %bitcast.45), channel_id=1, replica_groups=mesh['side'=2,'x'=4,'yp'=4,'yq'=2,'zl'=2,'head'=4] {'x','yq','zl','side'}, dimensions={0} | all-to-all | bytes 8388608 | tf_op jit(solution)/shard_map/all_to_all | solution.py:135
  135.3 0.0 copy-done
  135.3 0.0 copy-done.1
  135.3 0.0 copy-done.2
  135.4 5.4 %experts.1 = bf16[1024,2048]{1,0:T(8,128)(2,1)} custom-call(bf16[1024,2048]{1,0:T(8,128)(2,1)S(1)} %bitcast.40, bf16[192,2048]{1,0:T(8,128)(2,1)S(1)} %bitcast.42, bf16[192,2048]{1,0:T(8,128)(2,1)S(1)} %bitcast.43, bf16[192,2048]{1,0:T(8,128)(2,1)S(1)} %bitcast.44), custom_call_target="tpu_custom_call" | custom-call | flops 2500000000 | bytes 11000000 | tf_op jit(solution)/shard_map/experts/pallas_call | solution.py:251
  140.8 4.7 %all-to-all-start.3 = ((bf16[32,32,2048]{2,1,0:T(8,128)(2,1)}), bf16[32,32,2048]{2,1,0:T(8,128)(2,1)}, u32[]{:S(2)}, u32[]{:S(2)}) async-start(bf16[32,32,2048]{2,1,0:T(8,128)(2,1)} %bitcast.46), calls=%async_computation.3 | async-start | bytes 8388608 | tf_op jit(solution)/shard_map/all_to_all | solution.py:135
  145.5 0.1 copy.35
  145.5 0.3 fusion.1
  145.8 0.1 select_convert_fusion
  145.9 0.2 copy.36.combine_ref
  146.1 51.1 %all-to-all-done.3 = bf16[32,32,2048]{2,1,0:T(8,128)(2,1)} async-done(((bf16[32,32,2048]{2,1,0:T(8,128)(2,1)}), bf16[32,32,2048]{2,1,0:T(8,128)(2,1)}, u32[]{:S(2)}, u32[]{:S(2)}) %all-to-all-start.3) | async-done | bytes 4194336 | tf_op jit(solution)/shard_map/all_to_all | solution.py:135
  197.3 3.9 %combine.1 = bf16[256,2048]{1,0:T(8,128)(2,1)S(1)} custom-call(bf16[256,1024]{1,0:T(8,128)(2,1)S(1)} %copy.36.combine_ref, bf16[1024,2048]{1,0:T(8,128)(2,1)} %bitcast.19.rows_ref), custom_call_target="tpu_custom_call" | custom-call | flops 1100000000 | bytes 6000000 | tf_op jit(solution)/shard_map/combine/pallas_call | solution.py:270
  201.1 34.3 %all_to_all.26 = bf16[16,16,2048]{2,1,0:T(8,128)(2,1)S(1)} all-to-all(bf16[16,16,2048]{2,1,0:T(8,128)(2,1)S(1)} %bitcast.41), channel_id=1, replica_groups=mesh['side'=2,'x'=4,'yp'=4,'yq'=2,'zl'=2,'head'=4] {'head','yp'}, dimensions={0} | all-to-all | bytes 2097152 | tf_op jit(solution)/shard_map/all_to_all | solution.py:135
  235.5 0.1 convert_reduce_fusion
  235.6 0.6 fusion.4
  (11 shorter events, 0.1 us)
Async XLA Ops:
  0.0 14.4 %copy-start.5 = (f32[1,16,8]{1,2,0:T(8,128)S(1)}, f32[1,16,8]{1,2,0:T(8,128)}, u32[]{:S(2)}) copy-start(f32[1,16,8]{1,2,0:T(8,128)} %param.24) | copy-start | bytes 1540
  0.0 14.4 %collective-permute-start = (bf16[1024,1024]{1,0:T(8,128)(2,1)}, bf16[1024,1024]{1,0:T(8,128)(2,1)S(1)}, u32[]{:S(2)}, u32[]{:S(2)}) collective-permute-start(bf16[1024,1024]{1,0:T(8,128)(2,1)} %proj_hbm.1), channel_id=1, source_target_pairs={{0,256},{256,0},{1,257},{257,1},{2,258},{258,2},{3,259},{259,3},{4... | collective-permute-start | bytes 6291464 | tf_op jit(solution)/shard_map/ppermute | solution.py:170
  14.3 6.1 %copy-start.4 = (s32[1,16,8]{1,2,0:T(8,128)S(1)}, s32[1,16,8]{1,2,0:T(8,128)}, u32[]{:S(2)}) copy-start(s32[1,16,8]{1,2,0:T(8,128)} %param.23) | copy-start | bytes 1540
  14.3 15.5 %copy-start.3 = (bf16[1,16,2048]{2,1,0:T(8,128)(2,1)S(1)}, bf16[1,16,2048]{2,1,0:T(8,128)(2,1)}, u32[]{:S(2)}) copy-start(bf16[1,16,2048]{2,1,0:T(8,128)(2,1)} %param.20) | copy-start | bytes 196612
  14.3 15.6 %copy-start.6 = (f32[2048]{0:T(1024)S(1)}, f32[2048]{0:T(1024)}, u32[]{:S(2)}) copy-start(f32[2048]{0:T(1024)} %param.22) | copy-start | bytes 24580
  15.7 14.0 %all-to-all-start = ((bf16[4,16,2048]{2,1,0:T(8,128)(2,1)}), bf16[4,16,2048]{2,1,0:T(8,128)(2,1)S(1)}, u32[]{:S(2)}, u32[]{:S(2)}) async-start(bf16[4,16,2048]{2,1,0:T(8,128)(2,1)} %project.1), calls=%async_computation | async-start | bytes 524288 | tf_op jit(solution)/shard_map/all_to_all | solution.py:135
  31.1 43.9 %all-to-all-start.1 = ((bf16[16,16,2176]{2,1,0:T(8,128)(2,1)}), bf16[16,16,2176]{2,1,0:T(8,128)(2,1)S(1)}, u32[]{:S(2)}, u32[]{:S(2)}) async-start(bf16[16,16,2176]{2,1,0:T(8,128)(2,1)} %broadcast_in_dim.28), calls=%async_computation.1 | async-start | bytes 2228224 | tf_op jit(solution)/shard_map/all_to_all | solution.py:135
  76.9 58.5 %copy-start = (bf16[1,2048,192]{1,2,0:T(8,128)(2,1)S(1)}, bf16[1,2048,192]{1,2,0:T(8,128)(2,1)}, u32[]{:S(2)}) copy-start(bf16[1,2048,192]{1,2,0:T(8,128)(2,1)} %param.25) | copy-start | bytes 2359300
  76.9 58.5 %copy-start.1 = (bf16[1,2048,192]{1,2,0:T(8,128)(2,1)S(1)}, bf16[1,2048,192]{1,2,0:T(8,128)(2,1)}, u32[]{:S(2)}) copy-start(bf16[1,2048,192]{1,2,0:T(8,128)(2,1)} %param.26) | copy-start | bytes 2359300
  76.9 58.5 %copy-start.2 = (bf16[1,192,2048]{2,1,0:T(8,128)(2,1)S(1)}, bf16[1,192,2048]{2,1,0:T(8,128)(2,1)}, u32[]{:S(2)}) copy-start(bf16[1,192,2048]{2,1,0:T(8,128)(2,1)} %param.27) | copy-start | bytes 2359300
  140.8 56.5 %all-to-all-start.3 = ((bf16[32,32,2048]{2,1,0:T(8,128)(2,1)}), bf16[32,32,2048]{2,1,0:T(8,128)(2,1)}, u32[]{:S(2)}, u32[]{:S(2)}) async-start(bf16[32,32,2048]{2,1,0:T(8,128)(2,1)} %bitcast.46), calls=%async_computation.3 | async-start | bytes 8388608 | tf_op jit(solution)/shard_map/all_to_all | solution.py:135

commit v3 on v2

--- a/solution.py
+++ b/solution.py
@@ -135,12 +135,55 @@
     return lax.all_to_all(value, axes, split_axis=0, concat_axis=0, tiled=True)
 
 
-def slot_codes(chosen):
-    same = chosen[:, :, None, None] == chosen[None, None, :, :]
-    rows = jnp.arange(chosen.shape[0])
-    before = (rows[None, :] < rows[:, None])[:, None, :, None]
-    rank = jnp.sum((same & before).astype(jnp.int32), axis=(2, 3))
-    return chosen * 2 + rank
+def table_kernel(part_ref, routing_ref, dispatch_ref, combine_ref):
+    top_k = routing_ref.shape[2] // 16
+    blocks, block = routing_ref.shape[0], routing_ref.shape[1]
+    rows = blocks * block
+    columns = jnp.transpose(routing_ref[...].reshape(rows, routing_ref.shape[2]))
+    chosen = columns[:top_k]
+    weights = columns[top_k : 2 * top_k]
+    mixing = (weights / jnp.sum(weights, axis=0, keepdims=True)).astype(jnp.bfloat16)
+    mixing = mixing.astype(jnp.float32)
+    sides, xs, ps, qs, zs = 2, 4, 4, 2, 2
+    local = sides * xs * qs * zs
+    place = lax.broadcasted_iota(jnp.int32, (local, rows), 0)
+    at_z = (place // sides) % zs
+    at_q = (place // (sides * zs)) % qs
+    at_x = place // (sides * zs * qs)
+    expert = (((place % sides) * xs + at_x) * (ps * qs) + part_ref[0] * qs + at_q) * zs + at_z
+    expert = expert.astype(jnp.float32)
+    named = jnp.zeros((local, rows), jnp.float32)
+    weight = jnp.zeros((local, rows), jnp.float32)
+    for k in range(top_k):
+        hit = chosen[k : k + 1] == expert
+        named = jnp.where(hit, 1.0, named)
+        weight = jnp.where(hit, mixing[k : k + 1], weight)
+    first = lax.broadcasted_iota(jnp.int32, (rows, rows), 0)
+    second = lax.broadcasted_iota(jnp.int32, (rows, rows), 1)
+    earlier = (first < second) & (first // block == second // block)
+    rank = jnp.dot(
+        named.astype(jnp.bfloat16),
+        jnp.where(earlier, 1.0, 0.0).astype(jnp.bfloat16),
+        preferred_element_type=jnp.float32,
+    )
+    own = lax.broadcasted_iota(jnp.int32, (blocks, rows), 0) == (
+        lax.broadcasted_iota(jnp.int32, (blocks, rows), 1) // block
+    )
+    group = 128 // (2 * blocks)
+    for start in range(0, local, group):
+        tiles = []
+        for e in range(start, start + group):
+            for s in range(2):
+                takes = (named[e : e + 1] > 0.5) & (jnp.abs(rank[e : e + 1] - s) < 0.5)
+                at = (2 * e + s) * blocks
+                dispatch_ref[at : at + blocks] = jnp.where(
+                    own, jnp.where(takes, 1.0, 0.0), 0.0
+                ).astype(jnp.bfloat16)
+                tiles.append(jnp.where(own, jnp.where(takes, weight[e : e + 1], 0.0), 0.0))
+        at = 2 * start * blocks
+        combine_ref[:, at : at + 128] = jnp.transpose(jnp.concatenate(tiles, axis=0)).astype(
+            jnp.bfloat16
+        )
 
 
 def shards(
@@ -167,6 +210,10 @@
     far = lax.axis_size(FAR)
     slots = 2 * near
 
+    top_k = expert_ids.shape[2]
+    routing = jnp.concatenate([expert_ids[0].astype(jnp.float32), gate_wts[0]], axis=1)
+    routing = jnp.pad(routing, ((0, 0), (0, 128 - 2 * top_k)))
+    routing = a2a(jnp.broadcast_to(routing[None], (near,) + routing.shape), NEAR)
     partner_proj = lax.ppermute(out_proj, "side", [(0, 1), (1, 0)])
     half = out_proj.shape[1]
     rows_here = q_new.shape[1]
@@ -195,6 +242,7 @@
             for value in (q_new, k_cache, value_cache, k_new, new_value_rows, out_proj)
         ),
     )
+    partner_proj, routing = lax.optimization_barrier((partner_proj, routing))
     full_rows = pl.pallas_call(
         project_kernel,
         in_specs=[in_smem(), in_vmem(), pl.BlockSpec(memory_space=pl.ANY), in_vmem()],
@@ -213,36 +261,22 @@
         resid * lax.rsqrt(jnp.mean(resid * resid, axis=-1, keepdims=True) + 1e-06) * norm_gain
     ).astype(jnp.bfloat16)
 
-    raw_wts = gate_wts[0]
-    mixing = (raw_wts / jnp.sum(raw_wts, axis=-1, keepdims=True)).astype(jnp.bfloat16)
-    top_k = mixing.shape[1]
-    codes = slot_codes(expert_ids[0]).astype(jnp.bfloat16)
-    extra = jnp.pad(jnp.concatenate([codes, mixing], axis=1), ((0, 0), (0, 128 - 2 * top_k)))
-    payload = jnp.concatenate([normed, extra], axis=1)
-    gathered = a2a(jnp.broadcast_to(payload[None], (near,) + payload.shape), NEAR)
-    gathered = gathered.reshape(near * block, width + 128)
-    rows = gathered[:, :width]
-    code = gathered[:, width : width + top_k].astype(jnp.int32)
-    mix = gathered[:, width + top_k : width + 2 * top_k]
-
-    place = jnp.arange(far)
-    xs, ps, qs, zs = (lax.axis_size(name) for name in ("x", "yp", "yq", "zl"))
-    sides = lax.axis_size("side")
-    at_z = (place // sides) % zs
-    at_q = (place // (sides * zs)) % qs
-    at_x = place // (sides * zs * qs)
-    expert = (
-        ((place % sides) * xs + at_x) * (ps * qs) + lax.axis_index("yp") * qs + at_q
-    ) * zs + at_z
-    wanted = (expert[:, None] * 2 + jnp.arange(2)[None, :]).reshape(-1)
-    hit = wanted[:, None, None] == code.T[None, :, :]
-    takes = jnp.any(hit, axis=1)
-    weight = jnp.sum(jnp.where(hit, mix.T[None].astype(jnp.float32), 0.0), axis=1)
-    own_block = (jnp.arange(near)[:, None] == (jnp.arange(near * block) // block)[None, :])
-    dispatch = (takes[:, None, :] & own_block[None]).astype(jnp.bfloat16)
-    combine = jnp.where(own_block.T[:, None, :], weight.T[:, :, None], 0.0).astype(jnp.bfloat16)
-    dispatch = dispatch.reshape(far * slots, near * block)
-    combine = combine.reshape(near * block, far * slots)
+    rows = a2a(jnp.broadcast_to(normed[None], (near,) + normed.shape), NEAR)
+    rows = rows.reshape(near * block, width)
+    dispatch, combine = pl.pallas_call(
+        table_kernel,
+        in_specs=[in_smem(), in_vmem()],
+        out_specs=[in_vmem()] * 2,
+        out_shape=[
+            jax.ShapeDtypeStruct((far * slots, near * block), jnp.bfloat16),
+            jax.ShapeDtypeStruct((near * block, far * slots), jnp.bfloat16),
+        ],
+        cost_estimate=pl.CostEstimate(
+            flops=1_000_000_000, bytes_accessed=1_200_000, transcendentals=0
+        ),
+        compiler_params=pltpu.CompilerParams(vmem_limit_bytes=12 << 20),
+        name="tables",
+    )(lax.axis_index("yp").reshape(1), routing)
 
     outgoing = jnp.dot(dispatch, rows, preferred_element_type=jnp.float32).astype(jnp.bfloat16)
     flat_rows = a2a(outgoing.reshape(far, slots, width), FAR).reshape(far * slots, width)

time: 237 us -> 245 us (1.034)
  blocking collectives: 92.8 us -> 162 us
  waiting for transfers between devices: 92.1 us -> 38.1 us
  other arithmetic: 5.34 us -> 2.44 us
    all_to_all x2 -> x4, blocking collectives: 92.8 us -> 162 us  [a2a(): return lax.all_to_all(value, axes, split_axis=0, concat_axis=0, tiled=True)]
    all_to_all x3 -> x2, waiting for transfers between devices: 92.1 us -> 38.1 us  [a2a(): return lax.all_to_all(value, axes, split_axis=0, concat_axis=0, tiled=True)]
    reduce_sum x3 -> x0, other arithmetic: 3.5 us -> none  [the longest x1 2.54 us: slot_codes(): rank = jnp.sum((same & before).astype(jnp.int32), axis=(2, 3))]
    all_to_all x3 -> x2, starting transfers between devices: 18.7 us -> 16.7 us  [a2a(): return lax.all_to_all(value, axes, split_axis=0, concat_axis=0, tiled=True)]
  transfers between devices with their start and end apart: 4 -> 3, of which waited for: 3 -> 2; matrix products, arithmetic and copies ran while one was open for 2% -> 1% of each run, Pallas kernels for 1% -> 2%
where the time goes in v3:
time: 245 us
  blocking collectives  162 us (66%)
  waiting for transfers between devices  38.1 us (16%)
  starting transfers between devices  25.6 us (10%)
  Pallas kernels  12.1 us (5%)
    all_to_all x4, blocking collectives, a2a(): return lax.all_to_all(value, axes, split_axis=0, concat_axis=0, tiled=True)  162 us
    all_to_all x2, waiting for transfers between devices, a2a(): return lax.all_to_all(value, axes, split_axis=0, concat_axis=0, tiled=True)  38.1 us
    all_to_all x2, starting transfers between devices, a2a(): return lax.all_to_all(value, axes, split_axis=0, concat_axis=0, tiled=True)  16.7 us
    ppermute x1, starting transfers between devices, shards(): partner_proj = lax.ppermute(out_proj, 'side', [(0, 1), (1, 0)])  8.87 us
    pallas_call x1, Pallas kernels, shards(): pl.pallas_call(expert_kernel, grid=(far * slots // tile,), in_specs=[pl.B...  5.45 us
  transfers between devices with their start and end apart: 3, of which 2 were waited for; matrix products, arithmetic and copies ran while one was open for 1% of the time, Pallas kernels for 2%

profile of v3, /device:TPU:1, one launch (start us, length us, event | category | flops | bytes accessed | tf_op | source)
XLA Modules:
  0.0 244.5 jit_solution(2714487174574159399)
XLA Ops:
  0.0 0.0 copy-start.3
  0.0 0.0 copy-start.4
  0.0 8.9 %collective-permute-start = (bf16[1024,1024]{1,0:T(8,128)(2,1)}, bf16[1024,1024]{1,0:T(8,128)(2,1)S(1)}, u32[]{:S(2)}, u32[]{:S(2)}) collective-permute-start(bf16[1024,1024]{1,0:T(8,128)(2,1)} %proj_hbm.1), channel_id=1, source_target_pairs={{0,256},{256,0},{1,257},{257,1},{2,258},{258,2},{3,259},{259,3},{4... | collective-permute-start | bytes 6291464 | tf_op jit(solution)/shard_map/ppermute | solution.py:217
  8.9 0.7 convert_bitcast_fusion.1
  9.6 0.7 pad_maximum_fusion
  10.3 0.1 copy.16
  10.3 0.7 broadcast_in_dim.6
  11.0 10.0 %all-to-all-start = ((f32[16,16,128]{2,1,0:T(8,128)}), f32[16,16,128]{2,1,0:T(8,128)S(1)}, u32[]{:S(2)}, u32[]{:S(2)}) async-start(f32[16,16,128]{2,1,0:T(8,128)} %broadcast_in_dim.6), calls=%async_computation | async-start | bytes 262144 | tf_op jit(solution)/shard_map/all_to_all | solution.py:135
  21.7 3.3 %attention.1 = (bf16[64,1024]{1,0:T(8,128)(2,1)S(1)}, bf16[64,1024]{1,0:T(8,128)(2,1)S(1)}) custom-call(s32[1]{0:T(128)S(6)} %copy.17.len_ref, bf16[1,64,1024]{2,1,0:T(8,128)(2,1)} %q_hbm.1, bf16[1,1,512,128]{3,2,1,0:T(8,128)(2,1)} %k_hbm.1, bf16[1,1,512,128]{3,2,1,0:T(8,128)(2,1)} %v_hbm.1, bf16[1,64,128]{2,1,0:T(8,128)(2,1)} %kn_hbm.1, ...), custom_call_target="tpu_custom_call" | custom-call | flops 400000000 | bytes 3000000 | tf_op jit(solution)/shard_map/attention/pallas_call | solution.py:220
  25.0 7.6 %all-to-all-done.routing_ref = f32[16,16,128]{2,1,0:T(8,128)S(1)} async-done(((f32[16,16,128]{2,1,0:T(8,128)}), f32[16,16,128]{2,1,0:T(8,128)S(1)}, u32[]{:S(2)}, u32[]{:S(2)}) %all-to-all-start) | async-done | bytes 131104 | tf_op jit(solution)/shard_map/all_to_all | solution.py:135
  32.6 0.0 collective-permute-done.proj_any
  32.6 0.6 project.1
  33.3 11.5 %all_to_all.30 = bf16[4,16,2048]{2,1,0:T(8,128)(2,1)S(1)} all-to-all(bf16[4,16,2048]{2,1,0:T(8,128)(2,1)S(1)} %project.1), channel_id=1, replica_groups=mesh['side'=2,'x'=4,'yp'=4,'yq'=2,'zl'=2,'head'=4] {'head'}, dimensions={0} | all-to-all | bytes 524288 | tf_op jit(solution)/shard_map/all_to_all | solution.py:135
  44.8 0.0 copy-done.3
  44.8 0.1 fusion.2
  45.0 0.0 copy-done.4
  45.0 0.1 fusion.4
  45.1 1.1 broadcast_in_dim.8
  46.2 6.7 %all-to-all-start.2 = ((bf16[16,16,2048]{2,1,0:T(8,128)(2,1)}), bf16[16,16,2048]{2,1,0:T(8,128)(2,1)S(1)}, u32[]{:S(2)}, u32[]{:S(2)}) async-start(bf16[16,16,2048]{2,1,0:T(8,128)(2,1)} %broadcast_in_dim.8), calls=%async_computation.2 | async-start | bytes 2097152 | tf_op jit(solution)/shard_map/all_to_all | solution.py:135
  52.8 0.5 tables.1
  53.3 30.5 %all-to-all-done.2 = bf16[16,16,2048]{2,1,0:T(8,128)(2,1)S(1)} async-done(((bf16[16,16,2048]{2,1,0:T(8,128)(2,1)}), bf16[16,16,2048]{2,1,0:T(8,128)(2,1)S(1)}, u32[]{:S(2)}, u32[]{:S(2)}) %all-to-all-start.2) | async-done | bytes 1048608 | tf_op jit(solution)/shard_map/all_to_all | solution.py:135
  83.9 1.3 convolution_convert_fusion
  85.1 0.0 copy-start
  85.1 0.0 copy-start.1
  85.1 0.0 copy-start.2
  85.2 56.7 %all_to_all.31 = bf16[32,32,2048]{2,1,0:T(8,128)(2,1)S(1)} all-to-all(bf16[32,32,2048]{2,1,0:T(8,128)(2,1)S(1)} %bitcast.48), channel_id=1, replica_groups=mesh['side'=2,'x'=4,'yp'=4,'yq'=2,'zl'=2,'head'=4] {'x','yq','zl','side'}, dimensions={0} | all-to-all | bytes 8388608 | tf_op jit(solution)/shard_map/all_to_all | solution.py:135
  141.9 0.0 copy-done
  141.9 0.0 copy-done.1
  141.9 0.0 copy-done.2
  141.9 5.5 %experts.1 = bf16[1024,2048]{1,0:T(8,128)(2,1)} custom-call(bf16[1024,2048]{1,0:T(8,128)(2,1)S(1)} %bitcast.43, bf16[192,2048]{1,0:T(8,128)(2,1)S(1)} %bitcast.45, bf16[192,2048]{1,0:T(8,128)(2,1)S(1)} %bitcast.46, bf16[192,2048]{1,0:T(8,128)(2,1)S(1)} %bitcast.47), custom_call_target="tpu_custom_call" | custom-call | flops 2500000000 | bytes 11000000 | tf_op jit(solution)/shard_map/experts/pallas_call | solution.py:285
  147.4 54.8 %all_to_all.32 = bf16[32,32,2048]{2,1,0:T(8,128)(2,1)S(1)} all-to-all(bf16[32,32,2048]{2,1,0:T(8,128)(2,1)} %bitcast.49), channel_id=1, replica_groups=mesh['side'=2,'x'=4,'yp'=4,'yq'=2,'zl'=2,'head'=4] {'x','yq','zl','side'}, dimensions={0} | all-to-all | bytes 8388608 | tf_op jit(solution)/shard_map/all_to_all | solution.py:135
  202.2 2.2 combine.1
  204.3 39.4 %all_to_all.33 = bf16[16,16,2048]{2,1,0:T(8,128)(2,1)S(1)} all-to-all(bf16[16,16,2048]{2,1,0:T(8,128)(2,1)S(1)} %bitcast.44), channel_id=1, replica_groups=mesh['side'=2,'x'=4,'yp'=4,'yq'=2,'zl'=2,'head'=4] {'head','yp'}, dimensions={0} | all-to-all | bytes 2097152 | tf_op jit(solution)/shard_map/all_to_all | solution.py:135
  243.7 0.1 convert_reduce_fusion
  243.9 0.6 fusion.3
  (3 shorter events, 0.0 us)
Async XLA Ops:
  0.0 44.8 %copy-start.3 = (bf16[1,16,2048]{2,1,0:T(8,128)(2,1)S(1)}, bf16[1,16,2048]{2,1,0:T(8,128)(2,1)}, u32[]{:S(2)}) copy-start(bf16[1,16,2048]{2,1,0:T(8,128)(2,1)} %param.20) | copy-start | bytes 196612
  0.0 45.0 %copy-start.4 = (f32[2048]{0:T(1024)S(1)}, f32[2048]{0:T(1024)}, u32[]{:S(2)}) copy-start(f32[2048]{0:T(1024)} %param.22) | copy-start | bytes 24580
  0.0 32.6 %collective-permute-start = (bf16[1024,1024]{1,0:T(8,128)(2,1)}, bf16[1024,1024]{1,0:T(8,128)(2,1)S(1)}, u32[]{:S(2)}, u32[]{:S(2)}) collective-permute-start(bf16[1024,1024]{1,0:T(8,128)(2,1)} %proj_hbm.1), channel_id=1, source_target_pairs={{0,256},{256,0},{1,257},{257,1},{2,258},{258,2},{3,259},{259,3},{4... | collective-permute-start | bytes 6291464 | tf_op jit(solution)/shard_map/ppermute | solution.py:217
  11.0 21.6 %all-to-all-start = ((f32[16,16,128]{2,1,0:T(8,128)}), f32[16,16,128]{2,1,0:T(8,128)S(1)}, u32[]{:S(2)}, u32[]{:S(2)}) async-start(f32[16,16,128]{2,1,0:T(8,128)} %broadcast_in_dim.6), calls=%async_computation | async-start | bytes 262144 | tf_op jit(solution)/shard_map/all_to_all | solution.py:135
  46.2 37.7 %all-to-all-start.2 = ((bf16[16,16,2048]{2,1,0:T(8,128)(2,1)}), bf16[16,16,2048]{2,1,0:T(8,128)(2,1)S(1)}, u32[]{:S(2)}, u32[]{:S(2)}) async-start(bf16[16,16,2048]{2,1,0:T(8,128)(2,1)} %broadcast_in_dim.8), calls=%async_computation.2 | async-start | bytes 2097152 | tf_op jit(solution)/shard_map/all_to_all | solution.py:135
  85.1 56.8 %copy-start = (bf16[1,2048,192]{1,2,0:T(8,128)(2,1)S(1)}, bf16[1,2048,192]{1,2,0:T(8,128)(2,1)}, u32[]{:S(2)}) copy-start(bf16[1,2048,192]{1,2,0:T(8,128)(2,1)} %param.25) | copy-start | bytes 2359300
  85.1 56.8 %copy-start.1 = (bf16[1,2048,192]{1,2,0:T(8,128)(2,1)S(1)}, bf16[1,2048,192]{1,2,0:T(8,128)(2,1)}, u32[]{:S(2)}) copy-start(bf16[1,2048,192]{1,2,0:T(8,128)(2,1)} %param.26) | copy-start | bytes 2359300
  85.1 56.8 %copy-start.2 = (bf16[1,192,2048]{2,1,0:T(8,128)(2,1)S(1)}, bf16[1,192,2048]{2,1,0:T(8,128)(2,1)}, u32[]{:S(2)}) copy-start(bf16[1,192,2048]{2,1,0:T(8,128)(2,1)} %param.27) | copy-start | bytes 2359300

commit v4 on v3

--- a/solution.py
+++ b/solution.py
@@ -10,6 +10,7 @@
 
 STREAM = ("side", "x", "yp", "yq", "zl")
 NEAR = ("head", "yp")
+BACK = ("yp", "head")
 FAR = ("x", "yq", "zl", "side")
 
 
@@ -135,11 +136,17 @@
     return lax.all_to_all(value, axes, split_axis=0, concat_axis=0, tiled=True)
 
 
-def table_kernel(part_ref, routing_ref, dispatch_ref, combine_ref):
-    top_k = routing_ref.shape[2] // 16
+def table_kernel(place_ref, routing_ref, dispatch_ref, combine_ref, sorted_ref):
     blocks, block = routing_ref.shape[0], routing_ref.shape[1]
+    top_k = 8
     rows = blocks * block
-    columns = jnp.transpose(routing_ref[...].reshape(rows, routing_ref.shape[2]))
+    heads = 4
+    for step in range(blocks):
+        from_head = place_ref[0] ^ (step % heads)
+        from_part = place_ref[1] ^ (step // heads)
+        at = pl.multiple_of((from_head * (blocks // heads) + from_part) * block, block)
+        sorted_ref[pl.ds(at, block), :] = routing_ref[step]
+    columns = jnp.transpose(sorted_ref[...])
     chosen = columns[:top_k]
     weights = columns[top_k : 2 * top_k]
     mixing = (weights / jnp.sum(weights, axis=0, keepdims=True)).astype(jnp.bfloat16)
@@ -150,7 +157,7 @@
     at_z = (place // sides) % zs
     at_q = (place // (sides * zs)) % qs
     at_x = place // (sides * zs * qs)
-    expert = (((place % sides) * xs + at_x) * (ps * qs) + part_ref[0] * qs + at_q) * zs + at_z
+    expert = (((place % sides) * xs + at_x) * (ps * qs) + place_ref[1] * qs + at_q) * zs + at_z
     expert = expert.astype(jnp.float32)
     named = jnp.zeros((local, rows), jnp.float32)
     weight = jnp.zeros((local, rows), jnp.float32)
@@ -181,9 +188,12 @@
                 ).astype(jnp.bfloat16)
                 tiles.append(jnp.where(own, jnp.where(takes, weight[e : e + 1], 0.0), 0.0))
         at = 2 * start * blocks
-        combine_ref[:, at : at + 128] = jnp.transpose(jnp.concatenate(tiles, axis=0)).astype(
-            jnp.bfloat16
-        )
+        turned = jnp.transpose(jnp.concatenate(tiles, axis=0)).astype(jnp.bfloat16)
+        for source in range(blocks):
+            target = (source % (blocks // heads)) * heads + source // (blocks // heads)
+            combine_ref[target * block : (target + 1) * block, at : at + 128] = turned[
+                source * block : (source + 1) * block
+            ]
 
 
 def shards(
@@ -213,7 +223,6 @@
     top_k = expert_ids.shape[2]
     routing = jnp.concatenate([expert_ids[0].astype(jnp.float32), gate_wts[0]], axis=1)
     routing = jnp.pad(routing, ((0, 0), (0, 128 - 2 * top_k)))
-    routing = a2a(jnp.broadcast_to(routing[None], (near,) + routing.shape), NEAR)
     partner_proj = lax.ppermute(out_proj, "side", [(0, 1), (1, 0)])
     half = out_proj.shape[1]
     rows_here = q_new.shape[1]
@@ -242,7 +251,6 @@
             for value in (q_new, k_cache, value_cache, k_new, new_value_rows, out_proj)
         ),
     )
-    partner_proj, routing = lax.optimization_barrier((partner_proj, routing))
     full_rows = pl.pallas_call(
         project_kernel,
         in_specs=[in_smem(), in_vmem(), pl.BlockSpec(memory_space=pl.ANY), in_vmem()],
@@ -261,8 +269,14 @@
         resid * lax.rsqrt(jnp.mean(resid * resid, axis=-1, keepdims=True) + 1e-06) * norm_gain
     ).astype(jnp.bfloat16)
 
-    rows = a2a(jnp.broadcast_to(normed[None], (near,) + normed.shape), NEAR)
+    spread = jnp.broadcast_to(normed[None], (near,) + normed.shape)
+    spread, routing = lax.optimization_barrier((spread, routing[None]))
+    rows = a2a(spread, NEAR)
     rows = rows.reshape(near * block, width)
+    for axis in ("head", "yp"):
+        for bit in (1, 2):
+            pairs = [(i, i ^ bit) for i in range(lax.axis_size(axis))]
+            routing = jnp.concatenate([routing, lax.ppermute(routing, axis, pairs)], axis=0)
     dispatch, combine = pl.pallas_call(
         table_kernel,
         in_specs=[in_smem(), in_vmem()],
@@ -272,11 +286,12 @@
             jax.ShapeDtypeStruct((near * block, far * slots), jnp.bfloat16),
         ],
         cost_estimate=pl.CostEstimate(
-            flops=1_000_000_000, bytes_accessed=1_200_000, transcendentals=0
-        ),
+            flops=200_000_000, bytes_accessed=1_200_000, transcendentals=0
+        ),
+        scratch_shapes=[pltpu.VMEM((near * block, 128), jnp.float32)],
         compiler_params=pltpu.CompilerParams(vmem_limit_bytes=12 << 20),
         name="tables",
-    )(lax.axis_index("yp").reshape(1), routing)
+    )(jnp.stack([lax.axis_index("head"), lax.axis_index("yp")]), routing)
 
     outgoing = jnp.dot(dispatch, rows, preferred_element_type=jnp.float32).astype(jnp.bfloat16)
     flat_rows = a2a(outgoing.reshape(far, slots, width), FAR).reshape(far * slots, width)
@@ -316,7 +331,7 @@
         compiler_params=pltpu.CompilerParams(vmem_limit_bytes=16 << 20),
         name="combine",
     )(combine, returned)
-    parts = a2a(weighted.reshape(near, block, width), NEAR)
+    parts = a2a(weighted.reshape(near, block, width), BACK)
     moe_out = jnp.sum(parts.astype(jnp.float32), axis=0)
     return (resid + moe_out).astype(jnp.bfloat16)[None]
 

time: 245 us -> 260 us (1.061); the launches traced: 245 us -> 256 us
  starting transfers between devices: 25.6 us -> 58.5 us
  waiting for transfers between devices: 38.1 us -> 18.5 us
    ppermute x0 -> x4, starting transfers between devices: none -> 34.9 us  [shards(): lax.ppermute(routing, axis, pairs)]
    all_to_all x2, waiting for transfers between devices: 38.1 us -> 8.43 us  [a2a(): return lax.all_to_all(value, axes, split_axis=0, concat_axis=0, tiled=True)]
    ppermute x0 -> x4, waiting for transfers between devices: none -> 10 us  [shards(): lax.ppermute(routing, axis, pairs)]
    all_to_all x4 -> x3, blocking collectives: 162 us -> 161 us  [a2a(): return lax.all_to_all(value, axes, split_axis=0, concat_axis=0, tiled=True)]
  transfers between devices with their start and end apart: 3 -> 7, of which waited for: 2 -> 5; matrix products, arithmetic and copies ran while one was open for 1% -> 0% of each run, Pallas kernels for 2% -> 2%
where the time goes in v4:
time: 260 us; the launch traced here: 256 us
  blocking collectives  161 us (62%)
  starting transfers between devices  58.5 us (22%)
  waiting for transfers between devices  18.5 us (7%)
  Pallas kernels  13.3 us (5%)
    all_to_all x3, blocking collectives, a2a(): return lax.all_to_all(value, axes, split_axis=0, concat_axis=0, tiled=True)  161 us
    ppermute x4, starting transfers between devices, shards(): lax.ppermute(routing, axis, pairs)  34.9 us
    all_to_all x2, starting transfers between devices, a2a(): return lax.all_to_all(value, axes, split_axis=0, concat_axis=0, tiled=True)  14.7 us
    ppermute x4, waiting for transfers between devices, shards(): lax.ppermute(routing, axis, pairs)  10 us
    ppermute x1, starting transfers between devices, shards(): partner_proj = lax.ppermute(out_proj, 'side', [(0, 1), (1, 0)])  8.86 us
    all_to_all x2, waiting for transfers between devices, a2a(): return lax.all_to_all(value, axes, split_axis=0, concat_axis=0, tiled=True)  8.43 us
    pallas_call x1, Pallas kernels, shards(): pl.pallas_call(expert_kernel, grid=(far * slots // tile,), in_specs=[pl.B...  5.46 us
  transfers between devices with their start and end apart: 7, of which 5 were waited for; matrix products, arithmetic and copies ran while one was open for 0% of the time, Pallas kernels for 2%

profile of v4, /device:TPU:1, one launch (start us, length us, event | category | flops | bytes accessed | tf_op | source)
XLA Modules:
  0.0 256.0 jit_solution(7447536422647158223)
XLA Ops:
  0.0 0.0 copy-start.6
  0.0 0.0 copy-start.5
  0.0 0.0 copy-start.3
  0.0 0.0 copy-start.4
  0.0 8.9 %collective-permute-start = (bf16[1024,1024]{1,0:T(8,128)(2,1)}, bf16[1024,1024]{1,0:T(8,128)(2,1)S(1)}, u32[]{:S(2)}, u32[]{:S(2)}) collective-permute-start(bf16[1024,1024]{1,0:T(8,128)(2,1)} %proj_hbm.1), channel_id=1, source_target_pairs={{0,256},{256,0},{1,257},{257,1},{2,258},{258,2},{3,259},{259,3},{4... | collective-permute-start | bytes 6291464 | tf_op jit(solution)/shard_map/ppermute | solution.py:226
  9.5 3.3 %attention.1 = (bf16[64,1024]{1,0:T(8,128)(2,1)S(1)}, bf16[64,1024]{1,0:T(8,128)(2,1)S(1)}) custom-call(s32[1]{0:T(128)S(6)} %copy.21.len_ref, bf16[1,64,1024]{2,1,0:T(8,128)(2,1)} %q_hbm.1, bf16[1,1,512,128]{3,2,1,0:T(8,128)(2,1)} %k_hbm.1, bf16[1,1,512,128]{3,2,1,0:T(8,128)(2,1)} %v_hbm.1, bf16[1,64,128]{2,1,0:T(8,128)(2,1)} %kn_hbm.1, ...), custom_call_target="tpu_custom_call" | custom-call | flops 400000000 | bytes 3000000 | tf_op jit(solution)/shard_map/attention/pallas_call | solution.py:229
  12.9 0.0 collective-permute-done.proj_any
  12.9 1.3 project.1
  14.2 4.7 %all-to-all-start = ((bf16[4,16,2048]{2,1,0:T(8,128)(2,1)}), bf16[4,16,2048]{2,1,0:T(8,128)(2,1)S(1)}, u32[]{:S(2)}, u32[]{:S(2)}) async-start(bf16[4,16,2048]{2,1,0:T(8,128)(2,1)} %project.1), calls=%async_computation | async-start | bytes 524288 | tf_op jit(solution)/shard_map/all_to_all | solution.py:136
  18.9 0.0 copy-done.6
  18.9 0.1 copy.15
  19.0 0.0 copy-done.5
  19.0 0.1 copy.16
  19.1 0.1 fusion.5
  19.2 8.4 %all-to-all-done = bf16[4,16,2048]{2,1,0:T(8,128)(2,1)S(1)} async-done(((bf16[4,16,2048]{2,1,0:T(8,128)(2,1)}), bf16[4,16,2048]{2,1,0:T(8,128)(2,1)S(1)}, u32[]{:S(2)}, u32[]{:S(2)}) %all-to-all-start) | async-done | bytes 262176 | tf_op jit(solution)/shard_map/all_to_all | solution.py:136
  27.6 0.0 copy-done.3
  27.6 0.1 fusion.2
  27.8 0.0 copy-done.4
  27.8 0.1 fusion.4
  27.9 1.1 broadcast_in_dim.7
  29.0 10.0 %all-to-all-start.1 = ((bf16[16,16,2048]{2,1,0:T(8,128)(2,1)}), bf16[16,16,2048]{2,1,0:T(8,128)(2,1)S(1)}, u32[]{:S(2)}, u32[]{:S(2)}) async-start(bf16[16,16,2048]{2,1,0:T(8,128)(2,1)} %broadcast_in_dim.7), calls=%async_computation.1 | async-start | bytes 2097152 | tf_op jit(solution)/shard_map/all_to_all | solution.py:136
  39.0 0.1 pad_add_fusion.place_ref
  39.1 4.2 %collective-permute-start.1 = (f32[1,16,128]{2,1,0:T(8,128)S(1)}, f32[1,16,128]{2,1,0:T(8,128)S(1)}, u32[]{:S(2)}, u32[]{:S(2)}) collective-permute-start(f32[1,16,128]{2,1,0:T(8,128)S(1)} %fusion.5), channel_id=1, source_target_pairs={{0,1},{1,0},{2,3},{3,2},{4,5},{5,4},{6,7},{7,6},{8,9},{9,8},{10,11... | collective-permute-start | bytes 24584 | tf_op jit(solution)/shard_map/ppermute | solution.py:279
  43.2 1.9 collective-permute-done.1
  45.1 6.8 %collective-permute-start.2 = (f32[2,16,128]{2,1,0:T(8,128)S(1)}, f32[2,16,128]{2,1,0:T(8,128)S(1)}, u32[]{:S(2)}, u32[]{:S(2)}) collective-permute-start(f32[2,16,128]{2,1,0:T(8,128)S(1)} %pad_maximum_fusion.2), channel_id=1, source_target_pairs={{0,2},{1,3},{2,0},{3,1},{4,6},{5,7},{6,4},{7,5},{8,10},{9,11},{10,... | collective-permute-start | bytes 49160 | tf_op jit(solution)/shard_map/ppermute | solution.py:279
  51.9 2.6 %collective-permute-done.2 = f32[2,16,128]{2,1,0:T(8,128)S(1)} collective-permute-done((f32[2,16,128]{2,1,0:T(8,128)S(1)}, f32[2,16,128]{2,1,0:T(8,128)S(1)}, u32[]{:S(2)}, u32[]{:S(2)}) %collective-permute-start.2) | collective-permute-done | bytes 16416 | tf_op jit(solution)/shard_map/ppermute | solution.py:279
  54.6 6.2 %collective-permute-start.3 = (f32[4,16,128]{2,1,0:T(8,128)S(1)}, f32[4,16,128]{2,1,0:T(8,128)S(1)}, u32[]{:S(2)}, u32[]{:S(2)}) collective-permute-start(f32[4,16,128]{2,1,0:T(8,128)S(1)} %pad_maximum_fusion.1), channel_id=1, source_target_pairs={{0,16},{16,0},{32,48},{48,32},{1,17},{17,1},{33,49},{49,33},{2,18}... | collective-permute-start | bytes 98312 | tf_op jit(solution)/shard_map/ppermute | solution.py:279
  60.8 3.9 %collective-permute-done.3 = f32[4,16,128]{2,1,0:T(8,128)S(1)} collective-permute-done((f32[4,16,128]{2,1,0:T(8,128)S(1)}, f32[4,16,128]{2,1,0:T(8,128)S(1)}, u32[]{:S(2)}, u32[]{:S(2)}) %collective-permute-start.3) | collective-permute-done | bytes 32800 | tf_op jit(solution)/shard_map/ppermute | solution.py:279
  64.7 17.8 %collective-permute-start.4 = (f32[8,16,128]{2,1,0:T(8,128)S(1)}, f32[8,16,128]{2,1,0:T(8,128)S(1)}, u32[]{:S(2)}, u32[]{:S(2)}) collective-permute-start(f32[8,16,128]{2,1,0:T(8,128)S(1)} %pad_maximum_fusion), channel_id=1, source_target_pairs={{0,32},{16,48},{32,0},{48,16},{1,33},{17,49},{33,1},{49,17},{2,34}... | collective-permute-start | bytes 196616 | tf_op jit(solution)/shard_map/ppermute | solution.py:279
  82.4 1.6 collective-permute-done.4
  84.1 1.1 tables.1
  85.1 0.0 all-to-all-done.1
  85.1 1.3 convolution_convert_fusion
  86.4 0.0 copy-start
  86.4 0.0 copy-start.1
  86.4 0.0 copy-start.2
  86.4 66.7 %all_to_all.25 = bf16[32,32,2048]{2,1,0:T(8,128)(2,1)S(1)} all-to-all(bf16[32,32,2048]{2,1,0:T(8,128)(2,1)S(1)} %bitcast.51), channel_id=1, replica_groups=mesh['side'=2,'x'=4,'yp'=4,'yq'=2,'zl'=2,'head'=4] {'x','yq','zl','side'}, dimensions={0} | all-to-all | bytes 8388608 | tf_op jit(solution)/shard_map/all_to_all | solution.py:136
  153.1 0.0 copy-done
  153.1 0.0 copy-done.1
  153.1 0.0 copy-done.2
  153.1 5.5 %experts.1 = bf16[1024,2048]{1,0:T(8,128)(2,1)} custom-call(bf16[1024,2048]{1,0:T(8,128)(2,1)S(1)} %bitcast.46, bf16[192,2048]{1,0:T(8,128)(2,1)S(1)} %bitcast.48, bf16[192,2048]{1,0:T(8,128)(2,1)S(1)} %bitcast.49, bf16[192,2048]{1,0:T(8,128)(2,1)S(1)} %bitcast.50), custom_call_target="tpu_custom_call" | custom-call | flops 2500000000 | bytes 11000000 | tf_op jit(solution)/shard_map/experts/pallas_call | solution.py:300
  158.6 54.8 %all_to_all.26 = bf16[32,32,2048]{2,1,0:T(8,128)(2,1)S(1)} all-to-all(bf16[32,32,2048]{2,1,0:T(8,128)(2,1)} %bitcast.52), channel_id=1, replica_groups=mesh['side'=2,'x'=4,'yp'=4,'yq'=2,'zl'=2,'head'=4] {'x','yq','zl','side'}, dimensions={0} | all-to-all | bytes 8388608 | tf_op jit(solution)/shard_map/all_to_all | solution.py:136
  213.4 2.2 combine.1
  215.6 39.6 %all_to_all.27 = bf16[16,16,2048]{2,1,0:T(8,128)(2,1)S(1)} all-to-all(bf16[16,16,2048]{2,1,0:T(8,128)(2,1)S(1)} %bitcast.47), channel_id=1, replica_groups=mesh['side'=2,'x'=4,'yp'=4,'yq'=2,'zl'=2,'head'=4] {'yp','head'}, dimensions={0} | all-to-all | bytes 2097152 | tf_op jit(solution)/shard_map/all_to_all | solution.py:136
  255.2 0.1 convert_reduce_fusion
  255.3 0.6 fusion.3
  (11 shorter events, 0.1 us)
Async XLA Ops:
  0.0 18.9 %copy-start.6 = (s32[1,16,8]{1,2,0:T(8,128)S(1)}, s32[1,16,8]{1,2,0:T(8,128)}, u32[]{:S(2)}) copy-start(s32[1,16,8]{1,2,0:T(8,128)} %param.23) | copy-start | bytes 1540
  0.0 19.0 %copy-start.5 = (f32[1,16,8]{1,2,0:T(8,128)S(1)}, f32[1,16,8]{1,2,0:T(8,128)}, u32[]{:S(2)}) copy-start(f32[1,16,8]{1,2,0:T(8,128)} %param.24) | copy-start | bytes 1540
  0.0 27.6 %copy-start.3 = (bf16[1,16,2048]{2,1,0:T(8,128)(2,1)S(1)}, bf16[1,16,2048]{2,1,0:T(8,128)(2,1)}, u32[]{:S(2)}) copy-start(bf16[1,16,2048]{2,1,0:T(8,128)(2,1)} %param.20) | copy-start | bytes 196612
  0.0 27.8 %copy-start.4 = (f32[2048]{0:T(1024)S(1)}, f32[2048]{0:T(1024)}, u32[]{:S(2)}) copy-start(f32[2048]{0:T(1024)} %param.22) | copy-start | bytes 24580
  0.0 12.9 %collective-permute-start = (bf16[1024,1024]{1,0:T(8,128)(2,1)}, bf16[1024,1024]{1,0:T(8,128)(2,1)S(1)}, u32[]{:S(2)}, u32[]{:S(2)}) collective-permute-start(bf16[1024,1024]{1,0:T(8,128)(2,1)} %proj_hbm.1), channel_id=1, source_target_pairs={{0,256},{256,0},{1,257},{257,1},{2,258},{258,2},{3,259},{259,3},{4... | collective-permute-start | bytes 6291464 | tf_op jit(solution)/shard_map/ppermute | solution.py:226
  14.2 13.4 %all-to-all-start = ((bf16[4,16,2048]{2,1,0:T(8,128)(2,1)}), bf16[4,16,2048]{2,1,0:T(8,128)(2,1)S(1)}, u32[]{:S(2)}, u32[]{:S(2)}) async-start(bf16[4,16,2048]{2,1,0:T(8,128)(2,1)} %project.1), calls=%async_computation | async-start | bytes 524288 | tf_op jit(solution)/shard_map/all_to_all | solution.py:136
  29.0 56.2 %all-to-all-start.1 = ((bf16[16,16,2048]{2,1,0:T(8,128)(2,1)}), bf16[16,16,2048]{2,1,0:T(8,128)(2,1)S(1)}, u32[]{:S(2)}, u32[]{:S(2)}) async-start(bf16[16,16,2048]{2,1,0:T(8,128)(2,1)} %broadcast_in_dim.7), calls=%async_computation.1 | async-start | bytes 2097152 | tf_op jit(solution)/shard_map/all_to_all | solution.py:136
  39.1 6.1 %collective-permute-start.1 = (f32[1,16,128]{2,1,0:T(8,128)S(1)}, f32[1,16,128]{2,1,0:T(8,128)S(1)}, u32[]{:S(2)}, u32[]{:S(2)}) collective-permute-start(f32[1,16,128]{2,1,0:T(8,128)S(1)} %fusion.5), channel_id=1, source_target_pairs={{0,1},{1,0},{2,3},{3,2},{4,5},{5,4},{6,7},{7,6},{8,9},{9,8},{10,11... | collective-permute-start | bytes 24584 | tf_op jit(solution)/shard_map/ppermute | solution.py:279
  45.1 9.4 %collective-permute-start.2 = (f32[2,16,128]{2,1,0:T(8,128)S(1)}, f32[2,16,128]{2,1,0:T(8,128)S(1)}, u32[]{:S(2)}, u32[]{:S(2)}) collective-permute-start(f32[2,16,128]{2,1,0:T(8,128)S(1)} %pad_maximum_fusion.2), channel_id=1, source_target_pairs={{0,2},{1,3},{2,0},{3,1},{4,6},{5,7},{6,4},{7,5},{8,10},{9,11},{10,... | collective-permute-start | bytes 49160 | tf_op jit(solution)/shard_map/ppermute | solution.py:279
  54.6 10.1 %collective-permute-start.3 = (f32[4,16,128]{2,1,0:T(8,128)S(1)}, f32[4,16,128]{2,1,0:T(8,128)S(1)}, u32[]{:S(2)}, u32[]{:S(2)}) collective-permute-start(f32[4,16,128]{2,1,0:T(8,128)S(1)} %pad_maximum_fusion.1), channel_id=1, source_target_pairs={{0,16},{16,0},{32,48},{48,32},{1,17},{17,1},{33,49},{49,33},{2,18}... | collective-permute-start | bytes 98312 | tf_op jit(solution)/shard_map/ppermute | solution.py:279
  64.7 19.4 %collective-permute-start.4 = (f32[8,16,128]{2,1,0:T(8,128)S(1)}, f32[8,16,128]{2,1,0:T(8,128)S(1)}, u32[]{:S(2)}, u32[]{:S(2)}) collective-permute-start(f32[8,16,128]{2,1,0:T(8,128)S(1)} %pad_maximum_fusion), channel_id=1, source_target_pairs={{0,32},{16,48},{32,0},{48,16},{1,33},{17,49},{33,1},{49,17},{2,34}... | collective-permute-start | bytes 196616 | tf_op jit(solution)/shard_map/ppermute | solution.py:279
  86.4 66.7 %copy-start = (bf16[1,2048,192]{1,2,0:T(8,128)(2,1)S(1)}, bf16[1,2048,192]{1,2,0:T(8,128)(2,1)}, u32[]{:S(2)}) copy-start(bf16[1,2048,192]{1,2,0:T(8,128)(2,1)} %param.25) | copy-start | bytes 2359300
  86.4 66.7 %copy-start.1 = (bf16[1,2048,192]{1,2,0:T(8,128)(2,1)S(1)}, bf16[1,2048,192]{1,2,0:T(8,128)(2,1)}, u32[]{:S(2)}) copy-start(bf16[1,2048,192]{1,2,0:T(8,128)(2,1)} %param.26) | copy-start | bytes 2359300
  86.4 66.7 %copy-start.2 = (bf16[1,192,2048]{2,1,0:T(8,128)(2,1)S(1)}, bf16[1,192,2048]{2,1,0:T(8,128)(2,1)}, u32[]{:S(2)}) copy-start(bf16[1,192,2048]{2,1,0:T(8,128)(2,1)} %param.27) | copy-start | bytes 2359300

commit v5 on v3

--- a/solution.py
+++ b/solution.py
@@ -107,20 +107,34 @@
 
 
 def expert_kernel(rows_ref, gate_ref, up_ref, down_ref, out_ref):
+    tile = 256
     contract = (((1,), (1,)), ((), ()))
-    rows = rows_ref[...]
-    gate = lax.dot_general(rows, gate_ref[...], contract, preferred_element_type=jnp.float32)
-    up = lax.dot_general(rows, up_ref[...], contract, preferred_element_type=jnp.float32)
-    hidden = (gate / (1.0 + jnp.exp(-gate)) * up).astype(jnp.bfloat16)
-    out_ref[...] = jnp.dot(hidden, down_ref[...], preferred_element_type=jnp.float32).astype(
-        jnp.bfloat16
-    )
+
+    def step(index, carry):
+        take = pl.ds(pl.multiple_of(index * tile, tile), tile)
+        rows = rows_ref[take, :]
+        gate = lax.dot_general(rows, gate_ref[...], contract, preferred_element_type=jnp.float32)
+        up = lax.dot_general(rows, up_ref[...], contract, preferred_element_type=jnp.float32)
+        hidden = (gate / (1.0 + jnp.exp(-gate)) * up).astype(jnp.bfloat16)
+        out_ref[take, :] = jnp.dot(
+            hidden, down_ref[...], preferred_element_type=jnp.float32
+        ).astype(jnp.bfloat16)
+        return carry
+
+    lax.fori_loop(0, rows_ref.shape[0] // tile, step, 0)
 
 
 def combine_kernel(combine_ref, rows_ref, out_ref):
-    out_ref[...] = jnp.dot(
-        combine_ref[...], rows_ref[...], preferred_element_type=jnp.float32
-    ).astype(jnp.bfloat16)
+    tile = 512
+
+    def step(index, carry):
+        take = pl.ds(pl.multiple_of(index * tile, tile), tile)
+        out_ref[:, take] = jnp.dot(
+            combine_ref[...], rows_ref[:, take], preferred_element_type=jnp.float32
+        ).astype(jnp.bfloat16)
+        return carry
+
+    lax.fori_loop(0, rows_ref.shape[1] // tile, step, 0)
 
 
 def in_vmem():
@@ -135,15 +149,13 @@
     return lax.all_to_all(value, axes, split_axis=0, concat_axis=0, tiled=True)
 
 
-def table_kernel(part_ref, routing_ref, dispatch_ref, combine_ref):
-    top_k = routing_ref.shape[2] // 16
-    blocks, block = routing_ref.shape[0], routing_ref.shape[1]
-    rows = blocks * block
-    columns = jnp.transpose(routing_ref[...].reshape(rows, routing_ref.shape[2]))
+def dispatch_kernel(part_ref, gathered_ref, out_ref, combine_ref, dispatch_ref):
+    top_k, block = 8, 16
+    rows, width = gathered_ref.shape[0], gathered_ref.shape[1] - 128
+    blocks = rows // block
+    columns = jnp.transpose(gathered_ref[:, width:].astype(jnp.float32))
     chosen = columns[:top_k]
-    weights = columns[top_k : 2 * top_k]
-    mixing = (weights / jnp.sum(weights, axis=0, keepdims=True)).astype(jnp.bfloat16)
-    mixing = mixing.astype(jnp.float32)
+    mixing = columns[top_k : 2 * top_k]
     sides, xs, ps, qs, zs = 2, 4, 4, 2, 2
     local = sides * xs * qs * zs
     place = lax.broadcasted_iota(jnp.int32, (local, rows), 0)
@@ -181,9 +193,18 @@
                 ).astype(jnp.bfloat16)
                 tiles.append(jnp.where(own, jnp.where(takes, weight[e : e + 1], 0.0), 0.0))
         at = 2 * start * blocks
-        combine_ref[:, at : at + 128] = jnp.transpose(jnp.concatenate(tiles, axis=0)).astype(
-            jnp.bfloat16
-        )
+        turned = jnp.transpose(jnp.concatenate(tiles, axis=0)).astype(jnp.bfloat16)
+        combine_ref[:, at : at + 128] = turned
+    tile = 256
+
+    def step(index, carry):
+        take = pl.ds(pl.multiple_of(index * tile, tile), tile)
+        out_ref[take, :] = jnp.dot(
+            dispatch_ref[take, :], gathered_ref[:, :width], preferred_element_type=jnp.float32
+        ).astype(jnp.bfloat16)
+        return carry
+
+    lax.fori_loop(0, out_ref.shape[0] // tile, step, 0)
 
 
 def shards(
@@ -210,10 +231,6 @@
     far = lax.axis_size(FAR)
     slots = 2 * near
 
-    top_k = expert_ids.shape[2]
-    routing = jnp.concatenate([expert_ids[0].astype(jnp.float32), gate_wts[0]], axis=1)
-    routing = jnp.pad(routing, ((0, 0), (0, 128 - 2 * top_k)))
-    routing = a2a(jnp.broadcast_to(routing[None], (near,) + routing.shape), NEAR)
     partner_proj = lax.ppermute(out_proj, "side", [(0, 1), (1, 0)])
     half = out_proj.shape[1]
     rows_here = q_new.shape[1]
@@ -242,7 +259,6 @@
             for value in (q_new, k_cache, value_cache, k_new, new_value_rows, out_proj)
         ),
     )
-    partner_proj, routing = lax.optimization_barrier((partner_proj, routing))
     full_rows = pl.pallas_call(
         project_kernel,
         in_specs=[in_smem(), in_vmem(), pl.BlockSpec(memory_space=pl.ANY), in_vmem()],
@@ -261,38 +277,34 @@
         resid * lax.rsqrt(jnp.mean(resid * resid, axis=-1, keepdims=True) + 1e-06) * norm_gain
     ).astype(jnp.bfloat16)
 
-    rows = a2a(jnp.broadcast_to(normed[None], (near,) + normed.shape), NEAR)
-    rows = rows.reshape(near * block, width)
-    dispatch, combine = pl.pallas_call(
-        table_kernel,
+    raw_wts = gate_wts[0]
+    mixing = (raw_wts / jnp.sum(raw_wts, axis=-1, keepdims=True)).astype(jnp.bfloat16)
+    routing = jnp.concatenate([expert_ids[0].astype(jnp.bfloat16), mixing], axis=1)
+    routing = jnp.pad(routing, ((0, 0), (0, 128 - routing.shape[1])))
+    payload = jnp.concatenate([normed, routing], axis=1)
+    gathered = a2a(jnp.broadcast_to(payload[None], (near,) + payload.shape), NEAR)
+    outgoing, combine = pl.pallas_call(
+        dispatch_kernel,
         in_specs=[in_smem(), in_vmem()],
         out_specs=[in_vmem()] * 2,
         out_shape=[
-            jax.ShapeDtypeStruct((far * slots, near * block), jnp.bfloat16),
+            jax.ShapeDtypeStruct((far * slots, width), jnp.bfloat16),
             jax.ShapeDtypeStruct((near * block, far * slots), jnp.bfloat16),
         ],
         cost_estimate=pl.CostEstimate(
-            flops=1_000_000_000, bytes_accessed=1_200_000, transcendentals=0
-        ),
-        compiler_params=pltpu.CompilerParams(vmem_limit_bytes=12 << 20),
-        name="tables",
-    )(lax.axis_index("yp").reshape(1), routing)
-
-    outgoing = jnp.dot(dispatch, rows, preferred_element_type=jnp.float32).astype(jnp.bfloat16)
+            flops=1_200_000_000, bytes_accessed=6_000_000, transcendentals=0
+        ),
+        scratch_shapes=[pltpu.VMEM((far * slots, near * block), jnp.bfloat16)],
+        compiler_params=pltpu.CompilerParams(vmem_limit_bytes=20 << 20),
+        name="dispatch",
+    )(lax.axis_index("yp").reshape(1), gathered.reshape(near * block, width + 128))
+
     flat_rows = a2a(outgoing.reshape(far, slots, width), FAR).reshape(far * slots, width)
-    tile = 256
-    part = w_gate.shape[2]
     partial_value = pl.pallas_call(
         expert_kernel,
-        grid=(far * slots // tile,),
-        in_specs=[
-            pl.BlockSpec((tile, width), lambda i: (i, 0)),
-            pl.BlockSpec((part, width), lambda i: (0, 0)),
-            pl.BlockSpec((part, width), lambda i: (0, 0)),
-            pl.BlockSpec((part, width), lambda i: (0, 0)),
-        ],
-        out_specs=pl.BlockSpec((tile, width), lambda i: (i, 0)),
-        out_shape=pltpu.HBM((far * slots, width), jnp.bfloat16),
+        in_specs=[in_vmem()] * 4,
+        out_specs=in_vmem(),
+        out_shape=jax.ShapeDtypeStruct((far * slots, width), jnp.bfloat16),
         cost_estimate=pl.CostEstimate(
             flops=2_500_000_000, bytes_accessed=11_000_000, transcendentals=200_000
         ),
@@ -300,15 +312,10 @@
         name="experts",
     )(flat_rows, w_gate[0].T, w_up[0].T, w_down[0])
     returned = a2a(partial_value.reshape(far, slots, width), FAR).reshape(far * slots, width)
-    columns = 512
     weighted = pl.pallas_call(
         combine_kernel,
-        grid=(width // columns,),
-        in_specs=[
-            pl.BlockSpec((near * block, far * slots), lambda i: (0, 0)),
-            pl.BlockSpec((far * slots, columns), lambda i: (0, i)),
-        ],
-        out_specs=pl.BlockSpec((near * block, columns), lambda i: (0, i)),
+        in_specs=[in_vmem()] * 2,
+        out_specs=in_vmem(),
         out_shape=jax.ShapeDtypeStruct((near * block, width), jnp.bfloat16),
         cost_estimate=pl.CostEstimate(
             flops=1_100_000_000, bytes_accessed=6_000_000, transcendentals=0

time: 245 us -> 234 us (0.955)
  blocking collectives: 162 us -> 150 us
  waiting for transfers between devices: 38.1 us -> 43.3 us
    all_to_all x4 -> x3, blocking collectives: 162 us -> 150 us  [a2a(): return lax.all_to_all(value, axes, split_axis=0, concat_axis=0, tiled=True)]
    all_to_all x2, waiting for transfers between devices: 38.1 us -> 43.3 us  [a2a(): return lax.all_to_all(value, axes, split_axis=0, concat_axis=0, tiled=True)]
  transfers between devices with their start and end apart: 3 -> 3, of which waited for: 2 -> 2; matrix products, arithmetic and copies ran while one was open for 1% -> 0% of each run, Pallas kernels for 2% -> 1%
where the time goes in v5:
time: 234 us; the launch traced here: 233 us
  blocking collectives  150 us (64%)
  waiting for transfers between devices  43.3 us (19%)
  starting transfers between devices  23.4 us (10%)
  Pallas kernels  13.1 us (6%)
    all_to_all x3, blocking collectives, a2a(): return lax.all_to_all(value, axes, split_axis=0, concat_axis=0, tiled=True)  150 us
    all_to_all x2, waiting for transfers between devices, a2a(): return lax.all_to_all(value, axes, split_axis=0, concat_axis=0, tiled=True)  43.3 us
    all_to_all x2, starting transfers between devices, a2a(): return lax.all_to_all(value, axes, split_axis=0, concat_axis=0, tiled=True)  14.6 us
    ppermute x1, starting transfers between devices, shards(): partner_proj = lax.ppermute(out_proj, 'side', [(0, 1), (1, 0)])  8.73 us
  transfers between devices with their start and end apart: 3, of which 2 were waited for; matrix products, arithmetic and copies ran while one was open for 0% of the time, Pallas kernels for 1%

profile of v5, /device:TPU:1, one launch (start us, length us, event | category | flops | bytes accessed | tf_op | source)
XLA Modules:
  0.0 233.3 jit_solution(11847989628859006138)
XLA Ops:
  0.0 8.7 %collective-permute-start = (bf16[1024,1024]{1,0:T(8,128)(2,1)}, bf16[1024,1024]{1,0:T(8,128)(2,1)S(1)}, u32[]{:S(2)}, u32[]{:S(2)}) collective-permute-start(bf16[1024,1024]{1,0:T(8,128)(2,1)} %proj_hbm.1), channel_id=1, source_target_pairs={{0,256},{256,0},{1,257},{257,1},{2,258},{258,2},{3,259},{259,3},{4... | collective-permute-start | bytes 6291464 | tf_op jit(solution)/shard_map/ppermute | solution.py:234
  9.4 3.3 %attention.1 = (bf16[64,1024]{1,0:T(8,128)(2,1)S(1)}, bf16[64,1024]{1,0:T(8,128)(2,1)S(1)}) custom-call(s32[1]{0:T(128)S(6)} %copy.17.len_ref, bf16[1,64,1024]{2,1,0:T(8,128)(2,1)} %q_hbm.1, bf16[1,1,512,128]{3,2,1,0:T(8,128)(2,1)} %k_hbm.1, bf16[1,1,512,128]{3,2,1,0:T(8,128)(2,1)} %v_hbm.1, bf16[1,64,128]{2,1,0:T(8,128)(2,1)} %kn_hbm.1, ...), custom_call_target="tpu_custom_call" | custom-call | flops 400000000 | bytes 3000000 | tf_op jit(solution)/shard_map/attention/pallas_call | solution.py:237
  12.7 0.0 copy-start.6
  12.7 0.0 copy-start.4
  12.7 0.0 copy-start.3
  12.8 0.0 copy-start.5
  12.8 0.0 collective-permute-done.proj_any
  12.8 1.3 project.1
  14.1 4.7 %all-to-all-start = ((bf16[4,16,2048]{2,1,0:T(8,128)(2,1)}), bf16[4,16,2048]{2,1,0:T(8,128)(2,1)S(1)}, u32[]{:S(2)}, u32[]{:S(2)}) async-start(bf16[4,16,2048]{2,1,0:T(8,128)(2,1)} %project.1), calls=%async_computation | async-start | bytes 524288 | tf_op jit(solution)/shard_map/all_to_all | solution.py:149
  18.8 0.0 copy-done.6
  18.8 0.0 copy-done.4
  18.9 0.1 copy.16
  18.9 8.6 %all-to-all-done = bf16[4,16,2048]{2,1,0:T(8,128)(2,1)S(1)} async-done(((bf16[4,16,2048]{2,1,0:T(8,128)(2,1)}), bf16[4,16,2048]{2,1,0:T(8,128)(2,1)S(1)}, u32[]{:S(2)}, u32[]{:S(2)}) %all-to-all-start) | async-done | bytes 262176 | tf_op jit(solution)/shard_map/all_to_all | solution.py:149
  27.5 0.0 copy-done.3
  27.6 0.1 multiply_reduce_fusion
  27.7 0.0 copy-done.5
  27.7 0.1 multiply_convert_fusion
  27.8 1.1 broadcast_in_dim.2
  28.9 10.0 %all-to-all-start.1 = ((bf16[16,16,2176]{2,1,0:T(8,128)(2,1)}), bf16[16,16,2176]{2,1,0:T(8,128)(2,1)S(1)}, u32[]{:S(2)}, u32[]{:S(2)}) async-start(bf16[16,16,2176]{2,1,0:T(8,128)(2,1)} %broadcast_in_dim.2), calls=%async_computation.1 | async-start | bytes 2228224 | tf_op jit(solution)/shard_map/all_to_all | solution.py:149
  38.9 34.7 %all-to-all-done.1 = bf16[16,16,2176]{2,1,0:T(8,128)(2,1)S(1)} async-done(((bf16[16,16,2176]{2,1,0:T(8,128)(2,1)}), bf16[16,16,2176]{2,1,0:T(8,128)(2,1)S(1)}, u32[]{:S(2)}, u32[]{:S(2)}) %all-to-all-start.1) | async-done | bytes 1114144 | tf_op jit(solution)/shard_map/all_to_all | solution.py:149
  73.6 2.2 dispatch.1
  75.8 0.0 copy-start
  75.8 0.0 copy-start.1
  75.8 0.0 copy-start.2
  75.8 58.0 %all_to_all.25 = bf16[32,32,2048]{2,1,0:T(8,128)(2,1)S(1)} all-to-all(bf16[32,32,2048]{2,1,0:T(8,128)(2,1)S(1)} %bitcast.36), channel_id=1, replica_groups=mesh['side'=2,'x'=4,'yp'=4,'yq'=2,'zl'=2,'head'=4] {'x','yq','zl','side'}, dimensions={0} | all-to-all | bytes 8388608 | tf_op jit(solution)/shard_map/all_to_all | solution.py:149
  133.8 0.0 copy-done
  133.8 0.0 copy-done.1
  133.8 0.0 copy-done.2
  133.8 4.4 %experts.1 = bf16[1024,2048]{1,0:T(8,128)(2,1)S(1)} custom-call(bf16[1024,2048]{1,0:T(8,128)(2,1)S(1)} %bitcast.34, bf16[192,2048]{1,0:T(8,128)(2,1)S(1)} %bitcast.39, bf16[192,2048]{1,0:T(8,128)(2,1)S(1)} %bitcast.40, bf16[192,2048]{1,0:T(8,128)(2,1)S(1)} %bitcast.41), custom_call_target="tpu_custom_call" | custom-call | flops 2500000000 | bytes 11000000 | tf_op jit(solution)/shard_map/experts/pallas_call | solution.py:303
  138.2 54.6 %all_to_all.26 = bf16[32,32,2048]{2,1,0:T(8,128)(2,1)S(1)} all-to-all(bf16[32,32,2048]{2,1,0:T(8,128)(2,1)S(1)} %bitcast.35), channel_id=1, replica_groups=mesh['side'=2,'x'=4,'yp'=4,'yq'=2,'zl'=2,'head'=4] {'x','yq','zl','side'}, dimensions={0} | all-to-all | bytes 8388608 | tf_op jit(solution)/shard_map/all_to_all | solution.py:149
  192.9 1.8 combine.1
  194.6 37.8 %all_to_all.27 = bf16[16,16,2048]{2,1,0:T(8,128)(2,1)S(1)} all-to-all(bf16[16,16,2048]{2,1,0:T(8,128)(2,1)S(1)} %bitcast.37), channel_id=1, replica_groups=mesh['side'=2,'x'=4,'yp'=4,'yq'=2,'zl'=2,'head'=4] {'head','yp'}, dimensions={0} | all-to-all | bytes 2097152 | tf_op jit(solution)/shard_map/all_to_all | solution.py:149
  232.5 0.1 convert_reduce_fusion
  232.6 0.6 fusion.2
  (7 shorter events, 0.1 us)
Async XLA Ops:
  0.0 12.8 %collective-permute-start = (bf16[1024,1024]{1,0:T(8,128)(2,1)}, bf16[1024,1024]{1,0:T(8,128)(2,1)S(1)}, u32[]{:S(2)}, u32[]{:S(2)}) collective-permute-start(bf16[1024,1024]{1,0:T(8,128)(2,1)} %proj_hbm.1), channel_id=1, source_target_pairs={{0,256},{256,0},{1,257},{257,1},{2,258},{258,2},{3,259},{259,3},{4... | collective-permute-start | bytes 6291464 | tf_op jit(solution)/shard_map/ppermute | solution.py:234
  12.7 6.1 %copy-start.6 = (s32[1,16,8]{1,2,0:T(8,128)S(1)}, s32[1,16,8]{1,2,0:T(8,128)}, u32[]{:S(2)}) copy-start(s32[1,16,8]{1,2,0:T(8,128)} %param.23) | copy-start | bytes 1540
  12.7 6.1 %copy-start.4 = (f32[1,16,8]{1,2,0:T(8,128)S(1)}, f32[1,16,8]{1,2,0:T(8,128)}, u32[]{:S(2)}) copy-start(f32[1,16,8]{1,2,0:T(8,128)} %param.24) | copy-start | bytes 1540
  12.7 14.8 %copy-start.3 = (bf16[1,16,2048]{2,1,0:T(8,128)(2,1)S(1)}, bf16[1,16,2048]{2,1,0:T(8,128)(2,1)}, u32[]{:S(2)}) copy-start(bf16[1,16,2048]{2,1,0:T(8,128)(2,1)} %param.20) | copy-start | bytes 196612
  12.8 14.9 %copy-start.5 = (f32[2048]{0:T(1024)S(1)}, f32[2048]{0:T(1024)}, u32[]{:S(2)}) copy-start(f32[2048]{0:T(1024)} %param.22) | copy-start | bytes 24580
  14.1 13.4 %all-to-all-start = ((bf16[4,16,2048]{2,1,0:T(8,128)(2,1)}), bf16[4,16,2048]{2,1,0:T(8,128)(2,1)S(1)}, u32[]{:S(2)}, u32[]{:S(2)}) async-start(bf16[4,16,2048]{2,1,0:T(8,128)(2,1)} %project.1), calls=%async_computation | async-start | bytes 524288 | tf_op jit(solution)/shard_map/all_to_all | solution.py:149
  28.9 44.7 %all-to-all-start.1 = ((bf16[16,16,2176]{2,1,0:T(8,128)(2,1)}), bf16[16,16,2176]{2,1,0:T(8,128)(2,1)S(1)}, u32[]{:S(2)}, u32[]{:S(2)}) async-start(bf16[16,16,2176]{2,1,0:T(8,128)(2,1)} %broadcast_in_dim.2), calls=%async_computation.1 | async-start | bytes 2228224 | tf_op jit(solution)/shard_map/all_to_all | solution.py:149
  75.8 58.0 %copy-start = (bf16[1,2048,192]{1,2,0:T(8,128)(2,1)S(1)}, bf16[1,2048,192]{1,2,0:T(8,128)(2,1)}, u32[]{:S(2)}) copy-start(bf16[1,2048,192]{1,2,0:T(8,128)(2,1)} %param.25) | copy-start | bytes 2359300
  75.8 58.0 %copy-start.1 = (bf16[1,2048,192]{1,2,0:T(8,128)(2,1)S(1)}, bf16[1,2048,192]{1,2,0:T(8,128)(2,1)}, u32[]{:S(2)}) copy-start(bf16[1,2048,192]{1,2,0:T(8,128)(2,1)} %param.26) | copy-start | bytes 2359300
  75.8 58.0 %copy-start.2 = (bf16[1,192,2048]{2,1,0:T(8,128)(2,1)S(1)}, bf16[1,192,2048]{2,1,0:T(8,128)(2,1)}, u32[]{:S(2)}) copy-start(bf16[1,192,2048]{2,1,0:T(8,128)(2,1)} %param.27) | copy-start | bytes 2359300

commit v6 on v5

--- a/solution.py
+++ b/solution.py
@@ -149,6 +149,24 @@
     return lax.all_to_all(value, axes, split_axis=0, concat_axis=0, tiled=True)
 
 
+def norm_kernel(pieces_ref, hidden_ref, gain_ref, routing_ref, resid_ref, out_ref, row_ref, sems):
+    width = hidden_ref.shape[2]
+    resid = hidden_ref[0].astype(jnp.float32)
+    resid = resid + jnp.sum(pieces_ref[...].astype(jnp.float32), axis=0)
+    resid_ref[...] = resid
+    mean = jnp.mean(resid * resid, axis=1, keepdims=True)
+    row_ref[:, :width] = (resid * lax.rsqrt(mean + 1e-06) * gain_ref[...]).astype(jnp.bfloat16)
+    row_ref[:, width:] = routing_ref[...]
+    copies = [
+        pltpu.make_async_copy(row_ref, out_ref.at[peer], sems.at[peer])
+        for peer in range(out_ref.shape[0])
+    ]
+    for copy in copies:
+        copy.start()
+    for copy in copies:
+        copy.wait()
+
+
 def dispatch_kernel(part_ref, gathered_ref, out_ref, combine_ref, dispatch_ref):
     top_k, block = 8, 16
     rows, width = gathered_ref.shape[0], gathered_ref.shape[1] - 128
@@ -272,17 +290,27 @@
         name="project",
     )(side.reshape(1), context, partner_proj, own)
     pieces = a2a(full_rows, "head")
-    resid = hidden_in[0].astype(jnp.float32) + jnp.sum(pieces.astype(jnp.float32), axis=0)
-    normed = (
-        resid * lax.rsqrt(jnp.mean(resid * resid, axis=-1, keepdims=True) + 1e-06) * norm_gain
-    ).astype(jnp.bfloat16)
-
     raw_wts = gate_wts[0]
     mixing = (raw_wts / jnp.sum(raw_wts, axis=-1, keepdims=True)).astype(jnp.bfloat16)
     routing = jnp.concatenate([expert_ids[0].astype(jnp.bfloat16), mixing], axis=1)
     routing = jnp.pad(routing, ((0, 0), (0, 128 - routing.shape[1])))
-    payload = jnp.concatenate([normed, routing], axis=1)
-    gathered = a2a(jnp.broadcast_to(payload[None], (near,) + payload.shape), NEAR)
+    resid, payload = pl.pallas_call(
+        norm_kernel,
+        in_specs=[in_vmem()] * 4,
+        out_specs=[in_vmem(), pl.BlockSpec(memory_space=pltpu.HBM)],
+        out_shape=[
+            jax.ShapeDtypeStruct((block, width), jnp.float32),
+            jax.ShapeDtypeStruct((near, block, width + 128), jnp.bfloat16),
+        ],
+        scratch_shapes=[
+            pltpu.VMEM((block, width + 128), jnp.bfloat16),
+            pltpu.SemaphoreType.DMA((near,)),
+        ],
+        cost_estimate=pl.CostEstimate(flops=500_000, bytes_accessed=1_500_000, transcendentals=0),
+        compiler_params=pltpu.CompilerParams(vmem_limit_bytes=8 << 20),
+        name="norm",
+    )(pieces, hidden_in, norm_gain.reshape(1, width), routing)
+    gathered = a2a(payload, NEAR)
     outgoing, combine = pl.pallas_call(
         dispatch_kernel,
         in_specs=[in_smem(), in_vmem()],

time: 234 us -> 234 us (level)
  no operation moved by 1% of the time
where the time goes in v6:
time: 234 us; the launch traced here: 233 us
  blocking collectives  150 us (64%)
  waiting for transfers between devices  43.1 us (18%)
  starting transfers between devices  23.4 us (10%)
  Pallas kernels  14.4 us (6%)
    all_to_all x3, blocking collectives, a2a(): return lax.all_to_all(value, axes, split_axis=0, concat_axis=0, tiled=True)  150 us
    all_to_all x2, waiting for transfers between devices, a2a(): return lax.all_to_all(value, axes, split_axis=0, concat_axis=0, tiled=True)  43.1 us
    all_to_all x2, starting transfers between devices, a2a(): return lax.all_to_all(value, axes, split_axis=0, concat_axis=0, tiled=True)  14.7 us
    ppermute x1, starting transfers between devices, shards(): partner_proj = lax.ppermute(out_proj, 'side', [(0, 1), (1, 0)])  8.73 us
  transfers between devices with their start and end apart: 3, of which 2 were waited for; matrix products, arithmetic and copies ran while one was open for 0% of the time, Pallas kernels for 1%

profile of v6, /device:TPU:1, one launch (start us, length us, event | category | flops | bytes accessed | tf_op | source)
XLA Modules:
  0.0 233.2 jit_solution(10595003026608031124)
XLA Ops:
  0.0 8.7 %collective-permute-start = (bf16[1024,1024]{1,0:T(8,128)(2,1)}, bf16[1024,1024]{1,0:T(8,128)(2,1)S(1)}, u32[]{:S(2)}, u32[]{:S(2)}) collective-permute-start(bf16[1024,1024]{1,0:T(8,128)(2,1)} %proj_hbm.1), channel_id=1, source_target_pairs={{0,256},{256,0},{1,257},{257,1},{2,258},{258,2},{3,259},{259,3},{4... | collective-permute-start | bytes 6291464 | tf_op jit(solution)/shard_map/ppermute | solution.py:252
  9.4 3.3 %attention.1 = (bf16[64,1024]{1,0:T(8,128)(2,1)S(1)}, bf16[64,1024]{1,0:T(8,128)(2,1)S(1)}) custom-call(s32[1]{0:T(128)S(6)} %copy.20.len_ref, bf16[1,64,1024]{2,1,0:T(8,128)(2,1)} %q_hbm.1, bf16[1,1,512,128]{3,2,1,0:T(8,128)(2,1)} %k_hbm.1, bf16[1,1,512,128]{3,2,1,0:T(8,128)(2,1)} %v_hbm.1, bf16[1,64,128]{2,1,0:T(8,128)(2,1)} %kn_hbm.1, ...), custom_call_target="tpu_custom_call" | custom-call | flops 400000000 | bytes 3000000 | tf_op jit(solution)/shard_map/attention/pallas_call | solution.py:255
  12.7 0.0 copy-start.6
  12.7 0.0 copy-start.5
  12.7 0.0 copy-start.3
  12.8 0.0 copy-start.4
  12.8 0.0 collective-permute-done.proj_any
  12.8 1.3 project.1
  14.1 4.7 %all-to-all-start = ((bf16[4,16,2048]{2,1,0:T(8,128)(2,1)}), bf16[4,16,2048]{2,1,0:T(8,128)(2,1)S(1)}, u32[]{:S(2)}, u32[]{:S(2)}) async-start(bf16[4,16,2048]{2,1,0:T(8,128)(2,1)} %project.1), calls=%async_computation | async-start | bytes 524288 | tf_op jit(solution)/shard_map/all_to_all | solution.py:149
  18.8 0.0 copy-done.6
  18.8 0.1 copy.19
  18.9 0.0 copy-done.5
  18.9 0.1 copy.17
  19.0 0.1 divide_convert_fusion
  19.1 0.1 fusion.3.routing_ref
  19.2 8.4 %all-to-all-done.pieces_ref = bf16[4,16,2048]{2,1,0:T(8,128)(2,1)S(1)} async-done(((bf16[4,16,2048]{2,1,0:T(8,128)(2,1)}), bf16[4,16,2048]{2,1,0:T(8,128)(2,1)S(1)}, u32[]{:S(2)}, u32[]{:S(2)}) %all-to-all-start) | async-done | bytes 262176 | tf_op jit(solution)/shard_map/all_to_all | solution.py:149
  27.5 0.0 copy-done.3
  27.5 0.0 copy-done.4
  27.5 1.3 norm.1
  28.8 10.0 %all-to-all-start.1 = ((bf16[16,16,2176]{2,1,0:T(8,128)(2,1)}), bf16[16,16,2176]{2,1,0:T(8,128)(2,1)S(1)}, u32[]{:S(2)}, u32[]{:S(2)}) async-start(bf16[16,16,2176]{2,1,0:T(8,128)(2,1)} %get-tuple-element.14), calls=%async_computation.1 | async-start | bytes 2228224 | tf_op jit(solution)/shard_map/all_to_all | solution.py:149
  38.8 34.7 %all-to-all-done.1 = bf16[16,16,2176]{2,1,0:T(8,128)(2,1)S(1)} async-done(((bf16[16,16,2176]{2,1,0:T(8,128)(2,1)}), bf16[16,16,2176]{2,1,0:T(8,128)(2,1)S(1)}, u32[]{:S(2)}, u32[]{:S(2)}) %all-to-all-start.1) | async-done | bytes 1114144 | tf_op jit(solution)/shard_map/all_to_all | solution.py:149
  73.5 2.2 dispatch.1
  75.8 0.0 copy-start
  75.8 0.0 copy-start.1
  75.8 0.0 copy-start.2
  75.8 58.0 %all_to_all.25 = bf16[32,32,2048]{2,1,0:T(8,128)(2,1)S(1)} all-to-all(bf16[32,32,2048]{2,1,0:T(8,128)(2,1)S(1)} %bitcast.24), channel_id=1, replica_groups=mesh['side'=2,'x'=4,'yp'=4,'yq'=2,'zl'=2,'head'=4] {'x','yq','zl','side'}, dimensions={0} | all-to-all | bytes 8388608 | tf_op jit(solution)/shard_map/all_to_all | solution.py:149
  133.8 0.0 copy-done
  133.8 0.0 copy-done.1
  133.8 0.0 copy-done.2
  133.8 4.4 %experts.1 = bf16[1024,2048]{1,0:T(8,128)(2,1)S(1)} custom-call(bf16[1024,2048]{1,0:T(8,128)(2,1)S(1)} %bitcast.22, bf16[192,2048]{1,0:T(8,128)(2,1)S(1)} %bitcast.27, bf16[192,2048]{1,0:T(8,128)(2,1)S(1)} %bitcast.28, bf16[192,2048]{1,0:T(8,128)(2,1)S(1)} %bitcast.29), custom_call_target="tpu_custom_call" | custom-call | flops 2500000000 | bytes 11000000 | tf_op jit(solution)/shard_map/experts/pallas_call | solution.py:331
  138.2 54.6 %all_to_all.26 = bf16[32,32,2048]{2,1,0:T(8,128)(2,1)S(1)} all-to-all(bf16[32,32,2048]{2,1,0:T(8,128)(2,1)S(1)} %bitcast.23), channel_id=1, replica_groups=mesh['side'=2,'x'=4,'yp'=4,'yq'=2,'zl'=2,'head'=4] {'x','yq','zl','side'}, dimensions={0} | all-to-all | bytes 8388608 | tf_op jit(solution)/shard_map/all_to_all | solution.py:149
  192.8 1.8 combine.1
  194.6 37.8 %all_to_all.27 = bf16[16,16,2048]{2,1,0:T(8,128)(2,1)S(1)} all-to-all(bf16[16,16,2048]{2,1,0:T(8,128)(2,1)S(1)} %bitcast.25), channel_id=1, replica_groups=mesh['side'=2,'x'=4,'yp'=4,'yq'=2,'zl'=2,'head'=4] {'head','yp'}, dimensions={0} | all-to-all | bytes 2097152 | tf_op jit(solution)/shard_map/all_to_all | solution.py:149
  232.4 0.1 convert_reduce_fusion
  232.6 0.6 fusion
  (2 shorter events, 0.0 us)
Async XLA Ops:
  0.0 12.8 %collective-permute-start = (bf16[1024,1024]{1,0:T(8,128)(2,1)}, bf16[1024,1024]{1,0:T(8,128)(2,1)S(1)}, u32[]{:S(2)}, u32[]{:S(2)}) collective-permute-start(bf16[1024,1024]{1,0:T(8,128)(2,1)} %proj_hbm.1), channel_id=1, source_target_pairs={{0,256},{256,0},{1,257},{257,1},{2,258},{258,2},{3,259},{259,3},{4... | collective-permute-start | bytes 6291464 | tf_op jit(solution)/shard_map/ppermute | solution.py:252
  12.7 6.1 %copy-start.6 = (s32[1,16,8]{1,2,0:T(8,128)S(1)}, s32[1,16,8]{1,2,0:T(8,128)}, u32[]{:S(2)}) copy-start(s32[1,16,8]{1,2,0:T(8,128)} %param.23) | copy-start | bytes 1540
  12.7 6.2 %copy-start.5 = (f32[1,16,8]{1,2,0:T(8,128)S(1)}, f32[1,16,8]{1,2,0:T(8,128)}, u32[]{:S(2)}) copy-start(f32[1,16,8]{1,2,0:T(8,128)} %param.24) | copy-start | bytes 1540
  12.7 14.8 %copy-start.3 = (bf16[1,16,2048]{2,1,0:T(8,128)(2,1)S(1)}, bf16[1,16,2048]{2,1,0:T(8,128)(2,1)}, u32[]{:S(2)}) copy-start(bf16[1,16,2048]{2,1,0:T(8,128)(2,1)} %hidden_ref.1) | copy-start | bytes 196612
  12.8 14.8 %copy-start.4 = (f32[2048]{0:T(1024)S(1)}, f32[2048]{0:T(1024)}, u32[]{:S(2)}) copy-start(f32[2048]{0:T(1024)} %param.22) | copy-start | bytes 24580
  14.1 13.4 %all-to-all-start = ((bf16[4,16,2048]{2,1,0:T(8,128)(2,1)}), bf16[4,16,2048]{2,1,0:T(8,128)(2,1)S(1)}, u32[]{:S(2)}, u32[]{:S(2)}) async-start(bf16[4,16,2048]{2,1,0:T(8,128)(2,1)} %project.1), calls=%async_computation | async-start | bytes 524288 | tf_op jit(solution)/shard_map/all_to_all | solution.py:149
  28.8 44.7 %all-to-all-start.1 = ((bf16[16,16,2176]{2,1,0:T(8,128)(2,1)}), bf16[16,16,2176]{2,1,0:T(8,128)(2,1)S(1)}, u32[]{:S(2)}, u32[]{:S(2)}) async-start(bf16[16,16,2176]{2,1,0:T(8,128)(2,1)} %get-tuple-element.14), calls=%async_computation.1 | async-start | bytes 2228224 | tf_op jit(solution)/shard_map/all_to_all | solution.py:149
  75.8 58.0 %copy-start = (bf16[1,2048,192]{1,2,0:T(8,128)(2,1)S(1)}, bf16[1,2048,192]{1,2,0:T(8,128)(2,1)}, u32[]{:S(2)}) copy-start(bf16[1,2048,192]{1,2,0:T(8,128)(2,1)} %param.25) | copy-start | bytes 2359300
  75.8 58.0 %copy-start.1 = (bf16[1,2048,192]{1,2,0:T(8,128)(2,1)S(1)}, bf16[1,2048,192]{1,2,0:T(8,128)(2,1)}, u32[]{:S(2)}) copy-start(bf16[1,2048,192]{1,2,0:T(8,128)(2,1)} %param.26) | copy-start | bytes 2359300
  75.8 58.0 %copy-start.2 = (bf16[1,192,2048]{2,1,0:T(8,128)(2,1)S(1)}, bf16[1,192,2048]{2,1,0:T(8,128)(2,1)}, u32[]{:S(2)}) copy-start(bf16[1,192,2048]{2,1,0:T(8,128)(2,1)} %param.27) | copy-start | bytes 2359300

commit v7 on v6

--- a/solution.py
+++ b/solution.py
@@ -1,3 +1,4 @@
+import functools
 import math
 
 import jax
@@ -106,35 +107,65 @@
         out_ref[part, :, other] = partner[take]
 
 
-def expert_kernel(rows_ref, gate_ref, up_ref, down_ref, out_ref):
-    tile = 256
+def fetch_tiles(source_hbm, target_ref, sems, tiles):
+    tile = source_hbm.shape[0] // tiles
+    loads = [
+        pltpu.make_async_copy(
+            source_hbm.at[pl.ds(index * tile, tile)],
+            target_ref.at[pl.ds(index * tile, tile)],
+            sems.at[index],
+        )
+        for index in range(tiles)
+    ]
+    for load in loads:
+        load.start()
+    return loads
+
+
+def expert_kernel(
+    rows_hbm, gate_ref, up_ref, down_hbm, out_hbm, rows_ref, down_ref, in_sems, stage_ref, sems
+):
     contract = (((1,), (1,)), ((), ()))
-
-    def step(index, carry):
-        take = pl.ds(pl.multiple_of(index * tile, tile), tile)
-        rows = rows_ref[take, :]
+    tiles = rows_hbm.shape[0] // stage_ref.shape[1]
+    loads = fetch_tiles(rows_hbm, rows_ref, in_sems, tiles)
+    down_load = pltpu.make_async_copy(down_hbm, down_ref, in_sems.at[tiles])
+    down_load.start()
+
+    def make(start, tile):
+        loads[start // tile].wait()
+        rows = rows_ref[start : start + tile]
         gate = lax.dot_general(rows, gate_ref[...], contract, preferred_element_type=jnp.float32)
         up = lax.dot_general(rows, up_ref[...], contract, preferred_element_type=jnp.float32)
         hidden = (gate / (1.0 + jnp.exp(-gate)) * up).astype(jnp.bfloat16)
-        out_ref[take, :] = jnp.dot(
-            hidden, down_ref[...], preferred_element_type=jnp.float32
-        ).astype(jnp.bfloat16)
-        return carry
-
-    lax.fori_loop(0, rows_ref.shape[0] // tile, step, 0)
-
-
-def combine_kernel(combine_ref, rows_ref, out_ref):
-    tile = 512
-
-    def step(index, carry):
-        take = pl.ds(pl.multiple_of(index * tile, tile), tile)
-        out_ref[:, take] = jnp.dot(
-            combine_ref[...], rows_ref[:, take], preferred_element_type=jnp.float32
-        ).astype(jnp.bfloat16)
-        return carry
-
-    lax.fori_loop(0, rows_ref.shape[1] // tile, step, 0)
+        if start == 0:
+            down_load.wait()
+        return jnp.dot(hidden, down_ref[...], preferred_element_type=jnp.float32).astype(
+            jnp.bfloat16
+        )
+
+    send_tiles(make, out_hbm, stage_ref, sems)
+
+
+def combine_kernel(first_ref, second_ref, rows_hbm, out_ref, rows_ref, total_ref, sems):
+    half = first_ref.shape[1]
+    tiles = sems.shape[0]
+    tile = rows_hbm.shape[0] // tiles
+    loads = fetch_tiles(rows_hbm, rows_ref, sems, tiles)
+    for index, load in enumerate(loads):
+        load.wait()
+        start = index * tile
+        table = first_ref if start < half else second_ref
+        product = jnp.dot(
+            table[:, start % half : start % half + tile],
+            rows_ref[start : start + tile],
+            preferred_element_type=jnp.float32,
+        )
+        if index == 0:
+            total_ref[...] = product
+        elif index < tiles - 1:
+            total_ref[...] += product
+        else:
+            out_ref[...] = (total_ref[...] + product).astype(jnp.bfloat16)
 
 
 def in_vmem():
@@ -167,10 +198,9 @@
         copy.wait()
 
 
-def dispatch_kernel(part_ref, gathered_ref, out_ref, combine_ref, dispatch_ref):
+def routed(part_ref, gathered_ref):
     top_k, block = 8, 16
     rows, width = gathered_ref.shape[0], gathered_ref.shape[1] - 128
-    blocks = rows // block
     columns = jnp.transpose(gathered_ref[:, width:].astype(jnp.float32))
     chosen = columns[:top_k]
     mixing = columns[top_k : 2 * top_k]
@@ -196,33 +226,66 @@
         jnp.where(earlier, 1.0, 0.0).astype(jnp.bfloat16),
         preferred_element_type=jnp.float32,
     )
+    blocks = rows // block
     own = lax.broadcasted_iota(jnp.int32, (blocks, rows), 0) == (
         lax.broadcasted_iota(jnp.int32, (blocks, rows), 1) // block
     )
+    return named, rank, weight, own
+
+
+def send_tiles(make, out_hbm, stage_ref, sems):
+    slots, tile = stage_ref.shape[0], stage_ref.shape[1]
+    copies = []
+    for index in range(out_hbm.shape[0] // tile):
+        slot = index % slots
+        if index >= slots:
+            copies[index - slots].wait()
+        stage_ref[slot] = make(index * tile, tile)
+        copy = pltpu.make_async_copy(
+            stage_ref.at[slot], out_hbm.at[pl.ds(index * tile, tile)], sems.at[slot]
+        )
+        copy.start()
+        copies.append(copy)
+    for copy in copies[-slots:]:
+        copy.wait()
+
+
+def dispatch_kernel(part_ref, gathered_ref, out_hbm, dispatch_ref, stage_ref, sems):
+    width = gathered_ref.shape[1] - 128
+    named, rank, _, own = routed(part_ref, gathered_ref)
+    blocks = own.shape[0]
+    for e in range(named.shape[0]):
+        for s in range(2):
+            takes = (named[e : e + 1] > 0.5) & (jnp.abs(rank[e : e + 1] - s) < 0.5)
+            at = (2 * e + s) * blocks
+            dispatch_ref[at : at + blocks] = jnp.where(
+                own, jnp.where(takes, 1.0, 0.0), 0.0
+            ).astype(jnp.bfloat16)
+
+    def make(start, tile):
+        return jnp.dot(
+            dispatch_ref[start : start + tile],
+            gathered_ref[:, :width],
+            preferred_element_type=jnp.float32,
+        ).astype(jnp.bfloat16)
+
+    send_tiles(make, out_hbm, stage_ref, sems)
+
+
+def weight_kernel(begin, part_ref, gathered_ref, combine_ref):
+    named, rank, weight, own = routed(part_ref, gathered_ref)
+    blocks = own.shape[0]
     group = 128 // (2 * blocks)
-    for start in range(0, local, group):
+    for start in range(0, named.shape[0] // 2, group):
         tiles = []
-        for e in range(start, start + group):
+        for e in range(begin + start, begin + start + group):
             for s in range(2):
                 takes = (named[e : e + 1] > 0.5) & (jnp.abs(rank[e : e + 1] - s) < 0.5)
-                at = (2 * e + s) * blocks
-                dispatch_ref[at : at + blocks] = jnp.where(
-                    own, jnp.where(takes, 1.0, 0.0), 0.0
-                ).astype(jnp.bfloat16)
                 tiles.append(jnp.where(own, jnp.where(takes, weight[e : e + 1], 0.0), 0.0))
         at = 2 * start * blocks
-        turned = jnp.transpose(jnp.concatenate(tiles, axis=0)).astype(jnp.bfloat16)
-        combine_ref[:, at : at + 128] = turned
-    tile = 256
-
-    def step(index, carry):
-        take = pl.ds(pl.multiple_of(index * tile, tile), tile)
-        out_ref[take, :] = jnp.dot(
-            dispatch_ref[take, :], gathered_ref[:, :width], preferred_element_type=jnp.float32
-        ).astype(jnp.bfloat16)
-        return carry
-
-    lax.fori_loop(0, out_ref.shape[0] // tile, step, 0)
+        combine_ref[:, at : at + 128] = jnp.transpose(jnp.concatenate(tiles, axis=0)).astype(
+            jnp.bfloat16
+        )
 
 
 def shards(
@@ -311,46 +374,84 @@
         name="norm",
     )(pieces, hidden_in, norm_gain.reshape(1, width), routing)
     gathered = a2a(payload, NEAR)
-    outgoing, combine = pl.pallas_call(
+    gathered = gathered.reshape(near * block, width + 128)
+    part = lax.axis_index("yp").reshape(1)
+    tile = 256
+    staging = [pltpu.VMEM((2, tile, width), jnp.bfloat16), pltpu.SemaphoreType.DMA((2,))]
+    slot_rows = pltpu.HBM((far * slots, width), jnp.bfloat16)
+    outgoing = pl.pallas_call(
         dispatch_kernel,
         in_specs=[in_smem(), in_vmem()],
-        out_specs=[in_vmem()] * 2,
-        out_shape=[
-            jax.ShapeDtypeStruct((far * slots, width), jnp.bfloat16),
-            jax.ShapeDtypeStruct((near * block, far * slots), jnp.bfloat16),
-        ],
+        out_specs=pl.BlockSpec(memory_space=pltpu.HBM),
+        out_shape=slot_rows,
         cost_estimate=pl.CostEstimate(
             flops=1_200_000_000, bytes_accessed=6_000_000, transcendentals=0
         ),
-        scratch_shapes=[pltpu.VMEM((far * slots, near * block), jnp.bfloat16)],
+        scratch_shapes=[pltpu.VMEM((far * slots, near * block), jnp.bfloat16)] + staging,
         compiler_params=pltpu.CompilerParams(vmem_limit_bytes=20 << 20),
         name="dispatch",
-    )(lax.axis_index("yp").reshape(1), gathered.reshape(near * block, width + 128))
-
+    )(part, gathered)
+
+    def weights_of(begin, rows):
+        return pl.pallas_call(
+            functools.partial(weight_kernel, begin),
+            in_specs=[in_smem(), in_vmem()],
+            out_specs=in_vmem(),
+            out_shape=jax.ShapeDtypeStruct((near * block, far * slots // 2), jnp.bfloat16),
+            cost_estimate=pl.CostEstimate(
+                flops=200_000_000, bytes_accessed=1_200_000, transcendentals=0
+            ),
+            compiler_params=pltpu.CompilerParams(vmem_limit_bytes=12 << 20),
+            name="weights",
+        )(part, rows)
+
+    outgoing, gathered = lax.optimization_barrier((outgoing, gathered))
+    first_weights = weights_of(0, gathered)
     flat_rows = a2a(outgoing.reshape(far, slots, width), FAR).reshape(far * slots, width)
+    flat_rows, first_weights = lax.optimization_barrier((flat_rows, first_weights))
     partial_value = pl.pallas_call(
         expert_kernel,
-        in_specs=[in_vmem()] * 4,
-        out_specs=in_vmem(),
-        out_shape=jax.ShapeDtypeStruct((far * slots, width), jnp.bfloat16),
+        in_specs=[pl.BlockSpec(memory_space=pl.ANY)]
+        + [in_vmem()] * 2
+        + [pl.BlockSpec(memory_space=pltpu.HBM)],
+        out_specs=pl.BlockSpec(memory_space=pltpu.HBM),
+        out_shape=slot_rows,
+        scratch_shapes=[
+            pltpu.VMEM((far * slots, width), jnp.bfloat16),
+            pltpu.VMEM(w_down.shape[1:], jnp.bfloat16),
+            pltpu.SemaphoreType.DMA((far * slots // tile + 1,)),
+        ]
+        + staging,
         cost_estimate=pl.CostEstimate(
             flops=2_500_000_000, bytes_accessed=11_000_000, transcendentals=200_000
         ),
         compiler_params=pltpu.CompilerParams(vmem_limit_bytes=24 << 20),
         name="experts",
-    )(flat_rows, w_gate[0].T, w_up[0].T, w_down[0])
+    )(
+        flat_rows,
+        w_gate[0].T,
+        w_up[0].T,
+        pltpu.with_memory_space_constraint(w_down[0], pltpu.HBM),
+    )
+    partial_value, gathered = lax.optimization_barrier((partial_value, gathered))
+    second_weights = weights_of(far // 2, gathered)
     returned = a2a(partial_value.reshape(far, slots, width), FAR).reshape(far * slots, width)
     weighted = pl.pallas_call(
         combine_kernel,
-        in_specs=[in_vmem()] * 2,
+        in_specs=[in_vmem()] * 2 + [pl.BlockSpec(memory_space=pl.ANY)],
         out_specs=in_vmem(),
+        scratch_shapes=[
+            pltpu.VMEM((far * slots, width), jnp.bfloat16),
+            pltpu.VMEM((near * block, width), jnp.float32),
+            pltpu.SemaphoreType.DMA((far * slots // tile,)),
+        ],
         out_shape=jax.ShapeDtypeStruct((near * block, width), jnp.bfloat16),
         cost_estimate=pl.CostEstimate(
             flops=1_100_000_000, bytes_accessed=6_000_000, transcendentals=0
         ),
         compiler_params=pltpu.CompilerParams(vmem_limit_bytes=16 << 20),
         name="combine",
-    )(combine, returned)
+    )(first_weights, second_weights, returned)
     parts = a2a(weighted.reshape(near, block, width), NEAR)
     moe_out = jnp.sum(parts.astype(jnp.float32), axis=0)
     return (resid + moe_out).astype(jnp.bfloat16)[None]

time: 234 us -> 241 us (1.030)
  the two profiles are of different devices: /device:TPU:1 before, /device:TPU:8 now
where the time goes in v7:
time: 241 us; the launch traced here: 240 us
  waiting for transfers between devices  142 us (59%)
  blocking collectives  39.4 us (16%)
  starting transfers between devices  36.3 us (15%)
  Pallas kernels  20.1 us (8%)
    all_to_all x4, waiting for transfers between devices, a2a(): return lax.all_to_all(value, axes, split_axis=0, concat_axis=0, tiled=True)  142 us
    all_to_all x1, blocking collectives, a2a(): return lax.all_to_all(value, axes, split_axis=0, concat_axis=0, tiled=True)  39.4 us
    all_to_all x4, starting transfers between devices, a2a(): return lax.all_to_all(value, axes, split_axis=0, concat_axis=0, tiled=True)  34.4 us
    pallas_call x1, Pallas kernels, shards(): pl.pallas_call(expert_kernel, in_specs=[pl.BlockSpec(memory_space=pl.ANY)...  7.2 us
  transfers between devices with their start and end apart: 5, of which 5 were waited for; matrix products, arithmetic and copies ran while one was open for 0% of the time, Pallas kernels for 2%

profile of v7, /device:TPU:8, one launch (start us, length us, event | category | flops | bytes accessed | tf_op | source)
XLA Modules:
  0.0 240.2 jit_solution(11589862310835242001)
XLA Ops:
  0.0 1.9 collective-permute-start
  2.6 3.3 %attention.1 = (bf16[64,1024]{1,0:T(8,128)(2,1)S(1)}, bf16[64,1024]{1,0:T(8,128)(2,1)S(1)}) custom-call(s32[1]{0:T(128)S(6)} %copy.20.len_ref, bf16[1,64,1024]{2,1,0:T(8,128)(2,1)} %q_hbm.1, bf16[1,1,512,128]{3,2,1,0:T(8,128)(2,1)} %k_hbm.1, bf16[1,1,512,128]{3,2,1,0:T(8,128)(2,1)} %v_hbm.1, bf16[1,64,128]{2,1,0:T(8,128)(2,1)} %kn_hbm.1, ...), custom_call_target="tpu_custom_call" | custom-call | flops 400000000 | bytes 3000000 | tf_op jit(solution)/shard_map/attention/pallas_call | solution.py:318
  5.9 0.0 copy-start.5
  5.9 0.0 copy-start.4
  5.9 0.0 copy-start.2
  5.9 0.0 copy-start.3
  5.9 0.3 collective-permute-done.proj_any
  6.3 1.3 project.1
  7.6 10.3 %all-to-all-start = ((bf16[4,16,2048]{2,1,0:T(8,128)(2,1)}), bf16[4,16,2048]{2,1,0:T(8,128)(2,1)S(1)}, u32[]{:S(2)}, u32[]{:S(2)}) async-start(bf16[4,16,2048]{2,1,0:T(8,128)(2,1)} %project.1), calls=%async_computation | async-start | bytes 524288 | tf_op jit(solution)/shard_map/all_to_all | solution.py:180
  17.9 0.0 copy-done.5
  17.9 0.1 copy.19
  18.0 0.0 copy-done.4
  18.0 0.1 copy.17
  18.1 0.1 divide_convert_fusion
  18.2 0.1 fusion.3.routing_ref
  18.3 11.2 %all-to-all-done.pieces_ref = bf16[4,16,2048]{2,1,0:T(8,128)(2,1)S(1)} async-done(((bf16[4,16,2048]{2,1,0:T(8,128)(2,1)}), bf16[4,16,2048]{2,1,0:T(8,128)(2,1)S(1)}, u32[]{:S(2)}, u32[]{:S(2)}) %all-to-all-start) | async-done | bytes 262176 | tf_op jit(solution)/shard_map/all_to_all | solution.py:180
  29.4 0.0 copy-done.2
  29.4 0.0 copy-done.3
  29.4 1.3 norm.1
  30.7 7.2 %all-to-all-start.1 = ((bf16[16,16,2176]{2,1,0:T(8,128)(2,1)}), bf16[16,16,2176]{2,1,0:T(8,128)(2,1)S(1)}, u32[]{:S(2)}, u32[]{:S(2)}) async-start(bf16[16,16,2176]{2,1,0:T(8,128)(2,1)} %get-tuple-element.18), calls=%async_computation.1 | async-start | bytes 2228224 | tf_op jit(solution)/shard_map/all_to_all | solution.py:180
  38.0 31.2 %all-to-all-done.1 = bf16[16,16,2176]{2,1,0:T(8,128)(2,1)S(1)} async-done(((bf16[16,16,2176]{2,1,0:T(8,128)(2,1)}), bf16[16,16,2176]{2,1,0:T(8,128)(2,1)S(1)}, u32[]{:S(2)}, u32[]{:S(2)}) %all-to-all-start.1) | async-done | bytes 1114144 | tf_op jit(solution)/shard_map/all_to_all | solution.py:180
  69.2 3.5 %dispatch.1 = bf16[1024,2048]{1,0:T(8,128)(2,1)} custom-call(s32[1]{0:T(128)} %bitcast.4.part_ref, bf16[256,2176]{1,0:T(8,128)(2,1)S(1)} %bitcast.21), custom_call_target="tpu_custom_call" | custom-call | flops 1200000000 | bytes 6000000 | tf_op jit(solution)/shard_map/dispatch/pallas_call | solution.py:382
  72.7 0.0 copy-start
  72.7 0.0 copy-start.1
  72.8 11.1 %all-to-all-start.2 = ((bf16[32,32,2048]{2,1,0:T(8,128)(2,1)}), bf16[32,32,2048]{2,1,0:T(8,128)(2,1)}, u32[]{:S(2)}, u32[]{:S(2)}) async-start(bf16[32,32,2048]{2,1,0:T(8,128)(2,1)} %bitcast.28), calls=%async_computation.2 | async-start | bytes 8388608 | tf_op jit(solution)/shard_map/all_to_all | solution.py:180
  83.8 0.3 weights.2.first_ref
  84.2 49.6 %all-to-all-done.2 = bf16[32,32,2048]{2,1,0:T(8,128)(2,1)} async-done(((bf16[32,32,2048]{2,1,0:T(8,128)(2,1)}), bf16[32,32,2048]{2,1,0:T(8,128)(2,1)}, u32[]{:S(2)}, u32[]{:S(2)}) %all-to-all-start.2) | async-done | bytes 4194336 | tf_op jit(solution)/shard_map/all_to_all | solution.py:180
  133.8 0.0 copy-done
  133.8 0.0 copy-done.1
  133.8 7.2 %experts.1 = bf16[1024,2048]{1,0:T(8,128)(2,1)} custom-call(bf16[1024,2048]{1,0:T(8,128)(2,1)} %bitcast.7.rows_hbm, bf16[192,2048]{1,0:T(8,128)(2,1)S(1)} %bitcast.25, bf16[192,2048]{1,0:T(8,128)(2,1)S(1)} %bitcast.26, bf16[192,2048]{1,0:T(8,128)(2,1)} %bitcast.30), custom_call_target="tpu_custom_call" | custom-call | flops 2500000000 | bytes 11000000 | tf_op jit(solution)/shard_map/experts/pallas_call | solution.py:412
  141.0 5.8 %all-to-all-start.3 = ((bf16[32,32,2048]{2,1,0:T(8,128)(2,1)}), bf16[32,32,2048]{2,1,0:T(8,128)(2,1)}, u32[]{:S(2)}, u32[]{:S(2)}) async-start(bf16[32,32,2048]{2,1,0:T(8,128)(2,1)} %bitcast.29), calls=%async_computation.3 | async-start | bytes 8388608 | tf_op jit(solution)/shard_map/all_to_all | solution.py:180
  146.8 0.4 weights.3.second_ref
  147.1 50.1 %all-to-all-done.3 = bf16[32,32,2048]{2,1,0:T(8,128)(2,1)} async-done(((bf16[32,32,2048]{2,1,0:T(8,128)(2,1)}), bf16[32,32,2048]{2,1,0:T(8,128)(2,1)}, u32[]{:S(2)}, u32[]{:S(2)}) %all-to-all-start.3) | async-done | bytes 4194336 | tf_op jit(solution)/shard_map/all_to_all | solution.py:180
  197.3 2.7 %combine.1 = bf16[256,2048]{1,0:T(8,128)(2,1)S(1)} custom-call(bf16[256,512]{1,0:T(8,128)(2,1)S(1)} %weights.2.first_ref, bf16[256,512]{1,0:T(8,128)(2,1)S(1)} %weights.3.second_ref, bf16[1024,2048]{1,0:T(8,128)(2,1)} %bitcast.14.rows_hbm), custom_call_target="tpu_custom_call" | custom-call | flops 1100000000 | bytes 6000000 | tf_op jit(solution)/shard_map/combine/pallas_call | solution.py:439
  199.9 39.4 %all_to_all.25 = bf16[16,16,2048]{2,1,0:T(8,128)(2,1)S(1)} all-to-all(bf16[16,16,2048]{2,1,0:T(8,128)(2,1)S(1)} %bitcast.24), channel_id=1, replica_groups=mesh['side'=2,'x'=4,'yp'=4,'yq'=2,'zl'=2,'head'=4] {'head','yp'}, dimensions={0} | all-to-all | bytes 2097152 | tf_op jit(solution)/shard_map/all_to_all | solution.py:180
  239.4 0.1 convert_reduce_fusion
  239.5 0.6 fusion
  (2 shorter events, 0.0 us)
Async XLA Ops:
  0.0 6.3 %collective-permute-start = (bf16[1024,1024]{1,0:T(8,128)(2,1)}, bf16[1024,1024]{1,0:T(8,128)(2,1)S(1)}, u32[]{:S(2)}, u32[]{:S(2)}) collective-permute-start(bf16[1024,1024]{1,0:T(8,128)(2,1)} %proj_hbm.1), channel_id=1, source_target_pairs={{0,256},{256,0},{1,257},{257,1},{2,258},{258,2},{3,259},{259,3},{4... | collective-permute-start | bytes 6291464 | tf_op jit(solution)/shard_map/ppermute | solution.py:315
  5.9 12.0 %copy-start.5 = (s32[1,16,8]{1,2,0:T(8,128)S(1)}, s32[1,16,8]{1,2,0:T(8,128)}, u32[]{:S(2)}) copy-start(s32[1,16,8]{1,2,0:T(8,128)} %param.23) | copy-start | bytes 1540
  5.9 12.1 %copy-start.4 = (f32[1,16,8]{1,2,0:T(8,128)S(1)}, f32[1,16,8]{1,2,0:T(8,128)}, u32[]{:S(2)}) copy-start(f32[1,16,8]{1,2,0:T(8,128)} %param.24) | copy-start | bytes 1540
  5.9 23.5 %copy-start.2 = (bf16[1,16,2048]{2,1,0:T(8,128)(2,1)S(1)}, bf16[1,16,2048]{2,1,0:T(8,128)(2,1)}, u32[]{:S(2)}) copy-start(bf16[1,16,2048]{2,1,0:T(8,128)(2,1)} %hidden_ref.1) | copy-start | bytes 196612
  5.9 23.5 %copy-start.3 = (f32[2048]{0:T(1024)S(1)}, f32[2048]{0:T(1024)}, u32[]{:S(2)}) copy-start(f32[2048]{0:T(1024)} %param.22) | copy-start | bytes 24580
  7.6 21.8 %all-to-all-start = ((bf16[4,16,2048]{2,1,0:T(8,128)(2,1)}), bf16[4,16,2048]{2,1,0:T(8,128)(2,1)S(1)}, u32[]{:S(2)}, u32[]{:S(2)}) async-start(bf16[4,16,2048]{2,1,0:T(8,128)(2,1)} %project.1), calls=%async_computation | async-start | bytes 524288 | tf_op jit(solution)/shard_map/all_to_all | solution.py:180
  30.7 38.5 %all-to-all-start.1 = ((bf16[16,16,2176]{2,1,0:T(8,128)(2,1)}), bf16[16,16,2176]{2,1,0:T(8,128)(2,1)S(1)}, u32[]{:S(2)}, u32[]{:S(2)}) async-start(bf16[16,16,2176]{2,1,0:T(8,128)(2,1)} %get-tuple-element.18), calls=%async_computation.1 | async-start | bytes 2228224 | tf_op jit(solution)/shard_map/all_to_all | solution.py:180
  72.7 61.1 %copy-start = (bf16[1,2048,192]{1,2,0:T(8,128)(2,1)S(1)}, bf16[1,2048,192]{1,2,0:T(8,128)(2,1)}, u32[]{:S(2)}) copy-start(bf16[1,2048,192]{1,2,0:T(8,128)(2,1)} %param.25) | copy-start | bytes 2359300
  72.7 61.1 %copy-start.1 = (bf16[1,2048,192]{1,2,0:T(8,128)(2,1)S(1)}, bf16[1,2048,192]{1,2,0:T(8,128)(2,1)}, u32[]{:S(2)}) copy-start(bf16[1,2048,192]{1,2,0:T(8,128)(2,1)} %param.26) | copy-start | bytes 2359300
  72.8 61.0 %all-to-all-start.2 = ((bf16[32,32,2048]{2,1,0:T(8,128)(2,1)}), bf16[32,32,2048]{2,1,0:T(8,128)(2,1)}, u32[]{:S(2)}, u32[]{:S(2)}) async-start(bf16[32,32,2048]{2,1,0:T(8,128)(2,1)} %bitcast.28), calls=%async_computation.2 | async-start | bytes 8388608 | tf_op jit(solution)/shard_map/all_to_all | solution.py:180
  141.0 56.2 %all-to-all-start.3 = ((bf16[32,32,2048]{2,1,0:T(8,128)(2,1)}), bf16[32,32,2048]{2,1,0:T(8,128)(2,1)}, u32[]{:S(2)}, u32[]{:S(2)}) async-start(bf16[32,32,2048]{2,1,0:T(8,128)(2,1)} %bitcast.29), calls=%async_computation.3 | async-start | bytes 8388608 | tf_op jit(solution)/shard_map/all_to_all | solution.py:180

commit v8 on v7

--- a/solution.py
+++ b/solution.py
@@ -1,4 +1,3 @@
-import functools
 import math
 
 import jax
@@ -122,23 +121,14 @@
     return loads
 
 
-def expert_kernel(
-    rows_hbm, gate_ref, up_ref, down_hbm, out_hbm, rows_ref, down_ref, in_sems, stage_ref, sems
-):
+def expert_kernel(rows_ref, gate_ref, up_ref, down_ref, out_hbm, stage_ref, sems):
     contract = (((1,), (1,)), ((), ()))
-    tiles = rows_hbm.shape[0] // stage_ref.shape[1]
-    loads = fetch_tiles(rows_hbm, rows_ref, in_sems, tiles)
-    down_load = pltpu.make_async_copy(down_hbm, down_ref, in_sems.at[tiles])
-    down_load.start()
 
     def make(start, tile):
-        loads[start // tile].wait()
         rows = rows_ref[start : start + tile]
         gate = lax.dot_general(rows, gate_ref[...], contract, preferred_element_type=jnp.float32)
         up = lax.dot_general(rows, up_ref[...], contract, preferred_element_type=jnp.float32)
         hidden = (gate / (1.0 + jnp.exp(-gate)) * up).astype(jnp.bfloat16)
-        if start == 0:
-            down_load.wait()
         return jnp.dot(hidden, down_ref[...], preferred_element_type=jnp.float32).astype(
             jnp.bfloat16
         )
@@ -146,19 +136,14 @@
     send_tiles(make, out_hbm, stage_ref, sems)
 
 
-def combine_kernel(first_ref, second_ref, rows_hbm, out_ref, rows_ref, total_ref, sems):
-    half = first_ref.shape[1]
+def combine_kernel(combine_ref, rows_hbm, out_ref, rows_ref, total_ref, sems):
     tiles = sems.shape[0]
     tile = rows_hbm.shape[0] // tiles
-    loads = fetch_tiles(rows_hbm, rows_ref, sems, tiles)
-    for index, load in enumerate(loads):
+    for index, load in enumerate(fetch_tiles(rows_hbm, rows_ref, sems, tiles)):
         load.wait()
-        start = index * tile
-        table = first_ref if start < half else second_ref
+        take = slice(index * tile, (index + 1) * tile)
         product = jnp.dot(
-            table[:, start % half : start % half + tile],
-            rows_ref[start : start + tile],
-            preferred_element_type=jnp.float32,
+            combine_ref[:, take], rows_ref[take], preferred_element_type=jnp.float32
         )
         if index == 0:
             total_ref[...] = product
@@ -250,7 +235,7 @@
         copy.wait()
 
 
-def dispatch_kernel(part_ref, gathered_ref, out_hbm, dispatch_ref, stage_ref, sems):
+def dispatch_kernel(part_ref, gathered_ref, out_ref, dispatch_ref):
     width = gathered_ref.shape[1] - 128
     named, rank, _, own = routed(part_ref, gathered_ref)
     blocks = own.shape[0]
@@ -261,24 +246,25 @@
             dispatch_ref[at : at + blocks] = jnp.where(
                 own, jnp.where(takes, 1.0, 0.0), 0.0
             ).astype(jnp.bfloat16)
-
-    def make(start, tile):
-        return jnp.dot(
-            dispatch_ref[start : start + tile],
-            gathered_ref[:, :width],
-            preferred_element_type=jnp.float32,
+    tile = 256
+
+    def step(index, carry):
+        take = pl.ds(pl.multiple_of(index * tile, tile), tile)
+        out_ref[take, :] = jnp.dot(
+            dispatch_ref[take, :], gathered_ref[:, :width], preferred_element_type=jnp.float32
         ).astype(jnp.bfloat16)
-
-    send_tiles(make, out_hbm, stage_ref, sems)
-
-
-def weight_kernel(begin, part_ref, gathered_ref, combine_ref):
+        return carry
+
+    lax.fori_loop(0, out_ref.shape[0] // tile, step, 0)
+
+
+def weight_kernel(part_ref, gathered_ref, combine_ref):
     named, rank, weight, own = routed(part_ref, gathered_ref)
     blocks = own.shape[0]
     group = 128 // (2 * blocks)
-    for start in range(0, named.shape[0] // 2, group):
+    for start in range(0, named.shape[0], group):
         tiles = []
-        for e in range(begin + start, begin + start + group):
+        for e in range(start, start + group):
             for s in range(2):
                 takes = (named[e : e + 1] > 0.5) & (jnp.abs(rank[e : e + 1] - s) < 0.5)
                 tiles.append(jnp.where(own, jnp.where(takes, weight[e : e + 1], 0.0), 0.0))
@@ -377,68 +363,50 @@
     gathered = gathered.reshape(near * block, width + 128)
     part = lax.axis_index("yp").reshape(1)
     tile = 256
-    staging = [pltpu.VMEM((2, tile, width), jnp.bfloat16), pltpu.SemaphoreType.DMA((2,))]
-    slot_rows = pltpu.HBM((far * slots, width), jnp.bfloat16)
     outgoing = pl.pallas_call(
         dispatch_kernel,
         in_specs=[in_smem(), in_vmem()],
-        out_specs=pl.BlockSpec(memory_space=pltpu.HBM),
-        out_shape=slot_rows,
+        out_specs=in_vmem(),
+        out_shape=jax.ShapeDtypeStruct((far * slots, width), jnp.bfloat16),
         cost_estimate=pl.CostEstimate(
             flops=1_200_000_000, bytes_accessed=6_000_000, transcendentals=0
         ),
-        scratch_shapes=[pltpu.VMEM((far * slots, near * block), jnp.bfloat16)] + staging,
+        scratch_shapes=[pltpu.VMEM((far * slots, near * block), jnp.bfloat16)],
         compiler_params=pltpu.CompilerParams(vmem_limit_bytes=20 << 20),
         name="dispatch",
     )(part, gathered)
-
-    def weights_of(begin, rows):
-        return pl.pallas_call(
-            functools.partial(weight_kernel, begin),
-            in_specs=[in_smem(), in_vmem()],
-            out_specs=in_vmem(),
-            out_shape=jax.ShapeDtypeStruct((near * block, far * slots // 2), jnp.bfloat16),
-            cost_estimate=pl.CostEstimate(
-                flops=200_000_000, bytes_accessed=1_200_000, transcendentals=0
-            ),
-            compiler_params=pltpu.CompilerParams(vmem_limit_bytes=12 << 20),
-            name="weights",
-        )(part, rows)
-
-    outgoing, gathered = lax.optimization_barrier((outgoing, gathered))
-    first_weights = weights_of(0, gathered)
     flat_rows = a2a(outgoing.reshape(far, slots, width), FAR).reshape(far * slots, width)
-    flat_rows, first_weights = lax.optimization_barrier((flat_rows, first_weights))
     partial_value = pl.pallas_call(
         expert_kernel,
-        in_specs=[pl.BlockSpec(memory_space=pl.ANY)]
-        + [in_vmem()] * 2
-        + [pl.BlockSpec(memory_space=pltpu.HBM)],
+        in_specs=[in_vmem()] * 4,
         out_specs=pl.BlockSpec(memory_space=pltpu.HBM),
-        out_shape=slot_rows,
+        out_shape=pltpu.HBM((far * slots, width), jnp.bfloat16),
         scratch_shapes=[
-            pltpu.VMEM((far * slots, width), jnp.bfloat16),
-            pltpu.VMEM(w_down.shape[1:], jnp.bfloat16),
-            pltpu.SemaphoreType.DMA((far * slots // tile + 1,)),
-        ]
-        + staging,
+            pltpu.VMEM((2, tile, width), jnp.bfloat16),
+            pltpu.SemaphoreType.DMA((2,)),
+        ],
         cost_estimate=pl.CostEstimate(
             flops=2_500_000_000, bytes_accessed=11_000_000, transcendentals=200_000
         ),
         compiler_params=pltpu.CompilerParams(vmem_limit_bytes=24 << 20),
         name="experts",
-    )(
-        flat_rows,
-        w_gate[0].T,
-        w_up[0].T,
-        pltpu.with_memory_space_constraint(w_down[0], pltpu.HBM),
-    )
+    )(flat_rows, w_gate[0].T, w_up[0].T, w_down[0])
     partial_value, gathered = lax.optimization_barrier((partial_value, gathered))
-    second_weights = weights_of(far // 2, gathered)
+    combine = pl.pallas_call(
+        weight_kernel,
+        in_specs=[in_smem(), in_vmem()],
+        out_specs=in_vmem(),
+        out_shape=jax.ShapeDtypeStruct((near * block, far * slots), jnp.bfloat16),
+        cost_estimate=pl.CostEstimate(
+            flops=200_000_000, bytes_accessed=1_200_000, transcendentals=0
+        ),
+        compiler_params=pltpu.CompilerParams(vmem_limit_bytes=12 << 20),
+        name="weights",
+    )(part, gathered)
     returned = a2a(partial_value.reshape(far, slots, width), FAR).reshape(far * slots, width)
     weighted = pl.pallas_call(
         combine_kernel,
-        in_specs=[in_vmem()] * 2 + [pl.BlockSpec(memory_space=pl.ANY)],
+        in_specs=[in_vmem(), pl.BlockSpec(memory_space=pl.ANY)],
         out_specs=in_vmem(),
         scratch_shapes=[
             pltpu.VMEM((far * slots, width), jnp.bfloat16),
@@ -451,7 +419,7 @@
         ),
         compiler_params=pltpu.CompilerParams(vmem_limit_bytes=16 << 20),
         name="combine",
-    )(first_weights, second_weights, returned)
+    )(combine, returned)
     parts = a2a(weighted.reshape(near, block, width), NEAR)
     moe_out = jnp.sum(parts.astype(jnp.float32), axis=0)
     return (resid + moe_out).astype(jnp.bfloat16)[None]

time: 241 us -> 235 us (0.975)
  the two profiles are of different devices: /device:TPU:8 before, /device:TPU:1 now
where the time goes in v8:
time: 235 us
  waiting for transfers between devices  94.4 us (40%)
  blocking collectives  93.8 us (40%)
  starting transfers between devices  28.1 us (12%)
  Pallas kernels  16.4 us (7%)
    all_to_all x3, waiting for transfers between devices, a2a(): return lax.all_to_all(value, axes, split_axis=0, concat_axis=0, tiled=True)  94.4 us
    all_to_all x2, blocking collectives, a2a(): return lax.all_to_all(value, axes, split_axis=0, concat_axis=0, tiled=True)  93.8 us
    all_to_all x3, starting transfers between devices, a2a(): return lax.all_to_all(value, axes, split_axis=0, concat_axis=0, tiled=True)  19.3 us
    ppermute x1, starting transfers between devices, shards(): partner_proj = lax.ppermute(out_proj, 'side', [(0, 1), (1, 0)])  8.73 us
    pallas_call x1, Pallas kernels, shards(): pl.pallas_call(expert_kernel, in_specs=[in_vmem()] * 4, out_specs=pl.Bloc...  5.31 us
  transfers between devices with their start and end apart: 4, of which 3 were waited for; matrix products, arithmetic and copies ran while one was open for 0% of the time, Pallas kernels for 2%

profile of v8, /device:TPU:1, one launch (start us, length us, event | category | flops | bytes accessed | tf_op | source)
XLA Modules:
  0.0 234.7 jit_solution(9667678546349697446)
XLA Ops:
  0.0 8.7 %collective-permute-start = (bf16[1024,1024]{1,0:T(8,128)(2,1)}, bf16[1024,1024]{1,0:T(8,128)(2,1)S(1)}, u32[]{:S(2)}, u32[]{:S(2)}) collective-permute-start(bf16[1024,1024]{1,0:T(8,128)(2,1)} %proj_hbm.1), channel_id=1, source_target_pairs={{0,256},{256,0},{1,257},{257,1},{2,258},{258,2},{3,259},{259,3},{4... | collective-permute-start | bytes 6291464 | tf_op jit(solution)/shard_map/ppermute | solution.py:301
  9.4 3.3 %attention.1 = (bf16[64,1024]{1,0:T(8,128)(2,1)S(1)}, bf16[64,1024]{1,0:T(8,128)(2,1)S(1)}) custom-call(s32[1]{0:T(128)S(6)} %copy.20.len_ref, bf16[1,64,1024]{2,1,0:T(8,128)(2,1)} %q_hbm.1, bf16[1,1,512,128]{3,2,1,0:T(8,128)(2,1)} %k_hbm.1, bf16[1,1,512,128]{3,2,1,0:T(8,128)(2,1)} %v_hbm.1, bf16[1,64,128]{2,1,0:T(8,128)(2,1)} %kn_hbm.1, ...), custom_call_target="tpu_custom_call" | custom-call | flops 400000000 | bytes 3000000 | tf_op jit(solution)/shard_map/attention/pallas_call | solution.py:304
  12.7 0.0 copy-start.6
  12.7 0.0 copy-start.5
  12.7 0.0 copy-start.3
  12.8 0.0 copy-start.4
  12.8 0.0 collective-permute-done.proj_any
  12.8 1.4 project.1
  14.1 4.7 %all-to-all-start = ((bf16[4,16,2048]{2,1,0:T(8,128)(2,1)}), bf16[4,16,2048]{2,1,0:T(8,128)(2,1)S(1)}, u32[]{:S(2)}, u32[]{:S(2)}) async-start(bf16[4,16,2048]{2,1,0:T(8,128)(2,1)} %project.1), calls=%async_computation | async-start | bytes 524288 | tf_op jit(solution)/shard_map/all_to_all | solution.py:165
  18.8 0.0 copy-done.6
  18.8 0.1 copy.19
  18.9 0.0 copy-done.5
  18.9 0.1 copy.17
  19.0 0.1 divide_convert_fusion
  19.1 0.1 fusion.3.routing_ref
  19.2 8.4 %all-to-all-done.pieces_ref = bf16[4,16,2048]{2,1,0:T(8,128)(2,1)S(1)} async-done(((bf16[4,16,2048]{2,1,0:T(8,128)(2,1)}), bf16[4,16,2048]{2,1,0:T(8,128)(2,1)S(1)}, u32[]{:S(2)}, u32[]{:S(2)}) %all-to-all-start) | async-done | bytes 262176 | tf_op jit(solution)/shard_map/all_to_all | solution.py:165
  27.5 0.0 copy-done.3
  27.5 0.0 copy-done.4
  27.5 1.3 norm.1
  28.9 10.0 %all-to-all-start.1 = ((bf16[16,16,2176]{2,1,0:T(8,128)(2,1)}), bf16[16,16,2176]{2,1,0:T(8,128)(2,1)S(1)}, u32[]{:S(2)}, u32[]{:S(2)}) async-start(bf16[16,16,2176]{2,1,0:T(8,128)(2,1)} %get-tuple-element.14), calls=%async_computation.1 | async-start | bytes 2228224 | tf_op jit(solution)/shard_map/all_to_all | solution.py:165
  38.8 34.7 %all-to-all-done.1 = bf16[16,16,2176]{2,1,0:T(8,128)(2,1)S(1)} async-done(((bf16[16,16,2176]{2,1,0:T(8,128)(2,1)}), bf16[16,16,2176]{2,1,0:T(8,128)(2,1)S(1)}, u32[]{:S(2)}, u32[]{:S(2)}) %all-to-all-start.1) | async-done | bytes 1114144 | tf_op jit(solution)/shard_map/all_to_all | solution.py:165
  73.5 2.0 dispatch.1
  75.6 0.0 copy-start
  75.6 0.0 copy-start.1
  75.6 0.0 copy-start.2
  75.6 58.0 %all_to_all.25 = bf16[32,32,2048]{2,1,0:T(8,128)(2,1)S(1)} all-to-all(bf16[32,32,2048]{2,1,0:T(8,128)(2,1)S(1)} %bitcast.21), channel_id=1, replica_groups=mesh['side'=2,'x'=4,'yp'=4,'yq'=2,'zl'=2,'head'=4] {'x','yq','zl','side'}, dimensions={0} | all-to-all | bytes 8388608 | tf_op jit(solution)/shard_map/all_to_all | solution.py:165
  133.6 0.0 copy-done
  133.6 0.0 copy-done.1
  133.6 0.0 copy-done.2
  133.6 5.3 %experts.1 = bf16[1024,2048]{1,0:T(8,128)(2,1)} custom-call(bf16[1024,2048]{1,0:T(8,128)(2,1)S(1)} %bitcast.22, bf16[192,2048]{1,0:T(8,128)(2,1)S(1)} %bitcast.26, bf16[192,2048]{1,0:T(8,128)(2,1)S(1)} %bitcast.27, bf16[192,2048]{1,0:T(8,128)(2,1)S(1)} %bitcast.28), custom_call_target="tpu_custom_call" | custom-call | flops 2500000000 | bytes 11000000 | tf_op jit(solution)/shard_map/experts/pallas_call | solution.py:379
  138.9 4.7 %all-to-all-start.3 = ((bf16[32,32,2048]{2,1,0:T(8,128)(2,1)}), bf16[32,32,2048]{2,1,0:T(8,128)(2,1)}, u32[]{:S(2)}, u32[]{:S(2)}) async-start(bf16[32,32,2048]{2,1,0:T(8,128)(2,1)} %bitcast.30), calls=%async_computation.3 | async-start | bytes 8388608 | tf_op jit(solution)/shard_map/all_to_all | solution.py:165
  143.6 0.4 weights.1.combine_ref
  144.0 51.4 %all-to-all-done.3 = bf16[32,32,2048]{2,1,0:T(8,128)(2,1)} async-done(((bf16[32,32,2048]{2,1,0:T(8,128)(2,1)}), bf16[32,32,2048]{2,1,0:T(8,128)(2,1)}, u32[]{:S(2)}, u32[]{:S(2)}) %all-to-all-start.3) | async-done | bytes 4194336 | tf_op jit(solution)/shard_map/all_to_all | solution.py:165
  195.4 2.7 %combine.1 = bf16[256,2048]{1,0:T(8,128)(2,1)S(1)} custom-call(bf16[256,1024]{1,0:T(8,128)(2,1)S(1)} %weights.1.combine_ref, bf16[1024,2048]{1,0:T(8,128)(2,1)} %bitcast.14.rows_hbm), custom_call_target="tpu_custom_call" | custom-call | flops 1100000000 | bytes 6000000 | tf_op jit(solution)/shard_map/combine/pallas_call | solution.py:407
  198.1 35.8 %all_to_all.26 = bf16[16,16,2048]{2,1,0:T(8,128)(2,1)S(1)} all-to-all(bf16[16,16,2048]{2,1,0:T(8,128)(2,1)S(1)} %bitcast.25), channel_id=1, replica_groups=mesh['side'=2,'x'=4,'yp'=4,'yq'=2,'zl'=2,'head'=4] {'head','yp'}, dimensions={0} | all-to-all | bytes 2097152 | tf_op jit(solution)/shard_map/all_to_all | solution.py:165
  233.9 0.1 convert_reduce_fusion
  234.1 0.6 fusion
  (2 shorter events, 0.0 us)
Async XLA Ops:
  0.0 12.8 %collective-permute-start = (bf16[1024,1024]{1,0:T(8,128)(2,1)}, bf16[1024,1024]{1,0:T(8,128)(2,1)S(1)}, u32[]{:S(2)}, u32[]{:S(2)}) collective-permute-start(bf16[1024,1024]{1,0:T(8,128)(2,1)} %proj_hbm.1), channel_id=1, source_target_pairs={{0,256},{256,0},{1,257},{257,1},{2,258},{258,2},{3,259},{259,3},{4... | collective-permute-start | bytes 6291464 | tf_op jit(solution)/shard_map/ppermute | solution.py:301
  12.7 6.1 %copy-start.6 = (s32[1,16,8]{1,2,0:T(8,128)S(1)}, s32[1,16,8]{1,2,0:T(8,128)}, u32[]{:S(2)}) copy-start(s32[1,16,8]{1,2,0:T(8,128)} %param.23) | copy-start | bytes 1540
  12.7 6.2 %copy-start.5 = (f32[1,16,8]{1,2,0:T(8,128)S(1)}, f32[1,16,8]{1,2,0:T(8,128)}, u32[]{:S(2)}) copy-start(f32[1,16,8]{1,2,0:T(8,128)} %param.24) | copy-start | bytes 1540
  12.7 14.8 %copy-start.3 = (bf16[1,16,2048]{2,1,0:T(8,128)(2,1)S(1)}, bf16[1,16,2048]{2,1,0:T(8,128)(2,1)}, u32[]{:S(2)}) copy-start(bf16[1,16,2048]{2,1,0:T(8,128)(2,1)} %hidden_ref.1) | copy-start | bytes 196612
  12.8 14.8 %copy-start.4 = (f32[2048]{0:T(1024)S(1)}, f32[2048]{0:T(1024)}, u32[]{:S(2)}) copy-start(f32[2048]{0:T(1024)} %param.22) | copy-start | bytes 24580
  14.1 13.4 %all-to-all-start = ((bf16[4,16,2048]{2,1,0:T(8,128)(2,1)}), bf16[4,16,2048]{2,1,0:T(8,128)(2,1)S(1)}, u32[]{:S(2)}, u32[]{:S(2)}) async-start(bf16[4,16,2048]{2,1,0:T(8,128)(2,1)} %project.1), calls=%async_computation | async-start | bytes 524288 | tf_op jit(solution)/shard_map/all_to_all | solution.py:165
  28.9 44.7 %all-to-all-start.1 = ((bf16[16,16,2176]{2,1,0:T(8,128)(2,1)}), bf16[16,16,2176]{2,1,0:T(8,128)(2,1)S(1)}, u32[]{:S(2)}, u32[]{:S(2)}) async-start(bf16[16,16,2176]{2,1,0:T(8,128)(2,1)} %get-tuple-element.14), calls=%async_computation.1 | async-start | bytes 2228224 | tf_op jit(solution)/shard_map/all_to_all | solution.py:165
  75.6 58.0 %copy-start = (bf16[1,2048,192]{1,2,0:T(8,128)(2,1)S(1)}, bf16[1,2048,192]{1,2,0:T(8,128)(2,1)}, u32[]{:S(2)}) copy-start(bf16[1,2048,192]{1,2,0:T(8,128)(2,1)} %param.25) | copy-start | bytes 2359300
  75.6 58.0 %copy-start.1 = (bf16[1,2048,192]{1,2,0:T(8,128)(2,1)S(1)}, bf16[1,2048,192]{1,2,0:T(8,128)(2,1)}, u32[]{:S(2)}) copy-start(bf16[1,2048,192]{1,2,0:T(8,128)(2,1)} %param.26) | copy-start | bytes 2359300
  75.6 58.0 %copy-start.2 = (bf16[1,192,2048]{2,1,0:T(8,128)(2,1)S(1)}, bf16[1,192,2048]{2,1,0:T(8,128)(2,1)}, u32[]{:S(2)}) copy-start(bf16[1,192,2048]{2,1,0:T(8,128)(2,1)} %param.27) | copy-start | bytes 2359300
  138.9 56.5 %all-to-all-start.3 = ((bf16[32,32,2048]{2,1,0:T(8,128)(2,1)}), bf16[32,32,2048]{2,1,0:T(8,128)(2,1)}, u32[]{:S(2)}, u32[]{:S(2)}) async-start(bf16[32,32,2048]{2,1,0:T(8,128)(2,1)} %bitcast.30), calls=%async_computation.3 | async-start | bytes 8388608 | tf_op jit(solution)/shard_map/all_to_all | solution.py:165

commit v9 on v6

--- a/solution.py
+++ b/solution.py
@@ -121,7 +121,7 @@
         ).astype(jnp.bfloat16)
         return carry
 
-    lax.fori_loop(0, rows_ref.shape[0] // tile, step, 0)
+    lax.fori_loop(0, rows_ref.shape[0] // tile, step, 0, unroll=True)
 
 
 def combine_kernel(combine_ref, rows_ref, out_ref):
@@ -134,7 +134,7 @@
         ).astype(jnp.bfloat16)
         return carry
 
-    lax.fori_loop(0, rows_ref.shape[1] // tile, step, 0)
+    lax.fori_loop(0, rows_ref.shape[1] // tile, step, 0, unroll=True)
 
 
 def in_vmem():
@@ -222,7 +222,7 @@
         ).astype(jnp.bfloat16)
         return carry
 
-    lax.fori_loop(0, out_ref.shape[0] // tile, step, 0)
+    lax.fori_loop(0, out_ref.shape[0] // tile, step, 0, unroll=True)
 
 
 def shards(

time: 234 us -> 232 us (level)
  no operation moved by 1% of the time
where the time goes in v9:
time: 232 us; the launch traced here: 231 us
  blocking collectives  150 us (65%)
  waiting for transfers between devices  43.1 us (19%)
  starting transfers between devices  23.4 us (10%)
  Pallas kernels  12.5 us (5%)
    all_to_all x3, blocking collectives, a2a(): return lax.all_to_all(value, axes, split_axis=0, concat_axis=0, tiled=True)  150 us
    all_to_all x2, waiting for transfers between devices, a2a(): return lax.all_to_all(value, axes, split_axis=0, concat_axis=0, tiled=True)  43.1 us
    all_to_all x2, starting transfers between devices, a2a(): return lax.all_to_all(value, axes, split_axis=0, concat_axis=0, tiled=True)  14.7 us
    ppermute x1, starting transfers between devices, shards(): partner_proj = lax.ppermute(out_proj, 'side', [(0, 1), (1, 0)])  8.73 us
  transfers between devices with their start and end apart: 3, of which 2 were waited for; matrix products, arithmetic and copies ran while one was open for 0% of the time, Pallas kernels for 1%

profile of v9, /device:TPU:1, one launch (start us, length us, event | category | flops | bytes accessed | tf_op | source)
XLA Modules:
  0.0 231.3 jit_solution(17585807513606010520)
XLA Ops:
  0.0 8.7 %collective-permute-start = (bf16[1024,1024]{1,0:T(8,128)(2,1)}, bf16[1024,1024]{1,0:T(8,128)(2,1)S(1)}, u32[]{:S(2)}, u32[]{:S(2)}) collective-permute-start(bf16[1024,1024]{1,0:T(8,128)(2,1)} %proj_hbm.1), channel_id=1, source_target_pairs={{0,256},{256,0},{1,257},{257,1},{2,258},{258,2},{3,259},{259,3},{4... | collective-permute-start | bytes 6291464 | tf_op jit(solution)/shard_map/ppermute | solution.py:252
  9.4 3.3 %attention.1 = (bf16[64,1024]{1,0:T(8,128)(2,1)S(1)}, bf16[64,1024]{1,0:T(8,128)(2,1)S(1)}) custom-call(s32[1]{0:T(128)S(6)} %copy.20.len_ref, bf16[1,64,1024]{2,1,0:T(8,128)(2,1)} %q_hbm.1, bf16[1,1,512,128]{3,2,1,0:T(8,128)(2,1)} %k_hbm.1, bf16[1,1,512,128]{3,2,1,0:T(8,128)(2,1)} %v_hbm.1, bf16[1,64,128]{2,1,0:T(8,128)(2,1)} %kn_hbm.1, ...), custom_call_target="tpu_custom_call" | custom-call | flops 400000000 | bytes 3000000 | tf_op jit(solution)/shard_map/attention/pallas_call | solution.py:255
  12.7 0.0 copy-start.6
  12.7 0.0 copy-start.5
  12.7 0.0 copy-start.3
  12.8 0.0 copy-start.4
  12.8 0.0 collective-permute-done.proj_any
  12.8 1.3 project.1
  14.1 4.7 %all-to-all-start = ((bf16[4,16,2048]{2,1,0:T(8,128)(2,1)}), bf16[4,16,2048]{2,1,0:T(8,128)(2,1)S(1)}, u32[]{:S(2)}, u32[]{:S(2)}) async-start(bf16[4,16,2048]{2,1,0:T(8,128)(2,1)} %project.1), calls=%async_computation | async-start | bytes 524288 | tf_op jit(solution)/shard_map/all_to_all | solution.py:149
  18.8 0.0 copy-done.6
  18.8 0.1 copy.19
  18.9 0.0 copy-done.5
  18.9 0.1 copy.17
  19.0 0.1 divide_convert_fusion
  19.1 0.1 fusion.3.routing_ref
  19.2 8.4 %all-to-all-done.pieces_ref = bf16[4,16,2048]{2,1,0:T(8,128)(2,1)S(1)} async-done(((bf16[4,16,2048]{2,1,0:T(8,128)(2,1)}), bf16[4,16,2048]{2,1,0:T(8,128)(2,1)S(1)}, u32[]{:S(2)}, u32[]{:S(2)}) %all-to-all-start) | async-done | bytes 262176 | tf_op jit(solution)/shard_map/all_to_all | solution.py:149
  27.5 0.0 copy-done.3
  27.5 0.0 copy-done.4
  27.5 1.3 norm.1
  28.8 10.0 %all-to-all-start.1 = ((bf16[16,16,2176]{2,1,0:T(8,128)(2,1)}), bf16[16,16,2176]{2,1,0:T(8,128)(2,1)S(1)}, u32[]{:S(2)}, u32[]{:S(2)}) async-start(bf16[16,16,2176]{2,1,0:T(8,128)(2,1)} %get-tuple-element.14), calls=%async_computation.1 | async-start | bytes 2228224 | tf_op jit(solution)/shard_map/all_to_all | solution.py:149
  38.8 34.7 %all-to-all-done.1 = bf16[16,16,2176]{2,1,0:T(8,128)(2,1)S(1)} async-done(((bf16[16,16,2176]{2,1,0:T(8,128)(2,1)}), bf16[16,16,2176]{2,1,0:T(8,128)(2,1)S(1)}, u32[]{:S(2)}, u32[]{:S(2)}) %all-to-all-start.1) | async-done | bytes 1114144 | tf_op jit(solution)/shard_map/all_to_all | solution.py:149
  73.5 1.5 dispatch.1
  75.0 0.0 copy-start
  75.0 0.0 copy-start.1
  75.0 0.0 copy-start.2
  75.0 58.0 %all_to_all.25 = bf16[32,32,2048]{2,1,0:T(8,128)(2,1)S(1)} all-to-all(bf16[32,32,2048]{2,1,0:T(8,128)(2,1)S(1)} %bitcast.24), channel_id=1, replica_groups=mesh['side'=2,'x'=4,'yp'=4,'yq'=2,'zl'=2,'head'=4] {'x','yq','zl','side'}, dimensions={0} | all-to-all | bytes 8388608 | tf_op jit(solution)/shard_map/all_to_all | solution.py:149
  133.0 0.0 copy-done
  133.0 0.0 copy-done.1
  133.0 0.0 copy-done.2
  133.0 3.8 %experts.1 = bf16[1024,2048]{1,0:T(8,128)(2,1)S(1)} custom-call(bf16[1024,2048]{1,0:T(8,128)(2,1)S(1)} %bitcast.22, bf16[192,2048]{1,0:T(8,128)(2,1)S(1)} %bitcast.27, bf16[192,2048]{1,0:T(8,128)(2,1)S(1)} %bitcast.28, bf16[192,2048]{1,0:T(8,128)(2,1)S(1)} %bitcast.29), custom_call_target="tpu_custom_call" | custom-call | flops 2500000000 | bytes 11000000 | tf_op jit(solution)/shard_map/experts/pallas_call | solution.py:331
  136.9 54.6 %all_to_all.26 = bf16[32,32,2048]{2,1,0:T(8,128)(2,1)S(1)} all-to-all(bf16[32,32,2048]{2,1,0:T(8,128)(2,1)S(1)} %bitcast.23), channel_id=1, replica_groups=mesh['side'=2,'x'=4,'yp'=4,'yq'=2,'zl'=2,'head'=4] {'x','yq','zl','side'}, dimensions={0} | all-to-all | bytes 8388608 | tf_op jit(solution)/shard_map/all_to_all | solution.py:149
  191.5 1.2 combine.1
  192.8 37.8 %all_to_all.27 = bf16[16,16,2048]{2,1,0:T(8,128)(2,1)S(1)} all-to-all(bf16[16,16,2048]{2,1,0:T(8,128)(2,1)S(1)} %bitcast.25), channel_id=1, replica_groups=mesh['side'=2,'x'=4,'yp'=4,'yq'=2,'zl'=2,'head'=4] {'head','yp'}, dimensions={0} | all-to-all | bytes 2097152 | tf_op jit(solution)/shard_map/all_to_all | solution.py:149
  230.5 0.1 convert_reduce_fusion
  230.7 0.6 fusion
  (2 shorter events, 0.0 us)
Async XLA Ops:
  0.0 12.8 %collective-permute-start = (bf16[1024,1024]{1,0:T(8,128)(2,1)}, bf16[1024,1024]{1,0:T(8,128)(2,1)S(1)}, u32[]{:S(2)}, u32[]{:S(2)}) collective-permute-start(bf16[1024,1024]{1,0:T(8,128)(2,1)} %proj_hbm.1), channel_id=1, source_target_pairs={{0,256},{256,0},{1,257},{257,1},{2,258},{258,2},{3,259},{259,3},{4... | collective-permute-start | bytes 6291464 | tf_op jit(solution)/shard_map/ppermute | solution.py:252
  12.7 6.1 %copy-start.6 = (s32[1,16,8]{1,2,0:T(8,128)S(1)}, s32[1,16,8]{1,2,0:T(8,128)}, u32[]{:S(2)}) copy-start(s32[1,16,8]{1,2,0:T(8,128)} %param.23) | copy-start | bytes 1540
  12.7 6.2 %copy-start.5 = (f32[1,16,8]{1,2,0:T(8,128)S(1)}, f32[1,16,8]{1,2,0:T(8,128)}, u32[]{:S(2)}) copy-start(f32[1,16,8]{1,2,0:T(8,128)} %param.24) | copy-start | bytes 1540
  12.7 14.8 %copy-start.3 = (bf16[1,16,2048]{2,1,0:T(8,128)(2,1)S(1)}, bf16[1,16,2048]{2,1,0:T(8,128)(2,1)}, u32[]{:S(2)}) copy-start(bf16[1,16,2048]{2,1,0:T(8,128)(2,1)} %hidden_ref.1) | copy-start | bytes 196612
  12.8 14.8 %copy-start.4 = (f32[2048]{0:T(1024)S(1)}, f32[2048]{0:T(1024)}, u32[]{:S(2)}) copy-start(f32[2048]{0:T(1024)} %param.22) | copy-start | bytes 24580
  14.1 13.4 %all-to-all-start = ((bf16[4,16,2048]{2,1,0:T(8,128)(2,1)}), bf16[4,16,2048]{2,1,0:T(8,128)(2,1)S(1)}, u32[]{:S(2)}, u32[]{:S(2)}) async-start(bf16[4,16,2048]{2,1,0:T(8,128)(2,1)} %project.1), calls=%async_computation | async-start | bytes 524288 | tf_op jit(solution)/shard_map/all_to_all | solution.py:149
  28.8 44.7 %all-to-all-start.1 = ((bf16[16,16,2176]{2,1,0:T(8,128)(2,1)}), bf16[16,16,2176]{2,1,0:T(8,128)(2,1)S(1)}, u32[]{:S(2)}, u32[]{:S(2)}) async-start(bf16[16,16,2176]{2,1,0:T(8,128)(2,1)} %get-tuple-element.14), calls=%async_computation.1 | async-start | bytes 2228224 | tf_op jit(solution)/shard_map/all_to_all | solution.py:149
  75.0 58.0 %copy-start = (bf16[1,2048,192]{1,2,0:T(8,128)(2,1)S(1)}, bf16[1,2048,192]{1,2,0:T(8,128)(2,1)}, u32[]{:S(2)}) copy-start(bf16[1,2048,192]{1,2,0:T(8,128)(2,1)} %param.25) | copy-start | bytes 2359300
  75.0 58.0 %copy-start.1 = (bf16[1,2048,192]{1,2,0:T(8,128)(2,1)S(1)}, bf16[1,2048,192]{1,2,0:T(8,128)(2,1)}, u32[]{:S(2)}) copy-start(bf16[1,2048,192]{1,2,0:T(8,128)(2,1)} %param.26) | copy-start | bytes 2359300
  75.0 58.0 %copy-start.2 = (bf16[1,192,2048]{2,1,0:T(8,128)(2,1)S(1)}, bf16[1,192,2048]{2,1,0:T(8,128)(2,1)}, u32[]{:S(2)}) copy-start(bf16[1,192,2048]{2,1,0:T(8,128)(2,1)} %param.27) | copy-start | bytes 2359300
